TPU v7x, 32 devices: a whole 2x2x4 slice. The times are simulated.
32 devices in a mesh: patch: 8 (over z, x), pair: 4 (over y, core).
Axes of the slice: x: 2, y: 2, z: 4, core: 2. Of those that a mesh axis runs over, the one named last changes fastest.
Arguments:
- node_latents: bfloat16 [8192, 1024], P('patch', 'pair'), may hold values from -12 to 12
- edge_latents: bfloat16 [16384, 1024], P('patch', 'pair'), may hold values from -12 to 12
- edge_sender: int32 [64, 256], P('patch'), may hold values from -1 to 2047, as said below
- edge_receiver: int32 [64, 256], P('patch'), may hold values from -1 to 255, as said below
- block_owner: int32 [64], P('patch'), may hold values from 0 to 7, as said below
- node_counts: int32 [8], P('patch'), may hold values from 512 to 1024, as said below
- halo_nodes: int32 [8, 8, 256], P('patch'), may hold values from 0 to 1023, as said below
- w_endpoints: bfloat16 [1024, 2, 1024], P(None, None, 'pair'), may hold values from -0.1875 to 0.1875
- w_edge_in: bfloat16 [1024, 1024], P(None, 'pair'), may hold values from -0.1875 to 0.1875
- edge_bias: float32 [1024], P('pair'), may hold values from -3 to 3
- w_edge_out: bfloat16 [1024, 1024], P('pair'), may hold values from -1 to 1
- edge_gain: float32 [1024], P('pair'), may hold values from 0.5 to 1.5
- edge_shift: float32 [1024], P('pair'), may hold values from -3 to 3
- w_node_in: bfloat16 [2, 1024, 1024], P(None, None, 'pair'), may hold values from -0.125 to 0.125
- node_bias: float32 [1024], P('pair'), may hold values from -3 to 3
- w_node_out: bfloat16 [1024, 1024], P('pair'), may hold values from -1 to 1
- node_gain: float32 [1024], P('pair'), may hold values from 0.5 to 1.5
- node_shift: float32 [1024], P('pair'), may hold values from -3 to 3
Outputs:
- updated_nodes: bfloat16 [8192, 1024], P('patch', 'pair')
- updated_edges: bfloat16 [16384, 1024], P('patch', 'pair')
Inputs may be any that keep to these rules, and one draw needn't show every extreme that they name: `edge_sender`: section q = slot // 256 of a patch's halo table holds, in order, the nodes halo_nodes[q, that patch]; -1 stands exactly where edge_receiver is -1. `edge_receiver`: -1 marks padding and stands only after the live edges of a block; within a block the live values never fall and take at most 16 distinct values; every patch has a block with 256 live edges and 16 distinct receivers. `block_owner`: no patch owns more than 1 of the blocks of one patch; every patch owns 1 of its own blocks, and some patch owns 1 block of every patch. `node_counts`: some patch has 1024 live nodes. halo_nodes[q, d] lists local live nodes of patch q (below node_counts[q]); entries may repeat.
All inputs are finite; a program needn't handle non-finite values.
Results may differ from a plain program's by a relative error of at most 0.008.
Values may be sent and summed in bfloat16 or wider, within the bound.
No kernel may reach another device: no remote copies, remote signals or barrier semaphores. Data moves between devices by JAX's collectives and lax.ppermute only.
A program may use at most 128 MiB of HBM per device.

v0:
```python
import jax
import jax.numpy as jnp
from jax import lax
from jax.sharding import PartitionSpec as P

RT = 16


EPS = 1e-05


def fold_product(weight, running, slab_rows):
    return running + jnp.dot(slab_rows, weight, preferred_element_type=jnp.float32)


def finish_norm(values, first_sum, second_sum, gain_row, shift_row, full_width):
    row_mean = first_sum[:, None] / full_width
    spread = second_sum[:, None] / full_width - row_mean * row_mean
    return (values - row_mean) * lax.rsqrt(spread + EPS) * gain_row[None, :] + shift_row[None, :]


def shards(
    node_latents,
    edge_latents,
    edge_sender,
    edge_receiver,
    block_owner,
    node_counts,
    halo_nodes,
    w_endpoints,
    w_edge_in,
    edge_bias,
    w_edge_out,
    edge_gain,
    edge_shift,
    w_node_in,
    node_bias,
    w_node_out,
    node_gain,
    node_shift,
):
    patches = lax.axis_size("patch")
    full_width = w_edge_in.shape[0]
    local_width = w_edge_in.shape[1]
    node_total = node_latents.shape[0]
    blocks = block_owner.shape[0]
    tile_size = edge_sender.shape[1]
    halo_size = halo_nodes.shape[2]
    capacity = max(1, blocks // patches)
    end_weight = w_endpoints.reshape(full_width, 2 * local_width)
    send_list = halo_nodes[0]
    full_nodes = lax.all_gather(node_latents, "pair", axis=1, tiled=True)
    projected = jnp.dot(full_nodes, end_weight, preferred_element_type=jnp.float32).astype(
        jnp.bfloat16
    )
    picked = projected[send_list.reshape(-1)].reshape(patches, halo_size, 2 * local_width)
    halo_table = lax.all_to_all(picked, "patch", split_axis=0, concat_axis=0, tiled=True).reshape(
        patches * halo_size, 2 * local_width
    )
    halo_pairs = halo_table.reshape(patches * halo_size, 2, local_width)
    senders = edge_sender.reshape(-1)
    receivers = edge_receiver.reshape(-1)
    is_live = receivers >= 0
    edge_owner = jnp.repeat(block_owner, tile_size)
    sender_rows = halo_pairs[jnp.maximum(senders, 0), 0]
    receiver_rows = halo_pairs[edge_owner * halo_size + jnp.maximum(receivers, 0), 1]
    start_value = (
        sender_rows.astype(jnp.float32) + receiver_rows.astype(jnp.float32) + edge_bias[None, :]
    )
    edge_pre = fold_product(
        w_edge_in, start_value, lax.all_gather(edge_latents, "pair", axis=1, tiled=True)
    )
    edge_hidden = jax.nn.silu(edge_pre).astype(jnp.bfloat16)
    edge_terms = jnp.dot(edge_hidden, w_edge_out, preferred_element_type=jnp.float32)
    edge_mixed = lax.psum_scatter(
        edge_terms.astype(jnp.bfloat16), "pair", scatter_dimension=1, tiled=True
    ).astype(jnp.float32)
    edge_first, edge_second = lax.psum(
        (jnp.sum(edge_mixed, axis=1), jnp.sum(edge_mixed * edge_mixed, axis=1)), "pair"
    )
    edge_norm = finish_norm(edge_mixed, edge_first, edge_second, edge_gain, edge_shift, full_width)
    old_edges = edge_latents.astype(jnp.float32)
    new_edges = jnp.where(is_live[:, None], old_edges + edge_norm, old_edges).astype(jnp.bfloat16)
    same_owner = block_owner[:, None] == block_owner[None, :]
    earlier = jnp.arange(blocks)[None, :] < jnp.arange(blocks)[:, None]
    slot_rank = jnp.sum((same_owner & earlier).astype(jnp.int32), axis=1)
    target_slot = block_owner * capacity + slot_rank
    kept_rows = jnp.where(is_live[:, None], new_edges, jnp.zeros_like(new_edges)).reshape(
        blocks, tile_size, local_width
    )
    previous = jnp.concatenate(
        [jnp.full((blocks, 1), -2, jnp.int32), edge_receiver[:, :-1]], axis=1
    )
    segment = jnp.cumsum((edge_receiver != previous).astype(jnp.int32), axis=1) - 1
    segment = jnp.where(edge_receiver >= 0, segment, RT)
    member = segment[:, None, :] == jnp.arange(RT, dtype=jnp.int32)[None, :, None]
    tile_sums = jnp.einsum(
        "brt,btd->brd", member.astype(jnp.bfloat16), kept_rows, preferred_element_type=jnp.float32
    )
    tile_ids = jnp.max(jnp.where(member, edge_receiver[:, None, :], -1), axis=2)
    send_values = (
        jnp.zeros((patches * capacity, RT, local_width), jnp.float32).at[target_slot].set(tile_sums)
    )
    send_ids = jnp.full((patches * capacity, RT), -1, jnp.int32).at[target_slot].set(tile_ids)
    got_values, got_ids = (
        lax.all_to_all(
            send_values.astype(jnp.bfloat16), "patch", split_axis=0, concat_axis=0, tiled=True
        ).astype(send_values.dtype),
        lax.all_to_all(send_ids, "patch", split_axis=0, concat_axis=0, tiled=True),
    )
    source = (jnp.arange(patches * capacity, dtype=jnp.int32) // capacity)[:, None]
    node_index = send_list[source, jnp.maximum(got_ids, 0)]
    node_index = jnp.where(got_ids >= 0, node_index, node_total)
    aggregate = jax.ops.segment_sum(
        got_values.reshape(-1, local_width), node_index.reshape(-1), num_segments=node_total + 1
    )
    aggregated = aggregate[:node_total].astype(jnp.bfloat16)
    node_start = (
        jnp.dot(full_nodes, w_node_in[0], preferred_element_type=jnp.float32) + node_bias[None, :]
    )
    node_pre = fold_product(
        w_node_in[1], node_start, lax.all_gather(aggregated, "pair", axis=1, tiled=True)
    )
    node_hidden = jax.nn.silu(node_pre).astype(jnp.bfloat16)
    node_terms = jnp.dot(node_hidden, w_node_out, preferred_element_type=jnp.float32)
    node_mixed = lax.psum_scatter(
        node_terms.astype(jnp.bfloat16), "pair", scatter_dimension=1, tiled=True
    ).astype(jnp.float32)
    node_first, node_second = lax.psum(
        (jnp.sum(node_mixed, axis=1), jnp.sum(node_mixed * node_mixed, axis=1)), "pair"
    )
    node_norm = finish_norm(node_mixed, node_first, node_second, node_gain, node_shift, full_width)
    live_nodes = jnp.arange(node_total, dtype=jnp.int32) < node_counts[0]
    old_nodes = node_latents.astype(jnp.float32)
    updated_nodes = jnp.where(live_nodes[:, None], old_nodes + node_norm, old_nodes).astype(
        jnp.bfloat16
    )
    return (updated_nodes, new_edges)


def solution(mesh):
    return jax.shard_map(
        shards,
        mesh=mesh,
        in_specs=(
            P("patch", "pair"),
            P("patch", "pair"),
            P("patch", None),
            P("patch", None),
            P("patch"),
            P("patch"),
            P("patch", None, None),
            P(None, None, "pair"),
            P(None, "pair"),
            P("pair"),
            P("pair", None),
            P("pair"),
            P("pair"),
            P(None, None, "pair"),
            P("pair"),
            P("pair", None),
            P("pair"),
            P("pair"),
        ),
        out_specs=(P("patch", "pair"), P("patch", "pair")),
        check_vma=False,
    )
```

profile of v0, /device:TPU:0, one launch (start us, length us, event | category | flops | bytes accessed | tf_op | source)
XLA Modules:
  0.0 302.4 jit_solution(14411088524748841558)
XLA Ops:
  7.2 0.0 all-gather.4.cloned.1.call-start
  7.2 0.7 all-gather.4.cloned.1.call-update
  7.9 0.0 all-gather.6.cloned.1.call-start
  8.0 0.7 all-gather.6.cloned.1.call-update
  8.7 0.2 copy.26
  9.0 26.1 %all-gather.4.cloned.1.call-done = bf16[1024,1024]{1,0:T(8,128)(2,1)} async-done(((bf16[1024,256]{1,0:T(8,128)(2,1)}), bf16[1024,1024]{1,0:T(8,128)(2,1)}) %all-gather.4.cloned.1.call-update) | async-done | bytes 2097168 | tf_op jit(solution)/shard_map/all_gather | solution.py:52
  35.1 2.8 convolution_convert_fusion.2
  38.0 9.2 %gather_fusion.1 = bf16[2048,512]{1,0:T(8,128)(2,1)} fusion(bf16[1024,512]{1,0:T(8,128)(2,1)S(1)} %convolution_convert_fusion.2, s32[2048]{0:T(1024)S(1)} %broadcast_clamp_fusion), kind=kCustom, calls=%fused_computation.1 | custom fusion | bytes 4202496 | tf_op jit(solution)/shard_map/gather | solution.py:56
  47.2 5.6 %all-to-all-start.1 = ((bf16[8,256,512]{2,1,0:T(8,128)(2,1)}), bf16[8,256,512]{2,1,0:T(8,128)(2,1)}, u32[]{:S(2)}, u32[]{:S(2)}) async-start(bf16[8,256,512]{2,1,0:T(8,128)(2,1)} %bitcast.64), calls=%async_computation.1 | async-start | bytes 4194304 | tf_op jit(solution)/shard_map/all_to_all | solution.py:57
  52.8 0.0 reduce-scatter.3.cloned.1.call-start
  52.9 0.1 convert_bitcast_fusion
  52.9 0.6 reduce-window.6
  53.5 0.2 slice_reduce_fusion
  53.8 0.2 convert_reduce_fusion.2
  54.0 0.1 bitcast_select_fusion
  54.1 47.5 %all-to-all-done.1 = bf16[8,256,512]{2,1,0:T(8,128)(2,1)} async-done(((bf16[8,256,512]{2,1,0:T(8,128)(2,1)}), bf16[8,256,512]{2,1,0:T(8,128)(2,1)}, u32[]{:S(2)}, u32[]{:S(2)}) %all-to-all-start.1) | async-done | bytes 2097184 | tf_op jit(solution)/shard_map/all_to_all | solution.py:57
  101.6 2.5 reshape_reshape.3
  104.1 20.5 %gather_fusion.3 = bf16[2048,256]{1,0:T(8,128)(2,1)} fusion(bf16[2048,2,256]{2,1,0:T(2,128)(2,1)S(1)} %reshape_reshape.3, s32[2048]{0:T(1024)S(1)} %bitcast.63), kind=kCustom, calls=%fused_computation.3 | custom fusion | bytes 2113536 | tf_op jit(solution)/shard_map/gather | solution.py:66
  124.6 20.3 %gather_fusion.2 = bf16[2048,256]{1,0:T(8,128)(2,1)} fusion(bf16[2048,2,256]{2,1,0:T(2,128)(2,1)S(1)} %reshape_reshape.3, s32[2048]{0:T(1024)S(1)} %bitcast.62), kind=kCustom, calls=%fused_computation.2 | custom fusion | bytes 2113536 | tf_op jit(solution)/shard_map/gather | solution.py:65
  144.9 9.1 %convolution_convert_fusion = bf16[2048,1024]{1,0:T(8,128)(2,1)} fusion(bf16[256,1024]{1,0:T(8,128)(2,1)S(1)} %copy-done, bf16[2048,1024]{1,0:T(8,128)(2,1)} %all-gather.6.cloned.1.call-done, bf16[1024,256]{1,0:T(8,128)(2,1)S(1)} %copy-done.13, bf16[2048,256]{1,0:T(8,128)(2,1)} %gather_fusion.3, bf16[2048,256]{1,0:T(8,128)(2,1)} %gather_fusion.2, ...), kind=kOutput, calls=%fused_computation.7 | convolution fusion | flops 2154823680 | bytes 11535360 | tf_op jit(solution)/shard_map/dot_general | solution.py:74
  154.1 0.2 select_reduce_fusion
  154.3 1.2 scatter_custom_fusion
  155.5 3.6 %all-to-all-start = ((s32[8,1,16]{2,1,0:T(1,128)}), s32[8,1,16]{2,1,0:T(1,128)S(1)}, u32[]{:S(2)}, u32[]{:S(2)}) async-start(s32[8,1,16]{2,1,0:T(1,128)} %bitcast.5), calls=%async_computation | async-start | bytes 8192 | tf_op jit(solution)/shard_map/all_to_all | solution.py:109
  159.1 6.4 %all-to-all-done = s32[8,1,16]{2,1,0:T(1,128)S(1)} async-done(((s32[8,1,16]{2,1,0:T(1,128)}), s32[8,1,16]{2,1,0:T(1,128)S(1)}, u32[]{:S(2)}, u32[]{:S(2)}) %all-to-all-start) | async-done | bytes 544 | tf_op jit(solution)/shard_map/all_to_all | solution.py:109
  165.6 0.1 ge.30
  165.6 0.1 reshape.202
  165.8 1.2 gather_fusion
  167.0 29.8 %reduce-scatter.3.cloned.1.call-done = bf16[2048,256]{1,0:T(8,128)(2,1)} async-done(((bf16[2048,1024]{1,0:T(8,128)(2,1)}), bf16[2048,256]{1,0:T(8,128)(2,1)}) %reduce-scatter.3.cloned.1.call-update) | async-done | bytes 1048592 | tf_op jit(solution)/shard_map/reduce_scatter | solution.py:75
  196.8 1.8 convert_reduce_fusion
  198.6 10.1 %all-reduce.4 = (f32[2048]{0:T(1024)S(1)}, f32[2048]{0:T(1024)S(1)}) all-reduce(f32[2048]{0:T(1024)S(1)} %get-tuple-element.3, f32[2048]{0:T(1024)S(1)} %get-tuple-element.2), channel_id=1, replica_groups=mesh['patch'=8,'pair'=4] {'pair'}, use_global_device_ids=true, to_apply=%region_9.10 | all-reduce | flops 4096 | bytes 32768 | tf_op jit(solution)/shard_map/psum | solution.py:78
  208.8 3.9 %broadcast_select_fusion = (bf16[2048,256]{1,0:T(8,128)(2,1)S(1)}, bf16[2048,256]{1,0:T(8,128)(2,1)}) fusion(pred[2048]{0:T(1024)(128)(4,1)S(1)} %ge.31, f32[256]{0:T(256)S(1)} %copy-done.7, f32[256]{0:T(256)S(1)} %copy-done.8, f32[2048]{0:T(1024)S(1)} %get-tuple-element.15, f32[2048]{0:T(1024)S(1)} %get-tuple-element.14, ...), kind=kLoop, calls=%fused_computation.36 | loop fusion | flops 5242880 | bytes 4214784 | tf_op jit(solution)/shard_map/jit(_where)/select_n | solution.py:88
  212.8 0.2 fusion.22
  213.0 0.7 scatter_fusion
  213.8 0.6 convert_element_type.59
  214.4 5.6 %all-to-all-start.2 = ((bf16[8,16,256]{2,1,0:T(8,128)(2,1)}), bf16[8,16,256]{2,1,0:T(8,128)(2,1)S(1)}, u32[]{:S(2)}, u32[]{:S(2)}) async-start(bf16[8,16,256]{2,1,0:T(8,128)(2,1)} %convert_element_type.59), calls=%async_computation.3 | async-start | bytes 131072 | tf_op jit(solution)/shard_map/all_to_all | solution.py:106
  220.0 0.0 all-gather.8.cloned.1.call-start
  220.1 6.8 %all-to-all-done.2 = bf16[8,16,256]{2,1,0:T(8,128)(2,1)S(1)} async-done(((bf16[8,16,256]{2,1,0:T(8,128)(2,1)}), bf16[8,16,256]{2,1,0:T(8,128)(2,1)S(1)}, u32[]{:S(2)}, u32[]{:S(2)}) %all-to-all-start.2) | async-done | bytes 65568 | tf_op jit(solution)/shard_map/all_to_all | solution.py:106
  226.9 1.5 scatter_custom_fusion.2
  228.4 0.8 slice.46
  229.3 0.2 reduce-scatter.5.cloned.1.call-start
  229.6 3.5 %convolution_add_fusion.2 = f32[1024,256]{1,0:T(8,128)} fusion(bf16[1024,1024]{1,0:T(8,128)(2,1)} %all-gather.4.cloned.1.call-done, f32[256]{0:T(256)S(1)} %copy-done.16, bf16[2,1024,256]{2,1,0:T(8,128)(2,1)} %param.31), kind=kOutput, calls=%fused_computation.26 | convolution fusion | flops 537133056 | bytes 3671040 | tf_op jit(solution)/shard_map/dot_general | solution.py:119
  233.0 16.3 %all-gather.8.cloned.1.call-done = bf16[1024,1024]{1,0:T(8,128)(2,1)} async-done(((bf16[1024,256]{1,0:T(8,128)(2,1)}), bf16[1024,1024]{1,0:T(8,128)(2,1)}) %all-gather.8.cloned.1.call-update) | async-done | bytes 2097168 | tf_op jit(solution)/shard_map/all_gather | solution.py:122
  249.3 5.4 %convolution_convert_fusion.1 = bf16[1024,1024]{1,0:T(8,128)(2,1)} fusion(bf16[256,1024]{1,0:T(8,128)(2,1)S(1)} %copy-done.14, f32[1024,256]{1,0:T(8,128)} %convolution_add_fusion.2, bf16[1024,1024]{1,0:T(8,128)(2,1)} %all-gather.8.cloned.1.call-done, bf16[2,1024,256]{2,1,0:T(8,128)(2,1)S(1)} %copy-done.12), kind=kOutput, calls=%fused_computation.19 | convolution fusion | flops 1076363264 | bytes 6291456 | tf_op jit(solution)/shard_map/dot_general | solution.py:125
  254.7 0.0 reduce-scatter.5.cloned.1.call-update
  255.4 30.6 %reduce-scatter.5.cloned.1.call-done = bf16[1024,256]{1,0:T(8,128)(2,1)} async-done(((bf16[1024,1024]{1,0:T(8,128)(2,1)}), bf16[1024,256]{1,0:T(8,128)(2,1)}) %reduce-scatter.5.cloned.1.call-update) | async-done | bytes 524304 | tf_op jit(solution)/shard_map/reduce_scatter | solution.py:126
  286.0 1.4 convert_reduce_fusion.1
  287.4 5.9 %all-reduce.3 = (f32[1024]{0:T(1024)S(1)}, f32[1024]{0:T(1024)S(1)}) all-reduce(f32[1024]{0:T(1024)S(1)} %get-tuple-element.5, f32[1024]{0:T(1024)S(1)} %get-tuple-element.4), channel_id=1, replica_groups=mesh['patch'=8,'pair'=4] {'pair'}, use_global_device_ids=true, to_apply=%region_16.17 | all-reduce | flops 2048 | bytes 16384 | tf_op jit(solution)/shard_map/psum | solution.py:129
  293.3 2.5 fusion.9
  (55 shorter events, 0.3 us)
Async XLA Ops:
  7.2 137.8 %copy-start = (bf16[256,1024]{1,0:T(8,128)(2,1)S(1)}, bf16[256,1024]{1,0:T(8,128)(2,1)}, u32[]{:S(2)}) copy-start(bf16[256,1024]{1,0:T(8,128)(2,1)} %param.28) | copy-start | bytes 1572868
  7.2 1.5 copy-start.4
  7.2 1.8 copy-start.1
  7.2 27.9 %all-gather.4.cloned.1.call-start = ((), (), s32[]{:S(2)}) async-start(), calls=%async_computation.5 | async-start | bytes 2621440 | tf_op jit(solution)/shard_map/all_gather | solution.py:52
  7.9 137.0 %all-gather.6.cloned.1.call-start = ((), (), s32[]{:S(2)}) async-start(), calls=%async_computation.6 | async-start | bytes 5242880 | tf_op jit(solution)/shard_map/all_gather | solution.py:71
  47.2 5.7 %copy-start.5 = (s32[8,256]{1,0:T(8,128)S(1)}, s32[8,256]{1,0:T(8,128)}, u32[]{:S(2)}) copy-start(s32[8,256]{1,0:T(8,128)} %param.21) | copy-start | bytes 24580
  47.2 6.6 %copy-start.11 = (s32[8]{0:T(128)S(1)}, s32[8]{0:T(128)}, u32[]{:S(2)}) copy-start(s32[8]{0:T(128)} %param.22) | copy-start | bytes 100
  47.2 6.9 %copy-start.6 = (s32[8,256]{1,0:T(8,128)S(1)}, s32[8,256]{1,0:T(8,128)}, u32[]{:S(2)}) copy-start(s32[8,256]{1,0:T(8,128)} %param.20) | copy-start | bytes 24580
  47.2 54.4 %all-to-all-start.1 = ((bf16[8,256,512]{2,1,0:T(8,128)(2,1)}), bf16[8,256,512]{2,1,0:T(8,128)(2,1)}, u32[]{:S(2)}, u32[]{:S(2)}) async-start(bf16[8,256,512]{2,1,0:T(8,128)(2,1)} %bitcast.64), calls=%async_computation.1 | async-start | bytes 4194304 | tf_op jit(solution)/shard_map/all_to_all | solution.py:57
  52.8 144.0 %reduce-scatter.3.cloned.1.call-start = ((), (), s32[]{:S(2)}) async-start(), calls=%async_computation.7 | async-start | bytes 5242880 | tf_op jit(solution)/shard_map/reduce_scatter | solution.py:75
  124.6 20.3 %copy-start.13 = (bf16[1024,256]{1,0:T(8,128)(2,1)S(1)}, bf16[1024,256]{1,0:T(8,128)(2,1)}, u32[]{:S(2)}) copy-start(bf16[1024,256]{1,0:T(8,128)(2,1)} %param.26) | copy-start | bytes 1572868
  124.6 20.3 %copy-start.15 = (f32[256]{0:T(256)S(1)}, f32[256]{0:T(256)}, u32[]{:S(2)}) copy-start(f32[256]{0:T(256)} %param.27) | copy-start | bytes 3076
  155.5 10.1 %all-to-all-start = ((s32[8,1,16]{2,1,0:T(1,128)}), s32[8,1,16]{2,1,0:T(1,128)S(1)}, u32[]{:S(2)}, u32[]{:S(2)}) async-start(s32[8,1,16]{2,1,0:T(1,128)} %bitcast.5), calls=%async_computation | async-start | bytes 8192 | tf_op jit(solution)/shard_map/all_to_all | solution.py:109
  165.7 43.1 %copy-start.2 = (bf16[2048,256]{1,0:T(8,128)(2,1)S(1)}, bf16[2048,256]{1,0:T(8,128)(2,1)}, u32[]{:S(2)}) copy-start(bf16[2048,256]{1,0:T(8,128)(2,1)} %param.19) | copy-start | bytes 3145732
  165.7 43.1 %copy-start.7 = (f32[256]{0:T(256)S(1)}, f32[256]{0:T(256)}, u32[]{:S(2)}) copy-start(f32[256]{0:T(256)} %param.30) | copy-start | bytes 3076
  165.7 43.1 %copy-start.8 = (f32[256]{0:T(256)S(1)}, f32[256]{0:T(256)}, u32[]{:S(2)}) copy-start(f32[256]{0:T(256)} %param.29) | copy-start | bytes 3076
  212.8 16.8 %copy-start.16 = (f32[256]{0:T(256)S(1)}, f32[256]{0:T(256)}, u32[]{:S(2)}) copy-start(f32[256]{0:T(256)} %param.32) | copy-start | bytes 3076
  214.4 12.5 %all-to-all-start.2 = ((bf16[8,16,256]{2,1,0:T(8,128)(2,1)}), bf16[8,16,256]{2,1,0:T(8,128)(2,1)S(1)}, u32[]{:S(2)}, u32[]{:S(2)}) async-start(bf16[8,16,256]{2,1,0:T(8,128)(2,1)} %convert_element_type.59), calls=%async_computation.3 | async-start | bytes 131072 | tf_op jit(solution)/shard_map/all_to_all | solution.py:106
  220.0 29.3 %all-gather.8.cloned.1.call-start = ((), (), s32[]{:S(2)}) async-start(), calls=%async_computation.8 | async-start | bytes 2621440 | tf_op jit(solution)/shard_map/all_gather | solution.py:122
  229.3 20.0 %copy-start.12 = (bf16[2,1024,256]{2,1,0:T(8,128)(2,1)S(1)}, bf16[2,1024,256]{2,1,0:T(8,128)(2,1)}, u32[]{:S(2)}) copy-start(bf16[2,1024,256]{2,1,0:T(8,128)(2,1)} %param.31) | copy-start | bytes 3145732
  229.3 20.0 %copy-start.14 = (bf16[256,1024]{1,0:T(8,128)(2,1)S(1)}, bf16[256,1024]{1,0:T(8,128)(2,1)}, u32[]{:S(2)}) copy-start(bf16[256,1024]{1,0:T(8,128)(2,1)} %param.33) | copy-start | bytes 1572868
  229.3 56.7 %reduce-scatter.5.cloned.1.call-start = ((), (), s32[]{:S(2)}) async-start(), calls=%async_computation.9 | async-start | bytes 2621440 | tf_op jit(solution)/shard_map/reduce_scatter | solution.py:126
  254.7 38.6 %copy-start.3 = (bf16[1024,256]{1,0:T(8,128)(2,1)S(1)}, bf16[1024,256]{1,0:T(8,128)(2,1)}, u32[]{:S(2)}) copy-start(bf16[1024,256]{1,0:T(8,128)(2,1)} %param.18) | copy-start | bytes 1572868
  254.7 38.6 %copy-start.9 = (f32[256]{0:T(256)S(1)}, f32[256]{0:T(256)}, u32[]{:S(2)}) copy-start(f32[256]{0:T(256)} %param.35) | copy-start | bytes 3076
  254.7 38.6 %copy-start.10 = (f32[256]{0:T(256)S(1)}, f32[256]{0:T(256)}, u32[]{:S(2)}) copy-start(f32[256]{0:T(256)} %param.34) | copy-start | bytes 3076
Sparse Core Ops, SparseCore 0:
  9.6 25.5 all-gather.3
  36.7 34.9 all-gather.5
  154.2 42.5 reduce-scatter.2
  229.4 19.8 all-gather.7
  254.8 31.1 reduce-scatter.4
where the time goes:
time: 303 us; the launch traced here: 302 us
  waiting for transfers between devices  165 us (54%)
  local copies, waits for them, and re-layouts  57.3 us (19%)
  matrix products  21.1 us (7%)
  blocking collectives  16 us (5%)
  starting transfers between devices  15.3 us (5%)
  between operations  14.8 us (5%)
  other arithmetic  13.1 us (4%)
    all_to_all x1, waiting for transfers between devices, shards(): lax.all_to_all(picked, 'patch', split_axis=0, concat_axis=0, tiled=True)  47.5 us
    reduce_scatter x1, waiting for transfers between devices, shards(): lax.psum_scatter(node_terms.astype(jnp.bfloat16), 'pair', scatter_dimensi...  30.6 us
    reduce_scatter x1, waiting for transfers between devices, shards(): lax.psum_scatter(edge_terms.astype(jnp.bfloat16), 'pair', scatter_dimensi...  29.8 us
    all_gather x1, waiting for transfers between devices, shards(): full_nodes = lax.all_gather(node_latents, 'pair', axis=1, tiled=True)  26.1 us
    gather x1, local copies, waits for them, and re-layouts, shards(): halo_pairs[edge_owner * halo_size + jnp.maximum(receivers, 0), 1]  20.5 us
    gather x1, local copies, waits for them, and re-layouts, shards(): sender_rows = halo_pairs[jnp.maximum(senders, 0), 0]  20.3 us
    all_gather x1, waiting for transfers between devices, shards(): lax.all_gather(aggregated, 'pair', axis=1, tiled=True)  16.3 us
    psum x1, blocking collectives, shards(): lax.psum((jnp.sum(edge_mixed, axis=1), jnp.sum(edge_mixed * edge_mixed, a...  10.1 us
  transfers between devices with their start and end apart: 8, of which 7 were waited for; matrix products, arithmetic and copies ran while one was open for 21% of the time, Pallas kernels for 0%

commit v1 on v0

v1 whole, which is shorter than its diff:
```python
import functools

import jax
import jax.numpy as jnp
from jax import lax
from jax.experimental import pallas as pl
from jax.experimental.pallas import tpu as pltpu
from jax.sharding import PartitionSpec as P

RT = 16
EPS = 1e-05
LANES = 128
TAIL = 16


BF = jnp.bfloat16
F32 = jnp.float32
VMEM = pl.BlockSpec(memory_space=pltpu.VMEM)
SMEM = pl.BlockSpec(memory_space=pltpu.SMEM)
ANY = pl.BlockSpec(memory_space=pl.ANY)


def swap(value, axis, mask):
    size = lax.axis_size(axis)
    return lax.ppermute(value, axis, [(i, i ^ mask) for i in range(size)])


def column(row):
    wide = jnp.broadcast_to(row.astype(F32), (LANES, row.shape[1]))
    return jnp.transpose(wide).astype(jnp.int32)


def hot_lanes(index, start, count):
    parts = []
    for at in range(0, count, LANES):
        width = min(LANES, count - at)
        lane = lax.broadcasted_iota(jnp.int32, (index.shape[0], width), 1) + (start + at)
        parts.append(jnp.where(index[:, :width] == lane, 1.0, 0.0).astype(BF))
    return parts[0] if len(parts) == 1 else jnp.concatenate(parts, axis=1)


def pick_kernel(count, groups, order_ref, index_ref, *refs):
    tables, outs = refs[:count], refs[count:]
    rows = outs[0].shape[0]
    for g in range(groups):
        index = column(index_ref[pl.ds(order_ref[g], 1), :])[:rows]
        total = None
        start = 0
        for table in tables:
            hot = hot_lanes(index, start, table.shape[0])
            part = jnp.dot(hot, table[...], preferred_element_type=F32)
            total = part if total is None else total + part
            start += table.shape[0]
        outs[g][...] = total.astype(BF)


def pick_rows(order, index, tables, rows):
    groups, width = index.shape[0], tables[0].shape[1]
    depth = sum(t.shape[0] for t in tables)
    return pl.pallas_call(
        functools.partial(pick_kernel, len(tables), groups),
        in_specs=[SMEM] + [VMEM] * (1 + len(tables)),
        out_specs=[VMEM] * groups,
        out_shape=[jax.ShapeDtypeStruct((rows, width), BF)] * groups,
        cost_estimate=pl.CostEstimate(
            flops=2 * groups * rows * depth * width,
            bytes_accessed=2 * (groups * rows + depth) * width,
            transcendentals=0,
        ),
    )(order, index, *tables)


def split_kernel(size, per, order_ref, in_ref, vectors_ref, *outs):
    value = vectors_ref[...]
    high = value.astype(BF).astype(F32)
    middle = (value - high).astype(BF).astype(F32)
    low = value - high - middle
    parts = [high, middle, low]
    parts.append(jnp.zeros((TAIL - 3 * value.shape[0], value.shape[1]), F32))
    tail = jnp.concatenate(parts, axis=0).astype(BF)
    for k, out in enumerate(outs):
        for i in range(per):
            at = pl.multiple_of(order_ref[k * per + i] * size, size)
            out[i * size : (i + 1) * size, :] = in_ref[pl.ds(at, size), :]
        out[per * size :, :] = tail


def unpack_vectors(tail, count):
    wide = tail.astype(F32)
    return wide[:count] + wide[count : 2 * count] + wide[2 * count : 3 * count]


def join_kernel(size, per, order_ref, *refs):
    out = refs[-1]
    for k, part in enumerate(refs[:-1]):
        for i in range(per):
            at = pl.multiple_of(order_ref[k * per + i] * size, size)
            out[pl.ds(at, size), :] = part[i * size : (i + 1) * size, :]


def split(order, size, per, value, vectors):
    parts = order.shape[0] // per
    return pl.pallas_call(
        functools.partial(split_kernel, size, per),
        in_specs=[SMEM, VMEM, VMEM],
        out_specs=[VMEM] * parts,
        out_shape=[jax.ShapeDtypeStruct((size * per + TAIL, value.shape[1]), BF)] * parts,
    )(order, value, vectors)


def pack_edge_kernel(flags_ref, in_ref, ends_ref, out_ref, packed, *pieces):
    odd = flags_ref[0]
    full, local = in_ref.shape
    packed[:full, :] = in_ref[...]
    step = 2 * LANES
    for side in range(2):
        lane = lax.broadcasted_iota(jnp.int32, (LANES, step), 1)
        row = lax.broadcasted_iota(jnp.int32, (LANES, step), 0)
        hot = jnp.where(lane == 2 * row + side, 1.0, 0.0).astype(BF)
        for n in range(full // LANES):
            part = jnp.dot(hot, ends_ref[n * step : (n + 1) * step, :], preferred_element_type=F32)
            base = (1 + side) * full + n * LANES
            packed[base : base + LANES, :] = part.astype(BF)
    for c in range(full // local):
        base = 3 * full + c * local
        packed[base : base + local, :] = out_ref[:, c * local : (c + 1) * local]
    copy_pieces(odd, packed, pieces)


def pack_node_kernel(flags_ref, in_ref, out_ref, packed, *pieces):
    odd = flags_ref[0]
    rows, local = in_ref.shape
    packed[:rows, :] = in_ref[...]
    for c in range(out_ref.shape[1] // local):
        base = rows + c * local
        packed[base : base + local, :] = out_ref[:, c * local : (c + 1) * local]
    copy_pieces(odd, packed, pieces)


def copy_pieces(odd, packed, pieces):
    start = 0
    for piece in pieces:
        half = piece.shape[0]
        piece[...] = packed[pl.ds(pl.multiple_of(start + odd * half, half), half), :]
        start += 2 * half


def pack(kernel, flags, chunks, *weights):
    total = sum(size for _, size in chunks)
    local = weights[0].shape[1]
    return pl.pallas_call(
        kernel,
        in_specs=[SMEM] + [VMEM] * len(weights),
        out_specs=[VMEM] * (1 + len(chunks)),
        out_shape=[jax.ShapeDtypeStruct((total, local), BF)]
        + [jax.ShapeDtypeStruct((size // 2, local), BF) for _, size in chunks],
    )(flags, *weights)


def join(order, size, per, values):
    return pl.pallas_call(
        functools.partial(join_kernel, size, per),
        in_specs=[SMEM] + [VMEM] * len(values),
        out_specs=VMEM,
        out_shape=jax.ShapeDtypeStruct((size * order.shape[0], values[0].shape[1]), BF),
    )(order, *values)


def silu(value):
    return value / (1.0 + jnp.exp(-value))


def finish(mixed, old, gain, shift, live):
    width = mixed.shape[1]
    mean = jnp.sum(mixed, axis=1, keepdims=True) / width
    square = jnp.sum(mixed * mixed, axis=1, keepdims=True) / width
    norm = (mixed - mean) * lax.rsqrt(square - mean * mean + EPS) * gain + shift
    return jnp.where(live, old + norm, old).astype(BF)


def weight_copies(odd, chunks, refs, store, sems):
    own, near, far = refs[0], refs[1], refs[2:]
    copies = [
        [pltpu.make_async_copy(own, store.at[0], sems.at[0])],
        [pltpu.make_async_copy(near, store.at[1], sems.at[1])],
    ]
    at = 2
    for k in (2, 3):
        mine = []
        for start, size in chunks:
            for slot in (odd, 1 - odd):
                half = size // 2
                row = pl.multiple_of(start + slot * half, half)
                mine.append(pltpu.make_async_copy(far[at - 2], store.at[k, pl.ds(row, half)], sems.at[at]))
                at += 1
        copies.append(mine)
    return copies


def edge_kernel(pairs, groups, chunks, flags_ref, segrow_ref, ids_ref, *refs):
    e_refs, refs = refs[:pairs], refs[pairs:]
    s_refs, refs = refs[:pairs], refs[pairs:]
    count = 2 + 4 * len(chunks)
    w_refs, refs = refs[:count], refs[count:]
    outs, refs = refs[:pairs], refs[pairs:]
    sum_refs, refs = refs[:groups], refs[groups:]
    both, r_all, hidden, new_all, wide, store, sems = refs
    me, odd, turn = flags_ref[0], flags_ref[1], flags_ref[2]
    copies = weight_copies(odd, chunks, w_refs, store, sems)
    for group in copies:
        for copy in group:
            copy.start()
    rows, full = new_all.shape
    local = full // pairs
    tile = rows // groups
    bias = []
    for k in range(pairs):
        at = pl.multiple_of((me ^ k) * local, local)
        both[:, pl.ds(at, local)] = e_refs[k][:rows, :]
        both[:, pl.ds(at + full, local)] = s_refs[k][:rows, :]
        r_all[:, pl.ds(at, local)] = s_refs[k][rows:, :]
        vectors = unpack_vectors(e_refs[k][rows:, :], 3)
        bias.append(vectors[:1])
        wide[:1, pl.ds(at, local)] = vectors[1:2]
        wide[1:2, pl.ds(at, local)] = vectors[2:3]
    segments, hots = [], []
    for g in range(groups):
        segment = column(segrow_ref[g : g + 1, :])
        segments.append(segment)
        hots.append(hot_lanes(segment, 0, RT))
    for k in range(pairs):
        for copy in copies[k]:
            copy.wait()
        receivers = jnp.dot(r_all[...], store[k, 2 * full : 3 * full, :], preferred_element_type=F32).astype(BF)
        for g in range(groups):
            at = slice(g * tile, (g + 1) * tile)
            pre = jnp.dot(both[at, :], store[k, : 2 * full, :], preferred_element_type=F32)
            pre += jnp.dot(hots[g], receivers[g * RT : (g + 1) * RT], preferred_element_type=F32)
            hidden[at, k * local : (k + 1) * local] = silu(pre + bias[k]).astype(BF)
    for g in range(groups):
        at = slice(g * tile, (g + 1) * tile)
        mixed = []
        for c in range(pairs):
            base = 3 * full + c * local
            total = None
            for k in range(pairs):
                part = jnp.dot(
                    hidden[at, k * local : (k + 1) * local],
                    store[k, base : base + local, :],
                    preferred_element_type=F32,
                )
                total = part if total is None else total + part
            mixed.append(total)
        mixed = jnp.concatenate(mixed, axis=1)
        live = segments[g][:, :1] < RT
        old = both[at, :full].astype(F32)
        new_all[at, :] = finish(mixed, old, wide[:1, :], wide[1:2, :], live)
    for t in range(groups):
        g = t ^ turn
        segrow = segrow_ref[pl.ds(g, 1), :]
        member = segrow == lax.broadcasted_iota(jnp.int32, (RT, tile), 0)
        member = jnp.where(member, 1.0, 0.0).astype(BF)
        new = new_all[pl.ds(pl.multiple_of(g * tile, tile), tile), :]
        total = jnp.dot(member, new, preferred_element_type=F32)
        sum_refs[t][:, :full] = total.astype(BF)
        sum_refs[t][:, full:] = ids_ref[pl.ds(pl.multiple_of(g * RT, RT), RT), :]
    for k in range(pairs):
        at = pl.ds(pl.multiple_of((me ^ k) * local, local), local)
        outs[k][...] = new_all[:, at]


def node_kernel(pairs, sources, chunks, flags_ref, count_ref, from_ref, list_ref, *refs):
    n_refs, refs = refs[:pairs], refs[pairs:]
    r_refs, refs = refs[:sources], refs[sources:]
    count = 2 + 4 * len(chunks)
    w_refs, refs = refs[:count], refs[count:]
    outs, refs = refs[:pairs], refs[pairs:]
    n_all, sums, nodes_of, wide, store, sems = refs
    me, odd = flags_ref[0], flags_ref[1]
    copies = weight_copies(odd, chunks, w_refs, store, sems)
    for group in copies:
        for copy in group:
            copy.start()
    rows, full = n_all.shape
    local = full // pairs
    first = me * rows
    bias = []
    for k in range(pairs):
        at = pl.ds(pl.multiple_of((me ^ k) * local, local), local)
        n_all[:, at] = n_refs[k][:rows, :]
        vectors = unpack_vectors(n_refs[k][rows:, :], 3)
        bias.append(vectors[:1])
        wide[:1, at] = vectors[1:2]
        wide[1:2, at] = vectors[2:3]
    halo = list_ref.shape[1]
    start = 0
    for r in r_refs:
        depth = r.shape[0]
        sums[start : start + depth, :] = r[:, :full]
        for at in range(0, depth, RT):
            ids = r[at : at + RT, full:].astype(F32)[:, :1].astype(jnp.int32)
            names = list_ref[pl.ds(from_ref[(start + at) // RT], 1), :]
            found = ids == lax.broadcasted_iota(jnp.int32, (RT, halo), 1)
            node = jnp.sum(jnp.where(found, names.astype(F32), 0.0), axis=1, keepdims=True)
            node = jnp.where(ids >= 0, node, -1.0)
            nodes_of[start + at : start + at + RT, :] = jnp.broadcast_to(node, (RT, LANES))
        start += depth
    total = None
    for at in range(0, start, LANES):
        row = jnp.transpose(nodes_of[at : at + LANES, :])[:1].astype(jnp.int32)
        hot = row == lax.broadcasted_iota(jnp.int32, (rows, LANES), 0) + first
        hot = jnp.where(hot, 1.0, 0.0).astype(BF)
        part = jnp.dot(hot, sums[at : at + LANES, :], preferred_element_type=F32)
        total = part if total is None else total + part
    aggregated = total.astype(BF)
    nodes = n_all[...]
    mixed = [None] * pairs
    for k in range(pairs):
        for copy in copies[k]:
            copy.wait()
        pre = jnp.dot(nodes, store[k, :full, :], preferred_element_type=F32)
        pre += jnp.dot(aggregated, store[k, full : 2 * full, :], preferred_element_type=F32)
        hidden = silu(pre + bias[k]).astype(BF)
        for c in range(pairs):
            base = 2 * full + c * local
            part = jnp.dot(hidden, store[k, base : base + local, :], preferred_element_type=F32)
            mixed[c] = part if k == 0 else mixed[c] + part
    live = lax.broadcasted_iota(jnp.int32, (rows, 1), 0) + first < count_ref[0]
    mixed = jnp.concatenate(mixed, axis=1)
    n_all[...] = finish(mixed, nodes.astype(F32), wide[:1, :], wide[1:2, :], live)
    for k in range(pairs):
        at = pl.ds(pl.multiple_of((me ^ k) * local, local), local)
        outs[k][...] = n_all[:, at]


def layer(
    node_latents,
    edge_latents,
    edge_sender,
    edge_receiver,
    block_owner,
    node_counts,
    halo_nodes,
    w_endpoints,
    w_edge_in,
    edge_bias,
    w_edge_out,
    edge_gain,
    edge_shift,
    w_node_in,
    node_bias,
    w_node_out,
    node_gain,
    node_shift,
):
    patches = lax.axis_size("patch")
    pairs = lax.axis_size("pair")
    patch = lax.axis_index("patch").astype(jnp.int32)
    me = lax.axis_index("pair").astype(jnp.int32)
    full, local = w_edge_in.shape
    node_total = node_latents.shape[0]
    edge_total = edge_latents.shape[0]
    blocks, tile = edge_sender.shape
    halo = halo_nodes.shape[2]
    mine = blocks // pairs
    rows = edge_total // pairs
    quarter = node_total // pairs
    if pairs != 4 or patches % 2 or mine % 2:
        raise ValueError("unsupported mesh")
    peers = jnp.arange(pairs, dtype=jnp.int32) ^ me
    odd = patch % 2
    by_swap = patches <= 8 and halo % LANES == 0
    direct = blocks == patches and mine == 2
    order = jnp.arange(patches, dtype=jnp.int32)
    order = order ^ patch if by_swap else order

    def to_pairs(pieces):
        far = {k: swap(pieces[k], "pair", k) for k in (2, 3, 1)}
        return [pieces[0]] + [far[k] for k in range(1, pairs)]

    send_list = halo_nodes[0]
    if by_swap:
        picked = pick_rows(order, send_list, [node_latents], halo)
        table = [picked[0]] + [swap(picked[k], "patch", k) for k in range(1, patches)]
    else:
        groups = patches * halo // 256
        flat = send_list.reshape(groups, 256)
        picked = pick_rows(jnp.arange(groups, dtype=jnp.int32), flat, [node_latents], 256)
        table = [lax.all_to_all(jnp.concatenate(picked, axis=0), "patch", 0, 0, tiled=True)]

    def gather_slices(packed, *pieces):
        parts = [packed, swap(packed, "pair", 1)]
        far, far_core = [], []
        for piece in pieces:
            near = swap(piece, "pair", 2)
            other = swap(near, "patch", 1)
            far += [near, other]
            far_core += [swap(near, "pair", 1), swap(other, "pair", 1)]
        return parts + far + far_core

    flags = jnp.stack([me, odd, odd if direct else 0 * odd])
    e_chunks = ((0, 2 * full), (2 * full, 2 * full))
    ends = w_endpoints.reshape(2 * full, local)
    e_weights = gather_slices(*pack(pack_edge_kernel, odd.reshape(1), e_chunks, w_edge_in, ends, w_edge_out))
    e_vectors = jnp.stack([edge_bias, edge_gain, edge_shift])
    n_vectors = jnp.stack([node_bias, node_gain, node_shift])

    if direct:
        spots = jnp.arange(blocks, dtype=jnp.int32)
        block_at = jnp.sum(jnp.where(block_owner[None, :] == spots[:, None], spots[None, :], 0), axis=1)
    else:
        block_at = jnp.arange(blocks, dtype=jnp.int32)
    pair_blocks = block_at.reshape(pairs, mine)[peers].reshape(-1)

    previous = jnp.concatenate([jnp.full((blocks, 1), -2, jnp.int32), edge_receiver[:, :-1]], axis=1)
    segment = jnp.cumsum((edge_receiver != previous).astype(jnp.int32), axis=1) - 1
    segment = jnp.where(edge_receiver >= 0, segment, RT)
    member = segment[:, None, :] == jnp.arange(RT, dtype=jnp.int32)[None, :, None]
    tile_ids = jnp.max(jnp.where(member, edge_receiver[:, None, :], -1), axis=2)

    def place(owner):
        return (owner ^ patch if by_swap else owner) * halo

    sender = jnp.maximum(edge_sender, 0)
    sender_at = place(sender // halo) + sender % halo
    receiver_at = place(block_owner)[:, None] + jnp.maximum(tile_ids, 0)
    short = -(mine * RT) % LANES
    wanted = jnp.concatenate(
        [
            sender_at[pair_blocks].reshape(pairs, rows),
            receiver_at[pair_blocks].reshape(pairs, mine * RT),
            jnp.zeros((pairs, short), jnp.int32),
        ],
        axis=1,
    )
    my_blocks = pair_blocks[:mine]
    my_segment = segment[my_blocks]
    my_ids = jnp.broadcast_to(tile_ids[my_blocks].reshape(-1, 1), (mine * RT, LANES)).astype(BF)

    e_parts = to_pairs(split(pair_blocks, tile, mine, edge_latents, e_vectors))
    groups = jnp.arange(pairs, dtype=jnp.int32)
    seen = pick_rows(groups, wanted, table, rows + mine * RT)
    s_parts = to_pairs(seen)

    wide = full + LANES
    results = pl.pallas_call(
        functools.partial(edge_kernel, pairs, mine, e_chunks),
        in_specs=[SMEM] + [VMEM] * (2 + 2 * pairs) + [ANY] * len(e_weights),
        out_specs=[VMEM] * (pairs + mine),
        out_shape=[jax.ShapeDtypeStruct((rows, local), BF)] * pairs
        + [jax.ShapeDtypeStruct((RT, wide), BF)] * mine,
        scratch_shapes=[
            pltpu.VMEM((rows, 2 * full), BF),
            pltpu.VMEM((mine * RT, full), BF),
            pltpu.VMEM((rows, full), BF),
            pltpu.VMEM((rows, full), BF),
            pltpu.VMEM((8, full), F32),
            pltpu.VMEM((pairs, 4 * full, local), BF),
            pltpu.SemaphoreType.DMA((len(e_weights),)),
        ],
        cost_estimate=pl.CostEstimate(
            flops=6 * rows * full * full, bytes_accessed=10 * full * full, transcendentals=rows * full
        ),
    )(
        flags,
        my_segment,
        my_ids,
        *e_parts,
        *s_parts,
        *e_weights,
    )
    new_edges, sums = results[:pairs], results[pairs:]

    if direct:
        got = []
        for t in range(mine):
            route = []
            for p in range(patches):
                for j in range(pairs):
                    to = (j * mine + (p % 2 ^ t)) * pairs + p // mine
                    route.append((p * pairs + j, to))
            got.append(lax.ppermute(sums[t], ("patch", "pair"), route))
        got = to_pairs([jnp.concatenate(got, axis=0)] * pairs)
        near = jnp.stack([odd, 1 - odd])
        sources = (peers[:, None] * mine + near[None, :]).reshape(-1)
    else:
        all_sums = jnp.stack(to_pairs([jnp.stack(sums)] * pairs)).reshape(blocks, RT * wide)
        owners = block_owner.reshape(pairs, mine)[peers].reshape(-1)
        take = owners[None, :] == jnp.arange(patches, dtype=jnp.int32)[:, None]
        sent = jnp.dot(take.astype(BF), all_sums, preferred_element_type=F32).reshape(patches, RT, wide)
        none = jnp.any(take, axis=1)[:, None, None] | (jnp.arange(wide)[None, None, :] < full)
        sent = jnp.where(none, sent, -1.0).astype(BF)
        got = [lax.all_to_all(sent, "patch", 0, 0, tiled=True).reshape(patches * RT, wide)]
        sources = jnp.arange(patches, dtype=jnp.int32)

    new_edges = to_pairs(new_edges)
    edges_out = join(pair_blocks, tile, mine, new_edges)

    n_chunks = ((0, 2 * full), (2 * full, full))
    n_weights = gather_slices(
        *pack(pack_node_kernel, odd.reshape(1), n_chunks, w_node_in.reshape(2 * full, local), w_node_out)
    )
    n_parts = to_pairs(split(peers, quarter, 1, node_latents, n_vectors))
    new_nodes = pl.pallas_call(
        functools.partial(node_kernel, pairs, len(got), n_chunks),
        in_specs=[SMEM] * 3 + [VMEM] * (1 + pairs + len(got)) + [ANY] * len(n_weights),
        out_specs=[VMEM] * pairs,
        out_shape=[jax.ShapeDtypeStruct((quarter, local), BF)] * pairs,
        scratch_shapes=[
            pltpu.VMEM((quarter, full), BF),
            pltpu.VMEM((patches * RT, full), BF),
            pltpu.VMEM((patches * RT, LANES), F32),
            pltpu.VMEM((8, full), F32),
            pltpu.VMEM((pairs, 3 * full, local), BF),
            pltpu.SemaphoreType.DMA((len(n_weights),)),
        ],
        cost_estimate=pl.CostEstimate(
            flops=6 * quarter * full * full, bytes_accessed=8 * full * full, transcendentals=quarter * full
        ),
    )(
        flags,
        node_counts,
        sources,
        send_list,
        *n_parts,
        *got,
        *n_weights,
    )
    nodes_out = join(peers, quarter, 1, to_pairs(new_nodes))
    return (nodes_out, edges_out)


def solution(mesh):
    return jax.shard_map(
        layer,
        mesh=mesh,
        in_specs=(
            P("patch", "pair"),
            P("patch", "pair"),
            P("patch", None),
            P("patch", None),
            P("patch"),
            P("patch"),
            P("patch", None, None),
            P(None, None, "pair"),
            P(None, "pair"),
            P("pair"),
            P("pair", None),
            P("pair"),
            P("pair"),
            P(None, None, "pair"),
            P("pair"),
            P("pair", None),
            P("pair"),
            P("pair"),
        ),
        out_specs=(P("patch", "pair"), P("patch", "pair")),
        check_vma=False,
    )
```

time: 303 us -> 188 us (0.62)
  waiting for transfers between devices: 165 us -> 81.9 us
  local copies, waits for them, and re-layouts: 57.3 us -> 12 us
  Pallas kernels: 0 us -> 41 us
  starting transfers between devices: 15.3 us -> 44.1 us
  matrix products: 21.1 us -> 0 us
  blocking collectives: 16 us -> 0 us
  between operations: 14.8 us -> 1.74 us
  other arithmetic: 13.1 us -> 7.19 us
    ppermute x0 -> x45, waiting for transfers between devices: none -> 81.9 us  [the longest x43 79.3 us: swap(): return lax.ppermute(value, axis, [(i, i ^ mask) for i in range(size)])]
    all_to_all x3 -> x0, waiting for transfers between devices: 60.7 us -> none  [the longest x1 47.5 us: shards(): lax.all_to_all(picked, 'patch', split_axis=0, concat_axis=0, tiled=True)]
    reduce_scatter x2 -> x0, waiting for transfers between devices: 60.4 us -> none  [the longest x1 30.6 us: shards(): lax.psum_scatter(node_terms.astype(jnp.bfloat16), 'pair', scatter_dimensi...]
    gather x4 -> x5, local copies, waits for them, and re-layouts: 51.2 us -> 3.36 us  [the longest x1 1.13 us: layer(): my_segment = segment[my_blocks]]
    ppermute x0 -> x45, starting transfers between devices: none -> 44.1 us  [the longest x43 42.2 us: swap(): return lax.ppermute(value, axis, [(i, i ^ mask) for i in range(size)])]
    all_gather x3 -> x0, waiting for transfers between devices: 42.4 us -> none  [the longest x1 26.1 us: shards(): full_nodes = lax.all_gather(node_latents, 'pair', axis=1, tiled=True)]
    pallas_call x0 -> x10, Pallas kernels: none -> 41 us  [the longest x1 10.8 us: layer(): pl.pallas_call(functools.partial(edge_kernel, pairs, mine, e_chunks), in_...]
    dot_general x5 -> x0, matrix products: 21.1 us -> none  [the longest x1 9.14 us: shards(): jnp.dot(edge_hidden, w_edge_out, preferred_element_type=jnp.float32)]
  transfers between devices with their start and end apart: 8 -> 45, of which waited for: 7 -> 14; matrix products, arithmetic and copies ran while one was open for 21% -> 8% of each run, Pallas kernels for 0% -> 15%
where the time goes in v1:
time: 188 us
  waiting for transfers between devices  81.9 us (44%)
  starting transfers between devices  44.1 us (23%)
  Pallas kernels  41 us (22%)
  local copies, waits for them, and re-layouts  12 us (6%)
  other arithmetic  7.19 us (4%)
    ppermute x43, waiting for transfers between devices, swap(): return lax.ppermute(value, axis, [(i, i ^ mask) for i in range(size)])  79.3 us
    ppermute x43, starting transfers between devices, swap(): return lax.ppermute(value, axis, [(i, i ^ mask) for i in range(size)])  42.2 us
    pallas_call x1, Pallas kernels, layer(): pl.pallas_call(functools.partial(edge_kernel, pairs, mine, e_chunks), in_...  10.8 us
    pallas_call x2, Pallas kernels, pick_rows(): pl.pallas_call(functools.partial(pick_kernel, len(tables), groups), in_sp...  7.93 us
    pallas_call x1, Pallas kernels, layer(): pl.pallas_call(functools.partial(node_kernel, pairs, len(got), n_chunks),...  7.41 us
    pallas_call x2, Pallas kernels, pack(): pl.pallas_call(kernel, in_specs=[SMEM] + [VMEM] * len(weights), out_specs...  6.47 us
    pallas_call x2, Pallas kernels, split(): pl.pallas_call(functools.partial(split_kernel, size, per), in_specs=[SMEM...  4.19 us
    pallas_call x2, Pallas kernels, join(): pl.pallas_call(functools.partial(join_kernel, size, per), in_specs=[SMEM]...  4.17 us
  transfers between devices with their start and end apart: 45, of which 14 were waited for; matrix products, arithmetic and copies ran while one was open for 8% of the time, Pallas kernels for 15%

profile of v1, /device:TPU:0, one launch (start us, length us, event | category | flops | bytes accessed | tf_op | source)
XLA Modules:
  0.0 187.9 jit_solution(10750219604218644277)
XLA Ops:
  0.7 1.2 iota_xor_fusion
  2.0 3.2 %shard_map.187 = (bf16[256,256]{1,0:T(8,128)(2,1)}, bf16[256,256]{1,0:T(8,128)(2,1)}, bf16[256,256]{1,0:T(8,128)(2,1)}, bf16[256,256]{1,0:T(8,128)(2,1)}, bf16[2...) custom-call(s32[8]{0:T(128)} %get-tuple-element.74.order_ref, ...), custom_call_target="tpu_custom_call" | custom-call | flops 1073741824 | bytes 1572864 | tf_op jit(solution)/shard_map/pallas_call | solution.py:60
  5.1 5.0 %collective-permute-start.10 = (bf16[256,256]{1,0:T(8,128)(2,1)}, bf16[256,256]{1,0:T(8,128)(2,1)S(1)}, u32[]{:S(2)}, u32[]{:S(2)}) collective-permute-start(bf16[256,256]{1,0:T(8,128)(2,1)} %get-tuple-element.51), channel_id=1, source_target_pairs={{0,20},{4,16},{8,28},{12,24},{16,4},{20,0},{24,12},{28,8},{1,21},{... | collective-permute-start | bytes 393224 | tf_op jit(solution)/shard_map/ppermute | solution.py:25
  10.1 1.3 collective-permute-start.11
  11.4 2.5 %collective-permute-start.12 = (bf16[256,256]{1,0:T(8,128)(2,1)}, bf16[256,256]{1,0:T(8,128)(2,1)S(1)}, u32[]{:S(2)}, u32[]{:S(2)}) collective-permute-start(bf16[256,256]{1,0:T(8,128)(2,1)} %get-tuple-element.53), channel_id=1, source_target_pairs={{0,28},{4,24},{8,20},{12,16},{16,12},{20,8},{24,4},{28,0},{1,29},{... | collective-permute-start | bytes 393224 | tf_op jit(solution)/shard_map/ppermute | solution.py:25
  13.9 1.5 collective-permute-start.6
  18.2 5.0 %collective-permute-done.10.refs_5_ = bf16[256,256]{1,0:T(8,128)(2,1)S(1)} collective-permute-done((bf16[256,256]{1,0:T(8,128)(2,1)}, bf16[256,256]{1,0:T(8,128)(2,1)S(1)}, u32[]{:S(2)}, u32[]{:S(2)}) %collective-permute-start.10) | collective-permute-done | bytes 131104 | tf_op jit(solution)/shard_map/ppermute | solution.py:25
  23.2 4.6 %collective-permute-start.9 = (bf16[256,256]{1,0:T(8,128)(2,1)}, bf16[256,256]{1,0:T(8,128)(2,1)S(1)}, u32[]{:S(2)}, u32[]{:S(2)}) collective-permute-start(bf16[256,256]{1,0:T(8,128)(2,1)} %get-tuple-element.50), channel_id=1, source_target_pairs={{0,16},{4,20},{8,24},{12,28},{16,0},{20,4},{24,8},{28,12},{1,17},{... | collective-permute-start | bytes 393224 | tf_op jit(solution)/shard_map/ppermute | solution.py:25
  28.5 1.2 reshape.135.ends_ref
  29.7 3.6 %shard_map.189 = (bf16[4096,256]{1,0:T(8,128)(2,1)}, bf16[1024,256]{1,0:T(8,128)(2,1)}, bf16[1024,256]{1,0:T(8,128)(2,1)}) custom-call(s32[1]{0:T(128)} %bitcast.1.flags_ref, bf16[1024,256]{1,0:T(8,128)(2,1)} %in_ref.5, bf16[2048,256]{1,0:T(8,128)(2,1)} %reshape.135.ends_ref, bf16[256,1024]{1,0:T(8,128)(2,1)} %out_ref.2), custom_call_target="tpu_custom_call" | custom-call | tf_op jit(solution)/shard_map/pallas_call | solution.py:151
  35.8 2.9 %shard_map.191 = (bf16[3072,256]{1,0:T(8,128)(2,1)}, bf16[1024,256]{1,0:T(8,128)(2,1)}, bf16[512,256]{1,0:T(8,128)(2,1)}) custom-call(s32[1]{0:T(128)} %bitcast.1.flags_ref, bf16[2048,256]{1,0:T(8,128)(2,1)} %bitcast.24, bf16[256,1024]{1,0:T(8,128)(2,1)} %out_ref.3), custom_call_target="tpu_custom_call" | custom-call | tf_op jit(solution)/shard_map/pallas_call | solution.py:151
  38.7 1.9 %shard_map.185 = (bf16[272,256]{1,0:T(8,128)(2,1)}, bf16[272,256]{1,0:T(8,128)(2,1)}, bf16[272,256]{1,0:T(8,128)(2,1)}, bf16[272,256]{1,0:T(8,128)(2,1)}) custom-call(s32[4]{0:T(128)} %iota_xor_fusion.1.order_ref, bf16[1024,256]{1,0:T(8,128)(2,1)} %refs_0_.1, f32[3,256]{1,0:T(4,128)} %pad_maximum_fusion.vectors_ref), custom_call_target="tpu_custom_call" | custom-call | tf_op jit(solution)/shard_map/pallas_call | solution.py:103
  40.6 2.3 %shard_map.186 = (bf16[528,256]{1,0:T(8,128)(2,1)}, bf16[528,256]{1,0:T(8,128)(2,1)}, bf16[528,256]{1,0:T(8,128)(2,1)}, bf16[528,256]{1,0:T(8,128)(2,1)}) custom-call(s32[8]{0:T(128)} %reshape.131.order_ref, bf16[2048,256]{1,0:T(8,128)(2,1)} %in_ref.4, f32[3,256]{1,0:T(4,128)} %pad_maximum_fusion.1.vectors_ref), custom_call_target="tpu_custom_call" | custom-call | tf_op jit(solution)/shard_map/pallas_call | solution.py:103
  43.4 1.5 collective-permute-start.4
  46.1 0.9 collective-permute-done.refs_1_
  47.0 1.3 collective-permute-start.5
  48.9 4.8 %shard_map.188 = (bf16[544,256]{1,0:T(8,128)(2,1)}, bf16[544,256]{1,0:T(8,128)(2,1)}, bf16[544,256]{1,0:T(8,128)(2,1)}, bf16[544,256]{1,0:T(8,128)(2,1)}) custom-call(s32[4]{0:T(128)} %iota.27.order_ref, s32[4,640]{1,0:T(4,128)} %add_add_fusion.index_ref, bf16[256,256]{1,0:T(8,128)(2,1)} %get-tuple-element.46.refs_0_, bf16[256,256]{1,0:T(8,128)(2,1)} %copy-done.36, ...), custom_call_target="tpu_custom_call" | custom-call | flops 2281701376 | bytes 2162688 | tf_op jit(solution)/shard_map/pallas_call | solution.py:60
  53.7 4.9 %collective-permute-done.33.refs_12_ = bf16[512,256]{1,0:T(8,128)(2,1)S(1)} collective-permute-done((bf16[512,256]{1,0:T(8,128)(2,1)}, bf16[512,256]{1,0:T(8,128)(2,1)S(1)}, u32[]{:S(2)}, u32[]{:S(2)}) %collective-permute-start.33) | collective-permute-done | bytes 262176 | tf_op jit(solution)/shard_map/ppermute | solution.py:25
  58.6 1.6 collective-permute-start.17
  60.7 2.8 %collective-permute-done.5.refs_3_ = bf16[528,256]{1,0:T(8,128)(2,1)} collective-permute-done((bf16[528,256]{1,0:T(8,128)(2,1)}, bf16[528,256]{1,0:T(8,128)(2,1)}, u32[]{:S(2)}, u32[]{:S(2)}) %collective-permute-start.5) | collective-permute-done | bytes 270368 | tf_op jit(solution)/shard_map/ppermute | solution.py:25
  64.3 1.4 collective-permute-start.15
  65.7 27.2 %collective-permute-done.14.refs_6_ = bf16[544,256]{1,0:T(8,128)(2,1)S(1)} collective-permute-done((bf16[544,256]{1,0:T(8,128)(2,1)}, bf16[544,256]{1,0:T(8,128)(2,1)S(1)}, u32[]{:S(2)}, u32[]{:S(2)}) %collective-permute-start.14) | collective-permute-done | bytes 278560 | tf_op jit(solution)/shard_map/ppermute | solution.py:25
  92.8 1.6 collective-permute-start.31
  95.0 1.5 collective-permute-start.20
  96.5 1.5 collective-permute-done.15.refs_7_
  97.9 1.1 collective-permute-start.21
  99.0 10.1 %collective-permute-done.31.refs_10_ = bf16[1024,256]{1,0:T(8,128)(2,1)S(1)} collective-permute-done((bf16[1024,256]{1,0:T(8,128)(2,1)S(1)}, bf16[1024,256]{1,0:T(8,128)(2,1)S(1)}, u32[]{:S(2)}, u32[]{:S(2)}) %collective-permute-start.31) | collective-permute-done | bytes 524320 | tf_op jit(solution)/shard_map/ppermute | solution.py:25
  110.0 7.7 %collective-permute-done.20.refs_13_ = bf16[1024,256]{1,0:T(8,128)(2,1)} collective-permute-done((bf16[1024,256]{1,0:T(8,128)(2,1)}, bf16[1024,256]{1,0:T(8,128)(2,1)}, u32[]{:S(2)}, u32[]{:S(2)}) %collective-permute-start.20) | collective-permute-done | bytes 524320 | tf_op jit(solution)/shard_map/ppermute | solution.py:25
  117.7 0.8 copy-done.29
  119.6 1.1 gather_fusion.1
  123.5 1.5 collective-permute-start.34
  125.7 10.8 %shard_map.190 = (bf16[512,256]{1,0:T(8,128)(2,1)}, bf16[512,256]{1,0:T(8,128)(2,1)}, bf16[512,256]{1,0:T(8,128)(2,1)}, bf16[512,256]{1,0:T(8,128)(2,1)}, bf16[1...) custom-call(s32[3]{0:T(128)} %pad_add_fusion.flags_ref, s32[2,256]{1,0:T(2,128)} %gather_fusion.1, ...), custom_call_target="tpu_custom_call" | custom-call | flops 3221225472 | bytes 10485760 | tf_op jit(solution)/shard_map/pallas_call | solution.py:446
  136.5 0.8 collective-permute-start.35
  137.3 1.4 collective-permute-start.25
  138.7 2.3 %collective-permute-done.34.refs_13_ = bf16[512,256]{1,0:T(8,128)(2,1)} collective-permute-done((bf16[512,256]{1,0:T(8,128)(2,1)S(1)}, bf16[512,256]{1,0:T(8,128)(2,1)}, u32[]{:S(2)}, u32[]{:S(2)}) %collective-permute-start.34) | collective-permute-done | bytes 262176 | tf_op jit(solution)/shard_map/ppermute | solution.py:25
  141.7 1.2 collective-permute-start.38
  142.8 2.6 %collective-permute-done.26 = bf16[16,1152]{1,0:T(8,128)(2,1)S(1)} collective-permute-done((bf16[16,1152]{1,0:T(8,128)(2,1)}, bf16[16,1152]{1,0:T(8,128)(2,1)S(1)}, u32[]{:S(2)}, u32[]{:S(2)}) %collective-permute-start.26) | collective-permute-done | bytes 36896 | tf_op jit(solution)/shard_map/ppermute | solution.py:482
  146.7 3.7 %collective-permute-start.28 = (bf16[32,1152]{1,0:T(8,128)(2,1)S(1)}, bf16[32,1152]{1,0:T(8,128)(2,1)}, u32[]{:S(2)}, u32[]{:S(2)}) collective-permute-start(bf16[32,1152]{1,0:T(8,128)(2,1)S(1)} %constant_dynamic-update-slice_fusion.refs_4_), channel_id=1, source_target_pairs={{0,2},{1,3},{2,0},{3,1},{4,6},{5,7},{6,4},{7,5},{8,10},{9,11},{10,... | collective-permute-start | bytes 221192 | tf_op jit(solution)/shard_map/ppermute | solution.py:25
  150.5 1.2 broadcast_add_fusion
  151.8 1.3 add.79.from_ref
  153.8 0.9 collective-permute-done.29.refs_7_
  154.9 7.4 %shard_map.192 = (bf16[256,256]{1,0:T(8,128)(2,1)}, bf16[256,256]{1,0:T(8,128)(2,1)}, bf16[256,256]{1,0:T(8,128)(2,1)}, bf16[256,256]{1,0:T(8,128)(2,1)}) custom-call(s32[3]{0:T(128)} %pad_add_fusion.flags_ref, s32[1]{0:T(128)S(6)} %copy.21.count_ref, s32[8]{0:T(128)} %add.79.from_ref, s32[8,256]{1,0:T(8,128)} %bitcast.27, ...), custom_call_target="tpu_custom_call" | custom-call | flops 1610612736 | bytes 8388608 | tf_op jit(solution)/shard_map/pallas_call | solution.py:504
  162.9 1.7 collective-permute-start.43
  164.6 1.6 collective-permute-start.40
  166.4 14.3 %collective-permute-done.40.refs_2_ = bf16[256,256]{1,0:T(8,128)(2,1)S(1)} collective-permute-done((bf16[256,256]{1,0:T(8,128)(2,1)}, bf16[256,256]{1,0:T(8,128)(2,1)S(1)}, u32[]{:S(2)}, u32[]{:S(2)}) %collective-permute-start.40) | collective-permute-done | bytes 131104 | tf_op jit(solution)/shard_map/ppermute | solution.py:25
  180.7 1.4 collective-permute-done.41.refs_3_
  182.8 1.9 %shard_map.193 = bf16[1024,256]{1,0:T(8,128)(2,1)} custom-call(s32[4]{0:T(128)} %iota_xor_fusion.1.order_ref, bf16[256,256]{1,0:T(8,128)(2,1)} %get-tuple-element.66.refs_0_, bf16[256,256]{1,0:T(8,128)(2,1)} %copy-done.13, bf16[256,256]{1,0:T(8,128)(2,1)} %copy-done.14, bf16[256,256]{1,0:T(8,128)(2,1)} %copy-done.15), custom_call_target="tpu_custom_call" | custom-call | tf_op jit(solution)/shard_map/pallas_call | solution.py:161
  185.6 2.2 %shard_map.194 = bf16[2048,256]{1,0:T(8,128)(2,1)} custom-call(s32[8]{0:T(128)} %reshape.131.order_ref, bf16[512,256]{1,0:T(8,128)(2,1)} %get-tuple-element.70.refs_0_, bf16[512,256]{1,0:T(8,128)(2,1)} %copy-done.6, bf16[512,256]{1,0:T(8,128)(2,1)} %copy-done.7, bf16[512,256]{1,0:T(8,128)(2,1)} %copy-done.8), custom_call_target="tpu_custom_call" | custom-call | tf_op jit(solution)/shard_map/pallas_call | solution.py:161
  (177 shorter events, 20.0 us)
Async XLA Ops:
  5.1 18.1 %collective-permute-start.10 = (bf16[256,256]{1,0:T(8,128)(2,1)}, bf16[256,256]{1,0:T(8,128)(2,1)S(1)}, u32[]{:S(2)}, u32[]{:S(2)}) collective-permute-start(bf16[256,256]{1,0:T(8,128)(2,1)} %get-tuple-element.51), channel_id=1, source_target_pairs={{0,20},{4,16},{8,28},{12,24},{16,4},{20,0},{24,12},{28,8},{1,21},{... | collective-permute-start | bytes 393224 | tf_op jit(solution)/shard_map/ppermute | solution.py:25
  10.1 13.1 %collective-permute-start.11 = (bf16[256,256]{1,0:T(8,128)(2,1)}, bf16[256,256]{1,0:T(8,128)(2,1)S(1)}, u32[]{:S(2)}, u32[]{:S(2)}) collective-permute-start(bf16[256,256]{1,0:T(8,128)(2,1)} %get-tuple-element.52), channel_id=1, source_target_pairs={{0,24},{4,28},{8,16},{12,20},{16,8},{20,12},{24,0},{28,4},{1,25},{... | collective-permute-start | bytes 393224 | tf_op jit(solution)/shard_map/ppermute | solution.py:25
  11.4 21.9 %collective-permute-start.12 = (bf16[256,256]{1,0:T(8,128)(2,1)}, bf16[256,256]{1,0:T(8,128)(2,1)S(1)}, u32[]{:S(2)}, u32[]{:S(2)}) collective-permute-start(bf16[256,256]{1,0:T(8,128)(2,1)} %get-tuple-element.53), channel_id=1, source_target_pairs={{0,28},{4,24},{8,20},{12,16},{16,12},{20,8},{24,4},{28,0},{1,29},{... | collective-permute-start | bytes 393224 | tf_op jit(solution)/shard_map/ppermute | solution.py:25
  13.9 29.0 %collective-permute-start.6 = (bf16[256,256]{1,0:T(8,128)(2,1)}, bf16[256,256]{1,0:T(8,128)(2,1)S(1)}, u32[]{:S(2)}, u32[]{:S(2)}) collective-permute-start(bf16[256,256]{1,0:T(8,128)(2,1)} %get-tuple-element.47), channel_id=1, source_target_pairs={{0,4},{4,0},{8,12},{12,8},{16,20},{20,16},{24,28},{28,24},{1,5},{5... | collective-permute-start | bytes 393224 | tf_op jit(solution)/shard_map/ppermute | solution.py:25
  15.4 28.0 %collective-permute-start.7 = (bf16[256,256]{1,0:T(8,128)(2,1)}, bf16[256,256]{1,0:T(8,128)(2,1)S(1)}, u32[]{:S(2)}, u32[]{:S(2)}) collective-permute-start(bf16[256,256]{1,0:T(8,128)(2,1)} %get-tuple-element.48), channel_id=1, source_target_pairs={{0,8},{4,12},{8,0},{12,4},{16,24},{20,28},{24,16},{28,20},{1,9},{5... | collective-permute-start | bytes 393224 | tf_op jit(solution)/shard_map/ppermute | solution.py:25
  23.2 21.8 %collective-permute-start.8 = (bf16[256,256]{1,0:T(8,128)(2,1)}, bf16[256,256]{1,0:T(8,128)(2,1)S(1)}, u32[]{:S(2)}, u32[]{:S(2)}) collective-permute-start(bf16[256,256]{1,0:T(8,128)(2,1)} %get-tuple-element.49), channel_id=1, source_target_pairs={{0,12},{4,8},{8,4},{12,0},{16,28},{20,24},{24,20},{28,16},{1,13},{... | collective-permute-start | bytes 393224 | tf_op jit(solution)/shard_map/ppermute | solution.py:25
  23.2 22.2 %collective-permute-start.9 = (bf16[256,256]{1,0:T(8,128)(2,1)}, bf16[256,256]{1,0:T(8,128)(2,1)S(1)}, u32[]{:S(2)}, u32[]{:S(2)}) collective-permute-start(bf16[256,256]{1,0:T(8,128)(2,1)} %get-tuple-element.50), channel_id=1, source_target_pairs={{0,16},{4,20},{8,24},{12,28},{16,0},{20,4},{24,8},{28,12},{1,17},{... | collective-permute-start | bytes 393224 | tf_op jit(solution)/shard_map/ppermute | solution.py:25
  33.3 90.2 %collective-permute-start.16 = (bf16[4096,256]{1,0:T(8,128)(2,1)}, bf16[4096,256]{1,0:T(8,128)(2,1)}, u32[]{:S(2)}, u32[]{:S(2)}) collective-permute-start(bf16[4096,256]{1,0:T(8,128)(2,1)} %get-tuple-element.58.refs_8_), channel_id=1, source_target_pairs={{0,1},{1,0},{2,3},{3,2},{4,5},{5,4},{6,7},{7,6},{8,9},{9,8},{10,11... | collective-permute-start | bytes 6291464 | tf_op jit(solution)/shard_map/ppermute | solution.py:25
  42.9 15.8 %collective-permute-start.3 = (bf16[528,256]{1,0:T(8,128)(2,1)}, bf16[528,256]{1,0:T(8,128)(2,1)}, u32[]{:S(2)}, u32[]{:S(2)}) collective-permute-start(bf16[528,256]{1,0:T(8,128)(2,1)} %get-tuple-element.43), channel_id=1, source_target_pairs={{0,1},{1,0},{2,3},{3,2},{4,5},{5,4},{6,7},{7,6},{8,9},{9,8},{10,11... | collective-permute-start | bytes 811016 | tf_op jit(solution)/shard_map/ppermute | solution.py:25
  43.4 16.8 %collective-permute-start.4 = (bf16[528,256]{1,0:T(8,128)(2,1)}, bf16[528,256]{1,0:T(8,128)(2,1)}, u32[]{:S(2)}, u32[]{:S(2)}) collective-permute-start(bf16[528,256]{1,0:T(8,128)(2,1)} %get-tuple-element.44), channel_id=1, source_target_pairs={{0,2},{1,3},{2,0},{3,1},{4,6},{5,7},{6,4},{7,5},{8,10},{9,11},{10,... | collective-permute-start | bytes 811016 | tf_op jit(solution)/shard_map/ppermute | solution.py:25
  44.9 13.7 %collective-permute-start.33 = (bf16[512,256]{1,0:T(8,128)(2,1)}, bf16[512,256]{1,0:T(8,128)(2,1)S(1)}, u32[]{:S(2)}, u32[]{:S(2)}) collective-permute-start(bf16[512,256]{1,0:T(8,128)(2,1)} %get-tuple-element.65), channel_id=1, source_target_pairs={{0,2},{1,3},{2,0},{3,1},{4,6},{5,7},{6,4},{7,5},{8,10},{9,11},{10,... | collective-permute-start | bytes 786440 | tf_op jit(solution)/shard_map/ppermute | solution.py:25
  45.5 1.6 collective-permute-start
  47.0 16.5 %collective-permute-start.5 = (bf16[528,256]{1,0:T(8,128)(2,1)}, bf16[528,256]{1,0:T(8,128)(2,1)}, u32[]{:S(2)}, u32[]{:S(2)}) collective-permute-start(bf16[528,256]{1,0:T(8,128)(2,1)} %get-tuple-element.45), channel_id=1, source_target_pairs={{0,3},{1,2},{2,1},{3,0},{4,7},{5,6},{6,5},{7,4},{8,11},{9,10},{10,... | collective-permute-start | bytes 811016 | tf_op jit(solution)/shard_map/ppermute | solution.py:25
  48.9 43.9 %copy-start.28 = (bf16[1024,256]{1,0:T(8,128)(2,1)S(1)}, bf16[1024,256]{1,0:T(8,128)(2,1)}, u32[]{:S(2)}) copy-start(bf16[1024,256]{1,0:T(8,128)(2,1)} %get-tuple-element.64) | copy-start | bytes 1572868
  48.9 60.4 %copy-start = (bf16[3072,256]{1,0:T(8,128)(2,1)S(1)}, bf16[3072,256]{1,0:T(8,128)(2,1)}, u32[]{:S(2)}) copy-start(bf16[3072,256]{1,0:T(8,128)(2,1)} %get-tuple-element.63.refs_8_) | copy-start | bytes 4718596
  58.6 96.0 %copy-start.4 = (bf16[512,256]{1,0:T(8,128)(2,1)}, bf16[512,256]{1,0:T(8,128)(2,1)S(1)}, u32[]{:S(2)}) copy-start(bf16[512,256]{1,0:T(8,128)(2,1)S(1)} %collective-permute-done.33.refs_12_) | copy-start | bytes 786436
  58.6 5.7 %collective-permute-start.13 = (bf16[544,256]{1,0:T(8,128)(2,1)}, bf16[544,256]{1,0:T(8,128)(2,1)S(1)}, u32[]{:S(2)}, u32[]{:S(2)}) collective-permute-start(bf16[544,256]{1,0:T(8,128)(2,1)} %get-tuple-element.55), channel_id=1, source_target_pairs={{0,1},{1,0},{2,3},{3,2},{4,5},{5,4},{6,7},{7,6},{8,9},{9,8},{10,11... | collective-permute-start | bytes 835592 | tf_op jit(solution)/shard_map/ppermute | solution.py:25
  58.6 35.8 %collective-permute-start.17 = (bf16[1024,256]{1,0:T(8,128)(2,1)S(1)}, bf16[1024,256]{1,0:T(8,128)(2,1)S(1)}, u32[]{:S(2)}, u32[]{:S(2)}) collective-permute-start(bf16[1024,256]{1,0:T(8,128)(2,1)S(1)} %copy-done.26), channel_id=1, source_target_pairs={{0,2},{1,3},{2,0},{3,1},{4,6},{5,7},{6,4},{7,5},{8,10},{9,11},{10,... | collective-permute-start | bytes 1572872 | tf_op jit(solution)/shard_map/ppermute | solution.py:25
  60.2 34.8 %collective-permute-start.19 = (bf16[1024,256]{1,0:T(8,128)(2,1)S(1)}, bf16[1024,256]{1,0:T(8,128)(2,1)}, u32[]{:S(2)}, u32[]{:S(2)}) collective-permute-start(bf16[1024,256]{1,0:T(8,128)(2,1)S(1)} %copy-done.25), channel_id=1, source_target_pairs={{0,2},{1,3},{2,0},{3,1},{4,6},{5,7},{6,4},{7,5},{8,10},{9,11},{10,... | collective-permute-start | bytes 1572872 | tf_op jit(solution)/shard_map/ppermute | solution.py:25
  63.5 29.3 %collective-permute-start.14 = (bf16[544,256]{1,0:T(8,128)(2,1)}, bf16[544,256]{1,0:T(8,128)(2,1)S(1)}, u32[]{:S(2)}, u32[]{:S(2)}) collective-permute-start(bf16[544,256]{1,0:T(8,128)(2,1)} %get-tuple-element.56), channel_id=1, source_target_pairs={{0,2},{1,3},{2,0},{3,1},{4,6},{5,7},{6,4},{7,5},{8,10},{9,11},{10,... | collective-permute-start | bytes 835592 | tf_op jit(solution)/shard_map/ppermute | solution.py:25
  64.3 33.7 %collective-permute-start.15 = (bf16[544,256]{1,0:T(8,128)(2,1)}, bf16[544,256]{1,0:T(8,128)(2,1)}, u32[]{:S(2)}, u32[]{:S(2)}) collective-permute-start(bf16[544,256]{1,0:T(8,128)(2,1)} %get-tuple-element.57), channel_id=1, source_target_pairs={{0,3},{1,2},{2,1},{3,0},{4,7},{5,6},{6,5},{7,4},{8,11},{9,10},{10,... | collective-permute-start | bytes 835592 | tf_op jit(solution)/shard_map/ppermute | solution.py:25
  92.8 16.3 %collective-permute-start.31 = (bf16[1024,256]{1,0:T(8,128)(2,1)S(1)}, bf16[1024,256]{1,0:T(8,128)(2,1)S(1)}, u32[]{:S(2)}, u32[]{:S(2)}) collective-permute-start(bf16[1024,256]{1,0:T(8,128)(2,1)S(1)} %copy-done.28), channel_id=1, source_target_pairs={{0,2},{1,3},{2,0},{3,1},{4,6},{5,7},{6,4},{7,5},{8,10},{9,11},{10,... | collective-permute-start | bytes 1572872 | tf_op jit(solution)/shard_map/ppermute | solution.py:25
  94.4 14.9 %collective-permute-start.18 = (bf16[1024,256]{1,0:T(8,128)(2,1)S(1)}, bf16[1024,256]{1,0:T(8,128)(2,1)}, u32[]{:S(2)}, u32[]{:S(2)}) collective-permute-start(bf16[1024,256]{1,0:T(8,128)(2,1)S(1)} %collective-permute-done.17.refs_10_), channel_id=1, source_target_pairs={{0,4},{4,0},{8,12},{12,8},{16,20},{20,16},{24,28},{28,24},{1,5},{5... | collective-permute-start | bytes 1572872 | tf_op jit(solution)/shard_map/ppermute | solution.py:25
  95.0 22.7 %collective-permute-start.20 = (bf16[1024,256]{1,0:T(8,128)(2,1)}, bf16[1024,256]{1,0:T(8,128)(2,1)}, u32[]{:S(2)}, u32[]{:S(2)}) collective-permute-start(bf16[1024,256]{1,0:T(8,128)(2,1)} %collective-permute-done.19.refs_12_), channel_id=1, source_target_pairs={{0,4},{4,0},{8,12},{12,8},{16,20},{20,16},{24,28},{28,24},{1,5},{5... | collective-permute-start | bytes 1572872 | tf_op jit(solution)/shard_map/ppermute | solution.py:25
  97.9 19.7 %collective-permute-start.21 = (bf16[1024,256]{1,0:T(8,128)(2,1)S(1)}, bf16[1024,256]{1,0:T(8,128)(2,1)S(1)}, u32[]{:S(2)}, u32[]{:S(2)}) collective-permute-start(bf16[1024,256]{1,0:T(8,128)(2,1)S(1)} %collective-permute-done.17.refs_10_), channel_id=1, source_target_pairs={{0,1},{1,0},{2,3},{3,2},{4,5},{5,4},{6,7},{7,6},{8,9},{9,8},{10,11... | collective-permute-start | bytes 1572872 | tf_op jit(solution)/shard_map/ppermute | solution.py:25
  109.2 12.1 %collective-permute-start.23 = (bf16[1024,256]{1,0:T(8,128)(2,1)}, bf16[1024,256]{1,0:T(8,128)(2,1)}, u32[]{:S(2)}, u32[]{:S(2)}) collective-permute-start(bf16[1024,256]{1,0:T(8,128)(2,1)} %collective-permute-done.19.refs_12_), channel_id=1, source_target_pairs={{0,1},{1,0},{2,3},{3,2},{4,5},{5,4},{6,7},{7,6},{8,9},{9,8},{10,11... | collective-permute-start | bytes 1572872 | tf_op jit(solution)/shard_map/ppermute | solution.py:25
  109.3 44.4 %collective-permute-start.30 = (bf16[3072,256]{1,0:T(8,128)(2,1)S(1)}, bf16[3072,256]{1,0:T(8,128)(2,1)S(1)}, u32[]{:S(2)}, u32[]{:S(2)}) collective-permute-start(bf16[3072,256]{1,0:T(8,128)(2,1)S(1)} %copy-done), channel_id=1, source_target_pairs={{0,1},{1,0},{2,3},{3,2},{4,5},{5,4},{6,7},{7,6},{8,9},{9,8},{10,11... | collective-permute-start | bytes 4718600 | tf_op jit(solution)/shard_map/ppermute | solution.py:25
  117.7 4.7 %collective-permute-start.22 = (bf16[1024,256]{1,0:T(8,128)(2,1)}, bf16[1024,256]{1,0:T(8,128)(2,1)}, u32[]{:S(2)}, u32[]{:S(2)}) collective-permute-start(bf16[1024,256]{1,0:T(8,128)(2,1)} %collective-permute-done.18.refs_11_), channel_id=1, source_target_pairs={{0,1},{1,0},{2,3},{3,2},{4,5},{5,4},{6,7},{7,6},{8,9},{9,8},{10,11... | collective-permute-start | bytes 1572872 | tf_op jit(solution)/shard_map/ppermute | solution.py:25
  118.5 4.4 %collective-permute-start.24 = (bf16[1024,256]{1,0:T(8,128)(2,1)}, bf16[1024,256]{1,0:T(8,128)(2,1)}, u32[]{:S(2)}, u32[]{:S(2)}) collective-permute-start(bf16[1024,256]{1,0:T(8,128)(2,1)} %collective-permute-done.20.refs_13_), channel_id=1, source_target_pairs={{0,1},{1,0},{2,3},{3,2},{4,5},{5,4},{6,7},{7,6},{8,9},{9,8},{10,11... | collective-permute-start | bytes 1572872 | tf_op jit(solution)/shard_map/ppermute | solution.py:25
  121.3 20.4 %collective-permute-start.32 = (bf16[1024,256]{1,0:T(8,128)(2,1)}, bf16[1024,256]{1,0:T(8,128)(2,1)}, u32[]{:S(2)}, u32[]{:S(2)}) collective-permute-start(bf16[1024,256]{1,0:T(8,128)(2,1)} %copy-done.3), channel_id=1, source_target_pairs={{0,4},{4,0},{8,12},{12,8},{16,20},{20,16},{24,28},{28,24},{1,5},{5... | collective-permute-start | bytes 1572872 | tf_op jit(solution)/shard_map/ppermute | solution.py:25
  122.4 14.1 %collective-permute-start.1 = (bf16[272,256]{1,0:T(8,128)(2,1)}, bf16[272,256]{1,0:T(8,128)(2,1)S(1)}, u32[]{:S(2)}, u32[]{:S(2)}) collective-permute-start(bf16[272,256]{1,0:T(8,128)(2,1)} %get-tuple-element.40), channel_id=1, source_target_pairs={{0,2},{1,3},{2,0},{3,1},{4,6},{5,7},{6,4},{7,5},{8,10},{9,11},{10,... | collective-permute-start | bytes 417800 | tf_op jit(solution)/shard_map/ppermute | solution.py:25
  122.9 14.4 %collective-permute-start.2 = (bf16[272,256]{1,0:T(8,128)(2,1)}, bf16[272,256]{1,0:T(8,128)(2,1)}, u32[]{:S(2)}, u32[]{:S(2)}) collective-permute-start(bf16[272,256]{1,0:T(8,128)(2,1)} %get-tuple-element.41), channel_id=1, source_target_pairs={{0,3},{1,2},{2,1},{3,0},{4,7},{5,6},{6,5},{7,4},{8,11},{9,10},{10,... | collective-permute-start | bytes 417800 | tf_op jit(solution)/shard_map/ppermute | solution.py:25
  123.5 17.5 %collective-permute-start.34 = (bf16[512,256]{1,0:T(8,128)(2,1)S(1)}, bf16[512,256]{1,0:T(8,128)(2,1)}, u32[]{:S(2)}, u32[]{:S(2)}) collective-permute-start(bf16[512,256]{1,0:T(8,128)(2,1)S(1)} %collective-permute-done.33.refs_12_), channel_id=1, source_target_pairs={{0,4},{4,0},{8,12},{12,8},{16,20},{20,16},{24,28},{28,24},{1,5},{5... | collective-permute-start | bytes 786440 | tf_op jit(solution)/shard_map/ppermute | solution.py:25
  136.5 13.9 %collective-permute-start.35 = (bf16[1024,256]{1,0:T(8,128)(2,1)}, bf16[1024,256]{1,0:T(8,128)(2,1)}, u32[]{:S(2)}, u32[]{:S(2)}) collective-permute-start(bf16[1024,256]{1,0:T(8,128)(2,1)} %copy-done.3), channel_id=1, source_target_pairs={{0,1},{1,0},{2,3},{3,2},{4,5},{5,4},{6,7},{7,6},{8,9},{9,8},{10,11... | collective-permute-start | bytes 1572872 | tf_op jit(solution)/shard_map/ppermute | solution.py:25
  137.3 4.3 %collective-permute-start.25 = (bf16[16,1152]{1,0:T(8,128)(2,1)}, bf16[16,1152]{1,0:T(8,128)(2,1)S(1)}, u32[]{:S(2)}, u32[]{:S(2)}) collective-permute-start(bf16[16,1152]{1,0:T(8,128)(2,1)} %get-tuple-element.61), channel_id=1, source_target_pairs={{0,0},{1,8},{2,16},{3,24},{4,4},{5,12},{6,20},{7,28},{8,1},{9,9},{... | collective-permute-start | bytes 110600 | tf_op jit(solution)/shard_map/ppermute | solution.py:482
  141.0 4.4 %collective-permute-start.26 = (bf16[16,1152]{1,0:T(8,128)(2,1)}, bf16[16,1152]{1,0:T(8,128)(2,1)S(1)}, u32[]{:S(2)}, u32[]{:S(2)}) collective-permute-start(bf16[16,1152]{1,0:T(8,128)(2,1)} %get-tuple-element.62), channel_id=1, source_target_pairs={{0,4},{1,12},{2,20},{3,28},{4,0},{5,8},{6,16},{7,24},{8,5},{9,13},... | collective-permute-start | bytes 110600 | tf_op jit(solution)/shard_map/ppermute | solution.py:482
  141.7 3.8 %collective-permute-start.37 = (bf16[512,256]{1,0:T(8,128)(2,1)S(1)}, bf16[512,256]{1,0:T(8,128)(2,1)S(1)}, u32[]{:S(2)}, u32[]{:S(2)}) collective-permute-start(bf16[512,256]{1,0:T(8,128)(2,1)S(1)} %collective-permute-done.33.refs_12_), channel_id=1, source_target_pairs={{0,1},{1,0},{2,3},{3,2},{4,5},{5,4},{6,7},{7,6},{8,9},{9,8},{10,11... | collective-permute-start | bytes 786440 | tf_op jit(solution)/shard_map/ppermute | solution.py:25
  141.7 5.0 %collective-permute-start.38 = (bf16[512,256]{1,0:T(8,128)(2,1)}, bf16[512,256]{1,0:T(8,128)(2,1)}, u32[]{:S(2)}, u32[]{:S(2)}) collective-permute-start(bf16[512,256]{1,0:T(8,128)(2,1)} %collective-permute-done.34.refs_13_), channel_id=1, source_target_pairs={{0,1},{1,0},{2,3},{3,2},{4,5},{5,4},{6,7},{7,6},{8,9},{9,8},{10,11... | collective-permute-start | bytes 786440 | tf_op jit(solution)/shard_map/ppermute | solution.py:25
  145.4 8.3 %collective-permute-start.36 = (bf16[1024,256]{1,0:T(8,128)(2,1)}, bf16[1024,256]{1,0:T(8,128)(2,1)}, u32[]{:S(2)}, u32[]{:S(2)}) collective-permute-start(bf16[1024,256]{1,0:T(8,128)(2,1)} %collective-permute-done.32.refs_11_), channel_id=1, source_target_pairs={{0,1},{1,0},{2,3},{3,2},{4,5},{5,4},{6,7},{7,6},{8,9},{9,8},{10,11... | collective-permute-start | bytes 1572872 | tf_op jit(solution)/shard_map/ppermute | solution.py:25
  146.2 7.5 %collective-permute-start.27 = (bf16[32,1152]{1,0:T(8,128)(2,1)S(1)}, bf16[32,1152]{1,0:T(8,128)(2,1)S(1)}, u32[]{:S(2)}, u32[]{:S(2)}) collective-permute-start(bf16[32,1152]{1,0:T(8,128)(2,1)S(1)} %constant_dynamic-update-slice_fusion.refs_4_), channel_id=1, source_target_pairs={{0,1},{1,0},{2,3},{3,2},{4,5},{5,4},{6,7},{7,6},{8,9},{9,8},{10,11... | collective-permute-start | bytes 221192 | tf_op jit(solution)/shard_map/ppermute | solution.py:25
  146.7 7.0 %collective-permute-start.28 = (bf16[32,1152]{1,0:T(8,128)(2,1)S(1)}, bf16[32,1152]{1,0:T(8,128)(2,1)}, u32[]{:S(2)}, u32[]{:S(2)}) collective-permute-start(bf16[32,1152]{1,0:T(8,128)(2,1)S(1)} %constant_dynamic-update-slice_fusion.refs_4_), channel_id=1, source_target_pairs={{0,2},{1,3},{2,0},{3,1},{4,6},{5,7},{6,4},{7,5},{8,10},{9,11},{10,... | collective-permute-start | bytes 221192 | tf_op jit(solution)/shard_map/ppermute | solution.py:25
  150.4 4.3 %collective-permute-start.29 = (bf16[32,1152]{1,0:T(8,128)(2,1)S(1)}, bf16[32,1152]{1,0:T(8,128)(2,1)}, u32[]{:S(2)}, u32[]{:S(2)}) collective-permute-start(bf16[32,1152]{1,0:T(8,128)(2,1)S(1)} %constant_dynamic-update-slice_fusion.refs_4_), channel_id=1, source_target_pairs={{0,3},{1,2},{2,1},{3,0},{4,7},{5,6},{6,5},{7,4},{8,11},{9,10},{10,... | collective-permute-start | bytes 221192 | tf_op jit(solution)/shard_map/ppermute | solution.py:25
  162.3 3.9 %collective-permute-start.39 = (bf16[256,256]{1,0:T(8,128)(2,1)}, bf16[256,256]{1,0:T(8,128)(2,1)S(1)}, u32[]{:S(2)}, u32[]{:S(2)}) collective-permute-start(bf16[256,256]{1,0:T(8,128)(2,1)} %get-tuple-element.67), channel_id=1, source_target_pairs={{0,1},{1,0},{2,3},{3,2},{4,5},{5,4},{6,7},{7,6},{8,9},{9,8},{10,11... | collective-permute-start | bytes 393224 | tf_op jit(solution)/shard_map/ppermute | solution.py:25
  162.4 22.3 %collective-permute-start.42 = (bf16[512,256]{1,0:T(8,128)(2,1)}, bf16[512,256]{1,0:T(8,128)(2,1)S(1)}, u32[]{:S(2)}, u32[]{:S(2)}) collective-permute-start(bf16[512,256]{1,0:T(8,128)(2,1)} %get-tuple-element.71), channel_id=1, source_target_pairs={{0,1},{1,0},{2,3},{3,2},{4,5},{5,4},{6,7},{7,6},{8,9},{9,8},{10,11... | collective-permute-start | bytes 786440 | tf_op jit(solution)/shard_map/ppermute | solution.py:25
  162.9 21.8 %collective-permute-start.43 = (bf16[512,256]{1,0:T(8,128)(2,1)}, bf16[512,256]{1,0:T(8,128)(2,1)S(1)}, u32[]{:S(2)}, u32[]{:S(2)}) collective-permute-start(bf16[512,256]{1,0:T(8,128)(2,1)} %get-tuple-element.72), channel_id=1, source_target_pairs={{0,2},{1,3},{2,0},{3,1},{4,6},{5,7},{6,4},{7,5},{8,10},{9,11},{10,... | collective-permute-start | bytes 786440 | tf_op jit(solution)/shard_map/ppermute | solution.py:25
  164.6 20.2 %collective-permute-start.44 = (bf16[512,256]{1,0:T(8,128)(2,1)S(1)}, bf16[512,256]{1,0:T(8,128)(2,1)S(1)}, u32[]{:S(2)}, u32[]{:S(2)}) collective-permute-start(bf16[512,256]{1,0:T(8,128)(2,1)S(1)} %copy-done.32), channel_id=1, source_target_pairs={{0,3},{1,2},{2,1},{3,0},{4,7},{5,6},{6,5},{7,4},{8,11},{9,10},{10,... | collective-permute-start | bytes 786440 | tf_op jit(solution)/shard_map/ppermute | solution.py:25
  164.6 16.1 %collective-permute-start.40 = (bf16[256,256]{1,0:T(8,128)(2,1)}, bf16[256,256]{1,0:T(8,128)(2,1)S(1)}, u32[]{:S(2)}, u32[]{:S(2)}) collective-permute-start(bf16[256,256]{1,0:T(8,128)(2,1)} %get-tuple-element.68), channel_id=1, source_target_pairs={{0,2},{1,3},{2,0},{3,1},{4,6},{5,7},{6,4},{7,5},{8,10},{9,11},{10,... | collective-permute-start | bytes 393224 | tf_op jit(solution)/shard_map/ppermute | solution.py:25
  166.2 15.9 %collective-permute-start.41 = (bf16[256,256]{1,0:T(8,128)(2,1)}, bf16[256,256]{1,0:T(8,128)(2,1)S(1)}, u32[]{:S(2)}, u32[]{:S(2)}) collective-permute-start(bf16[256,256]{1,0:T(8,128)(2,1)} %get-tuple-element.69), channel_id=1, source_target_pairs={{0,3},{1,2},{2,1},{3,0},{4,7},{5,6},{6,5},{7,4},{8,11},{9,10},{10,... | collective-permute-start | bytes 393224 | tf_op jit(solution)/shard_map/ppermute | solution.py:25
  (37 other events, 387.7 us)

commit v2 on v1

v2 whole, which is shorter than its diff:
```python
import functools

import jax
import jax.numpy as jnp
from jax import lax
from jax.experimental import pallas as pl
from jax.experimental.pallas import tpu as pltpu
from jax.sharding import PartitionSpec as P

RT = 16
EPS = 1e-05
LANES = 128
TAIL = 16
QUARTERS = 4


BF = jnp.bfloat16
F32 = jnp.float32
VMEM = pl.BlockSpec(memory_space=pltpu.VMEM)
SMEM = pl.BlockSpec(memory_space=pltpu.SMEM)
ANY = pl.BlockSpec(memory_space=pl.ANY)


def swap(value, axis, mask):
    size = lax.axis_size(axis)
    return lax.ppermute(value, axis, [(i, i ^ mask) for i in range(size)])


def grant(mib):
    return pltpu.CompilerParams(vmem_limit_bytes=mib * 2**20)


def column(row):
    wide = jnp.broadcast_to(row.astype(F32), (LANES, row.shape[1]))
    return jnp.transpose(wide).astype(jnp.int32)


def hot_lanes(index, start, count):
    parts = []
    for at in range(0, count, LANES):
        width = min(LANES, count - at)
        lane = lax.broadcasted_iota(jnp.int32, (index.shape[0], width), 1) + (start + at)
        parts.append(jnp.where(index[:, :width] == lane, 1.0, 0.0).astype(BF))
    return parts[0] if len(parts) == 1 else jnp.concatenate(parts, axis=1)


def gather_rows(index, tables):
    total = None
    start = 0
    for table in tables:
        hot = hot_lanes(index, start, table.shape[0])
        part = jnp.dot(hot, table[...], preferred_element_type=F32)
        total = part if total is None else total + part
        start += table.shape[0]
    return total.astype(BF)


def halo_kernel(by_swap, index_ref, table_ref, *outs):
    patch = lax.axis_index("patch")
    for g, out in enumerate(outs):
        row = index_ref[pl.ds(patch ^ g if by_swap else g, 1), :]
        out[...] = gather_rows(column(row), [table_ref])


def halo_rows(by_swap, index, table):
    groups, rows = index.shape
    depth, width = table.shape
    return pl.pallas_call(
        functools.partial(halo_kernel, by_swap),
        in_specs=[VMEM] * 2,
        out_specs=[VMEM] * groups,
        out_shape=[jax.ShapeDtypeStruct((rows, width), BF)] * groups,
        cost_estimate=pl.CostEstimate(
            flops=2 * groups * rows * depth * width, bytes_accessed=4 * rows * width, transcendentals=0
        ),
    )(index, table)


def block_of(owner_ref, spot, direct):
    if not direct:
        return spot
    found = 0
    for b in range(owner_ref.shape[0]):
        found = found + jnp.where(owner_ref[b] == spot, b, 0)
    return found


def sender_kernel(by_swap, direct, pairs, halo, owner_ref, sender_ref, receiver_ref, *refs):
    tables, refs = refs[:-(pairs + 2)], refs[-(pairs + 2) :]
    outs, segment_ref, ids_ref, changes = refs[:pairs], refs[pairs], refs[pairs + 1], None
    patch = lax.axis_index("patch")
    me = lax.axis_index("pair")
    blocks, tile = sender_ref.shape
    mine = blocks // pairs
    receiver = receiver_ref[...]
    lane = lax.broadcasted_iota(jnp.int32, (blocks, tile), 1)
    changes = (receiver != pltpu.roll(receiver, 1, axis=1)) | (lane == 0)
    upper = lax.broadcasted_iota(jnp.int32, (tile, tile), 0) <= lax.broadcasted_iota(jnp.int32, (tile, tile), 1)
    count = jnp.dot(
        jnp.where(changes, 1.0, 0.0).astype(BF), jnp.where(upper, 1.0, 0.0).astype(BF), preferred_element_type=F32
    )
    segments = jnp.where(receiver >= 0, count.astype(jnp.int32) - 1, RT)
    segment_ref[...] = segments
    for k in range(pairs):
        index = []
        extra = []
        for i in range(mine):
            block = block_of(owner_ref, (me ^ k) * mine + i, direct)
            slot = jnp.maximum(sender_ref[pl.ds(block, 1), :], 0)
            index.append(column(slot ^ (patch * halo) if by_swap else slot))
            segment = segment_ref[pl.ds(block, 1), :]
            names = receiver_ref[pl.ds(block, 1), :].astype(F32)
            member = segment == lax.broadcasted_iota(jnp.int32, (RT, tile), 0)
            ids = jnp.max(jnp.where(member, names, -1.0), axis=1, keepdims=True)
            if k == 0:
                ids_ref[i * RT : (i + 1) * RT, :] = jnp.broadcast_to(ids, (RT, LANES)).astype(BF)
            owner = owner_ref[block]
            base = (owner ^ patch if by_swap else owner) * halo
            at = jnp.maximum(ids, 0.0).astype(jnp.int32) + base
            extra.append(jnp.broadcast_to(at, (RT, LANES)))
        outs[k][...] = gather_rows(jnp.concatenate(index + extra, axis=0), tables)


def sender_rows(by_swap, direct, pairs, halo, owner, sender, receiver, tables):
    blocks, tile = sender.shape
    width = tables[0].shape[1]
    mine = blocks // pairs
    rows = mine * (tile + RT)
    results = pl.pallas_call(
        functools.partial(sender_kernel, by_swap, direct, pairs, halo),
        compiler_params=grant(16),
        in_specs=[SMEM] + [VMEM] * (2 + len(tables)),
        out_specs=[VMEM] * (pairs + 2),
        out_shape=[jax.ShapeDtypeStruct((rows, width), BF)] * pairs
        + [
            jax.ShapeDtypeStruct((blocks, tile), jnp.int32),
            jax.ShapeDtypeStruct((mine * RT, LANES), BF),
        ],
        cost_estimate=pl.CostEstimate(
            flops=2 * pairs * rows * 2048 * width, bytes_accessed=4 * pairs * rows * width, transcendentals=0
        ),
    )(owner, sender, receiver, *tables)
    return results[:pairs], results[pairs], results[pairs + 1]


def split_kernel(size, per, direct, owner_ref, in_ref, bias_ref, gain_ref, shift_ref, *outs):
    value = jnp.concatenate([bias_ref[...], gain_ref[...], shift_ref[...]], axis=0)
    high = value.astype(BF).astype(F32)
    middle = (value - high).astype(BF).astype(F32)
    low = value - high - middle
    parts = [high, middle, low]
    parts.append(jnp.zeros((TAIL - 3 * value.shape[0], value.shape[1]), F32))
    tail = jnp.concatenate(parts, axis=0).astype(BF)
    me = lax.axis_index("pair")
    for k, out in enumerate(outs):
        for i in range(per):
            at = pl.multiple_of(block_of(owner_ref, (me ^ k) * per + i, direct) * size, size)
            out[i * size : (i + 1) * size, :] = in_ref[pl.ds(at, size), :]
        out[per * size :, :] = tail


def unpack_vectors(tail, count):
    wide = tail.astype(F32)
    return wide[:count] + wide[count : 2 * count] + wide[2 * count : 3 * count]


def split(owner, size, per, direct, parts, value, *vectors):
    return pl.pallas_call(
        functools.partial(split_kernel, size, per, direct),
        compiler_params=grant(12),
        in_specs=[SMEM] + [VMEM] * 4,
        out_specs=[VMEM] * parts,
        out_shape=[jax.ShapeDtypeStruct((size * per + TAIL, value.shape[1]), BF)] * parts,
    )(owner, value, *[v.reshape(1, -1) for v in vectors])


def join_kernel(size, per, direct, owner_ref, *refs):
    out = refs[-1]
    me = lax.axis_index("pair")
    for k, part in enumerate(refs[:-1]):
        for i in range(per):
            at = pl.multiple_of(block_of(owner_ref, (me ^ k) * per + i, direct) * size, size)
            out[pl.ds(at, size), :] = part[i * size : (i + 1) * size, :]


def join(owner, size, per, direct, values):
    return pl.pallas_call(
        functools.partial(join_kernel, size, per, direct),
        compiler_params=grant(12),
        in_specs=[SMEM] + [VMEM] * len(values),
        out_specs=VMEM,
        out_shape=jax.ShapeDtypeStruct((size * per * len(values), values[0].shape[1]), BF),
    )(owner, *values)


def part_rows(source, rows, put):
    step = 2 * LANES
    for side in range(2):
        lane = lax.broadcasted_iota(jnp.int32, (LANES, step), 1)
        row = lax.broadcasted_iota(jnp.int32, (LANES, step), 0)
        hot = jnp.where(lane == 2 * row + side, 1.0, 0.0).astype(BF)
        for n in range(rows // step):
            part = jnp.dot(hot, source[n * step : (n + 1) * step, :], preferred_element_type=F32)
            put(side, n * LANES, part.astype(BF))


def parted_kernel(ends_ref, out_ref):
    half = ends_ref.shape[0] // 2

    def put(side, at, value):
        out_ref[side * half + at : side * half + at + LANES, :] = value

    part_rows(ends_ref, ends_ref.shape[0], put)


def pieces_kernel(unit, in_ref, ends_ref, out_ref, node_ref, last_ref, e_piece, n_piece, ends, sems):
    a = lax.axis_index("patch") % QUARTERS
    full = node_ref.shape[0] // 2
    at = pl.multiple_of(a * unit, unit)
    below = pl.multiple_of(full + a * unit, unit)
    copies = [
        (ends_ref.at[pl.ds(pl.multiple_of(a * 2 * unit, 2 * unit), 2 * unit)], ends),
        (in_ref.at[pl.ds(at, unit)], e_piece.at[pl.ds(0, unit)]),
        (out_ref.at[:, pl.ds(at, unit)], e_piece.at[pl.ds(3 * unit, unit)]),
        (node_ref.at[pl.ds(at, unit)], n_piece.at[pl.ds(0, unit)]),
        (node_ref.at[pl.ds(below, unit)], n_piece.at[pl.ds(unit, unit)]),
        (last_ref.at[:, pl.ds(at, unit)], n_piece.at[pl.ds(2 * unit, unit)]),
    ]
    copies = [pltpu.make_async_copy(src, dst, sems.at[n]) for n, (src, dst) in enumerate(copies)]
    for copy in copies:
        copy.start()
    copies[0].wait()

    def put(side, row, value):
        base = (1 + side) * unit + row
        e_piece[base : base + LANES, :] = value

    part_rows(ends, 2 * unit, put)
    for copy in copies[1:]:
        copy.wait()


def silu(value):
    return value / (1.0 + jnp.exp(-value))


def finish(mixed, old, gain, shift, live):
    width = mixed.shape[1]
    mean = jnp.sum(mixed, axis=1, keepdims=True) / width
    square = jnp.sum(mixed * mixed, axis=1, keepdims=True) / width
    norm = (mixed - mean) * lax.rsqrt(square - mean * mean + EPS) * gain + shift
    return jnp.where(live, old + norm, old).astype(BF)


def far_spot(r, unit):
    quarter = (lax.axis_index("patch") % QUARTERS) ^ r
    return pl.ds(pl.multiple_of(quarter * unit, unit), unit)


def edge_kernel(pairs, groups, direct, owner_ref, segrow_ref, ids_ref, *refs):
    e_refs, refs = refs[:pairs], refs[pairs:]
    s_refs, refs = refs[:pairs], refs[pairs:]
    whole, far, refs = (refs[:3], refs[3:6]), (refs[6:10], refs[10:14]), refs[14:]
    outs, refs = refs[:pairs], refs[pairs:]
    sum_refs, refs = refs[:groups], refs[groups:]
    e_all, s_all, r_all, hidden, mixed_all, new_all, wide = refs
    me = lax.axis_index("pair")
    turn = lax.axis_index("patch") % 2 if direct else 0
    rows, full = new_all.shape
    local = full // pairs
    tile = rows // groups
    bias = []
    for k in range(pairs):
        at = pl.multiple_of((me ^ k) * local, local)
        s_all[:, pl.ds(at, local)] = s_refs[k][:rows, :]
        e_all[:, pl.ds(at, local)] = e_refs[k][:rows, :]
        r_all[:, pl.ds(at, local)] = s_refs[k][rows:, :]
        vectors = unpack_vectors(e_refs[k][rows:, :], 3)
        bias.append(vectors[:1])
        wide[:1, pl.ds(at, local)] = vectors[1:2]
        wide[1:2, pl.ds(at, local)] = vectors[2:3]
    segments, hots = [], []
    for g in range(groups):
        block = block_of(owner_ref, me * groups + g, direct)
        segment = column(segrow_ref[pl.ds(block, 1), :])
        segments.append(segment)
        hots.append(hot_lanes(segment, 0, RT))
    for k in range(pairs):
        if k < 2:
            w_edge, w_ends, _ = whole[k]
            receivers = jnp.dot(r_all[...], w_ends[full:, :], preferred_element_type=F32)
        else:
            receivers = None
            for r, piece in enumerate(far[k - 2]):
                part = r_all[:, far_spot(r, local)]
                part = jnp.dot(part, piece[2 * local : 3 * local, :], preferred_element_type=F32)
                receivers = part if receivers is None else receivers + part
        receivers = receivers.astype(BF)
        for g in range(groups):
            at = slice(g * tile, (g + 1) * tile)
            pre = jnp.dot(hots[g], receivers[g * RT : (g + 1) * RT], preferred_element_type=F32)
            if k < 2:
                pre += jnp.dot(e_all[at, :], w_edge[...], preferred_element_type=F32)
                pre += jnp.dot(s_all[at, :], w_ends[:full, :], preferred_element_type=F32)
            else:
                for r, piece in enumerate(far[k - 2]):
                    spot = far_spot(r, local)
                    pre += jnp.dot(e_all[at, spot], piece[:local, :], preferred_element_type=F32)
                    pre += jnp.dot(s_all[at, spot], piece[local : 2 * local, :], preferred_element_type=F32)
            hidden[at, k * local : (k + 1) * local] = silu(pre + bias[k]).astype(BF)
    for g in range(groups):
        at = slice(g * tile, (g + 1) * tile)
        first = hidden[at, :local], hidden[at, local : 2 * local]
        last = hidden[at, 2 * local : 3 * local], hidden[at, 3 * local :]
        for r in range(QUARTERS):
            spot = far_spot(r, local)
            total = None
            for near, (_, _, w_out), behind, pieces in zip(first, whole, last, far):
                part = jnp.dot(near, w_out[:, spot], preferred_element_type=F32)
                part += jnp.dot(behind, pieces[r][3 * local :, :], preferred_element_type=F32)
                total = part if total is None else total + part
            mixed_all[at, spot] = total
        live = segments[g][:, :1] < RT
        old = e_all[at, :].astype(F32)
        new_all[at, :] = finish(mixed_all[at, :], old, wide[:1, :], wide[1:2, :], live)
    for t in range(groups):
        g = t ^ turn
        segrow = segrow_ref[pl.ds(block_of(owner_ref, me * groups + g, direct), 1), :]
        member = segrow == lax.broadcasted_iota(jnp.int32, (RT, tile), 0)
        member = jnp.where(member, 1.0, 0.0).astype(BF)
        new = new_all[pl.ds(pl.multiple_of(g * tile, tile), tile), :]
        total = jnp.dot(member, new, preferred_element_type=F32)
        sum_refs[t][:, :full] = total.astype(BF)
        sum_refs[t][:, full:] = ids_ref[pl.ds(pl.multiple_of(g * RT, RT), RT), :]
    for k in range(pairs):
        at = pl.ds(pl.multiple_of((me ^ k) * local, local), local)
        outs[k][...] = new_all[:, at]


def node_kernel(pairs, sources, direct, count_ref, list_ref, *refs):
    n_refs, refs = refs[:pairs], refs[pairs:]
    r_refs, refs = refs[:sources], refs[sources:]
    whole, far, refs = (refs[:2], refs[2:4]), (refs[4:8], refs[8:12]), refs[12:]
    outs, refs = refs[:pairs], refs[pairs:]
    n_all, sums, nodes_of, aggregated, hidden, mixed_all, wide = refs
    me = lax.axis_index("pair")
    odd = lax.axis_index("patch") % 2
    rows, full = n_all.shape
    local = full // pairs
    first = me * rows
    bias = []
    for k in range(pairs):
        at = pl.ds(pl.multiple_of((me ^ k) * local, local), local)
        n_all[:, at] = n_refs[k][:rows, :]
        vectors = unpack_vectors(n_refs[k][rows:, :], 3)
        bias.append(vectors[:1])
        wide[:1, at] = vectors[1:2]
        wide[1:2, at] = vectors[2:3]
    halo = list_ref.shape[1]
    start = 0
    for r in r_refs:
        depth = r.shape[0]
        sums[start : start + depth, :] = r[:, :full]
        for at in range(0, depth, RT):
            ids = r[at : at + RT, full:].astype(F32)[:, :1].astype(jnp.int32)
            turn = (start + at) // RT
            if direct:
                turn = (me ^ (turn // 2)) * 2 + (odd ^ (turn % 2))
            names = list_ref[pl.ds(turn, 1), :]
            found = ids == lax.broadcasted_iota(jnp.int32, (RT, halo), 1)
            node = jnp.sum(jnp.where(found, names.astype(F32), 0.0), axis=1, keepdims=True)
            node = jnp.where(ids >= 0, node, -1.0)
            nodes_of[start + at : start + at + RT, :] = jnp.broadcast_to(node, (RT, LANES))
        start += depth
    total = None
    for at in range(0, start, LANES):
        row = jnp.transpose(nodes_of[at : at + LANES, :])[:1].astype(jnp.int32)
        hot = row == lax.broadcasted_iota(jnp.int32, (rows, LANES), 0) + first
        hot = jnp.where(hot, 1.0, 0.0).astype(BF)
        part = jnp.dot(hot, sums[at : at + LANES, :], preferred_element_type=F32)
        total = part if total is None else total + part
    aggregated[...] = total.astype(BF)
    for k in range(pairs):
        if k < 2:
            w_in = whole[k][0]
            pre = jnp.dot(n_all[...], w_in[:full, :], preferred_element_type=F32)
            pre += jnp.dot(aggregated[...], w_in[full:, :], preferred_element_type=F32)
        else:
            pre = None
            for r, piece in enumerate(far[k - 2]):
                spot = far_spot(r, local)
                part = jnp.dot(n_all[:, spot], piece[:local, :], preferred_element_type=F32)
                part += jnp.dot(aggregated[:, spot], piece[local : 2 * local, :], preferred_element_type=F32)
                pre = part if pre is None else pre + part
        hidden[:, k * local : (k + 1) * local] = silu(pre + bias[k]).astype(BF)
    for r in range(QUARTERS):
        spot = far_spot(r, local)
        total = None
        for k in range(2):
            part = jnp.dot(hidden[:, k * local : (k + 1) * local], whole[k][1][:, spot], preferred_element_type=F32)
            behind = hidden[:, (k + 2) * local : (k + 3) * local]
            part += jnp.dot(behind, far[k][r][2 * local :, :], preferred_element_type=F32)
            total = part if total is None else total + part
        mixed_all[:, spot] = total
    live = lax.broadcasted_iota(jnp.int32, (rows, 1), 0) + first < count_ref[0]
    n_all[...] = finish(mixed_all[...], n_all[...].astype(F32), wide[:1, :], wide[1:2, :], live)
    for k in range(pairs):
        at = pl.ds(pl.multiple_of((me ^ k) * local, local), local)
        outs[k][...] = n_all[:, at]


def layer(
    node_latents,
    edge_latents,
    edge_sender,
    edge_receiver,
    block_owner,
    node_counts,
    halo_nodes,
    w_endpoints,
    w_edge_in,
    edge_bias,
    w_edge_out,
    edge_gain,
    edge_shift,
    w_node_in,
    node_bias,
    w_node_out,
    node_gain,
    node_shift,
):
    patches = lax.axis_size("patch")
    pairs = lax.axis_size("pair")
    me = lax.axis_index("pair")
    full, local = w_edge_in.shape
    node_total = node_latents.shape[0]
    edge_total = edge_latents.shape[0]
    blocks, tile = edge_sender.shape
    halo = halo_nodes.shape[2]
    mine = blocks // pairs
    rows = edge_total // pairs
    quarter = node_total // pairs
    if pairs != QUARTERS or patches % QUARTERS or mine % 2 or halo & (halo - 1):
        raise ValueError("unsupported mesh")
    by_swap = patches <= 8 and halo % LANES == 0
    direct = blocks == patches and mine == 2

    def to_pairs(pieces):
        far = {k: swap(pieces[k], "pair", k) for k in (2, 3, 1)}
        return [pieces[0]] + [far[k] for k in range(1, pairs)]

    send_list = halo_nodes[0]
    if by_swap:
        picked = halo_rows(True, send_list, node_latents)
        table = [picked[0]] + [swap(picked[k], "patch", k) for k in range(1, patches)]
    else:
        picked = halo_rows(False, send_list.reshape(-1, 2 * LANES), node_latents)
        table = [lax.all_to_all(jnp.concatenate(picked, axis=0), "patch", 0, 0, tiled=True)]

    ends = w_endpoints.reshape(2 * full, local)
    w_nodes = w_node_in.reshape(2 * full, local)
    e_piece, n_piece = pl.pallas_call(
        functools.partial(pieces_kernel, local),
        compiler_params=grant(12),
        in_specs=[ANY] * 5,
        out_specs=[VMEM] * 2,
        out_shape=[jax.ShapeDtypeStruct((4 * local, local), BF), jax.ShapeDtypeStruct((3 * local, local), BF)],
        scratch_shapes=[pltpu.VMEM((2 * local, local), BF), pltpu.SemaphoreType.DMA((6,))],
    )(w_edge_in, ends, w_edge_out, w_nodes, w_node_out)
    parted = pl.pallas_call(
        parted_kernel,
        compiler_params=grant(12),
        in_specs=[VMEM],
        out_specs=VMEM,
        out_shape=jax.ShapeDtypeStruct((2 * full, local), BF),
    )(ends)

    def gather_slices(own, piece):
        parts = list(own) + [swap(w, "pair", 1) for w in own]
        near = swap(piece, "pair", 2)
        side = swap(near, "patch", 1)
        far = [near, side, swap(near, "patch", 2), swap(side, "patch", 2)]
        return parts + far + [swap(w, "pair", 1) for w in far]

    e_weights = gather_slices((w_edge_in, parted, w_edge_out), e_piece)
    n_weights = gather_slices((w_nodes, w_node_out), n_piece)

    e_parts = to_pairs(split(block_owner, tile, mine, direct, pairs, edge_latents, edge_bias, edge_gain, edge_shift))
    seen, segment, my_ids = sender_rows(by_swap, direct, pairs, halo, block_owner, edge_sender, edge_receiver, table)
    s_parts = to_pairs(seen)

    wide = full + LANES
    results = pl.pallas_call(
        functools.partial(edge_kernel, pairs, mine, direct),
        compiler_params=grant(28),
        in_specs=[SMEM] + [VMEM] * (2 + 2 * pairs + len(e_weights)),
        out_specs=[VMEM] * (pairs + mine),
        out_shape=[jax.ShapeDtypeStruct((rows, local), BF)] * pairs
        + [jax.ShapeDtypeStruct((RT, wide), BF)] * mine,
        scratch_shapes=[
            pltpu.VMEM((rows, full), BF),
            pltpu.VMEM((rows, full), BF),
            pltpu.VMEM((mine * RT, full), BF),
            pltpu.VMEM((rows, full), BF),
            pltpu.VMEM((rows, full), F32),
            pltpu.VMEM((rows, full), BF),
            pltpu.VMEM((8, full), F32),
        ],
        cost_estimate=pl.CostEstimate(
            flops=6 * rows * full * full, bytes_accessed=10 * full * full, transcendentals=rows * full
        ),
    )(
        block_owner,
        segment,
        my_ids,
        *e_parts,
        *s_parts,
        *e_weights,
    )
    new_edges, sums = results[:pairs], results[pairs:]

    if direct:
        got = []
        for t in range(mine):
            route = []
            for p in range(patches):
                for j in range(pairs):
                    to = (j * mine + (p % 2 ^ t)) * pairs + p // mine
                    route.append((p * pairs + j, to))
            got.append(lax.ppermute(sums[t], ("patch", "pair"), route))
        got = to_pairs([jnp.concatenate(got, axis=0)] * pairs)
    else:
        all_sums = jnp.stack(to_pairs([jnp.stack(sums)] * pairs)).reshape(blocks, RT * wide)
        peers = jnp.arange(pairs, dtype=jnp.int32) ^ me
        owners = block_owner.reshape(pairs, mine)[peers].reshape(-1)
        take = owners[None, :] == jnp.arange(patches, dtype=jnp.int32)[:, None]
        sent = jnp.dot(take.astype(BF), all_sums, preferred_element_type=F32).reshape(patches, RT, wide)
        none = jnp.any(take, axis=1)[:, None, None] | (jnp.arange(wide)[None, None, :] < full)
        sent = jnp.where(none, sent, -1.0).astype(BF)
        got = [lax.all_to_all(sent, "patch", 0, 0, tiled=True).reshape(patches * RT, wide)]

    new_edges = to_pairs(new_edges)
    edges_out = join(block_owner, tile, mine, direct, new_edges)

    n_parts = to_pairs(split(node_counts, quarter, 1, False, pairs, node_latents, node_bias, node_gain, node_shift))
    new_nodes = pl.pallas_call(
        functools.partial(node_kernel, pairs, len(got), direct),
        compiler_params=grant(20),
        in_specs=[SMEM] + [VMEM] * (1 + pairs + len(got) + len(n_weights)),
        out_specs=[VMEM] * pairs,
        out_shape=[jax.ShapeDtypeStruct((quarter, local), BF)] * pairs,
        scratch_shapes=[
            pltpu.VMEM((quarter, full), BF),
            pltpu.VMEM((patches * RT, full), BF),
            pltpu.VMEM((patches * RT, LANES), F32),
            pltpu.VMEM((quarter, full), BF),
            pltpu.VMEM((quarter, full), BF),
            pltpu.VMEM((quarter, full), F32),
            pltpu.VMEM((8, full), F32),
        ],
        cost_estimate=pl.CostEstimate(
            flops=6 * quarter * full * full, bytes_accessed=8 * full * full, transcendentals=quarter * full
        ),
    )(
        node_counts,
        send_list,
        *n_parts,
        *got,
        *n_weights,
    )
    nodes_out = join(node_counts, quarter, 1, False, to_pairs(new_nodes))
    return (nodes_out, edges_out)


def solution(mesh):
    return jax.shard_map(
        layer,
        mesh=mesh,
        in_specs=(
            P("patch", "pair"),
            P("patch", "pair"),
            P("patch", None),
            P("patch", None),
            P("patch"),
            P("patch"),
            P("patch", None, None),
            P(None, None, "pair"),
            P(None, "pair"),
            P("pair"),
            P("pair", None),
            P("pair"),
            P("pair"),
            P(None, None, "pair"),
            P("pair"),
            P("pair", None),
            P("pair"),
            P("pair"),
        ),
        out_specs=(P("patch", "pair"), P("patch", "pair")),
        check_vma=False,
    )
```

time: 188 us -> 153 us (0.81)
  Pallas kernels: 41 us -> 19.8 us
  local copies, waits for them, and re-layouts: 12 us -> 3.92 us
  other arithmetic: 7.19 us -> 0 us
  waiting for transfers between devices: 81.9 us -> 86.9 us
  starting transfers between devices: 44.1 us -> 40.4 us
    pallas_call x10, Pallas kernels: 41 us -> 19.8 us  [the longest x1 6.09 us: layer(): pl.pallas_call(functools.partial(edge_kernel, pairs, mine, direct), compi...]
    ppermute x43 -> x46, waiting for transfers between devices: 79.3 us -> 86.9 us  [swap(): return lax.ppermute(value, axis, [(i, i ^ mask) for i in range(size)])]
    gather x5 -> x0, local copies, waits for them, and re-layouts: 3.36 us -> none  [the longest x1 1.13 us: layer(): my_segment = segment[my_blocks]]
    ppermute x43 -> x46, starting transfers between devices: 42.2 us -> 39.1 us  [swap(): return lax.ppermute(value, axis, [(i, i ^ mask) for i in range(size)])]
    ppermute x2, waiting for transfers between devices: 2.6 us -> 0.01 us  [layer(): got.append(lax.ppermute(sums[t], ('patch', 'pair'), route))]
    another operation x7 -> x0, other arithmetic: 2.56 us -> none
  transfers between devices with their start and end apart: 45 -> 48, of which waited for: 14 -> 17; matrix products, arithmetic and copies ran while one was open for 8% -> 1% of each run, Pallas kernels for 15% -> 8%
where the time goes in v2:
time: 153 us
  waiting for transfers between devices  86.9 us (57%)
  starting transfers between devices  40.4 us (26%)
  Pallas kernels  19.8 us (13%)
  local copies, waits for them, and re-layouts  3.92 us (3%)
  between operations  1.6 us (1%)
    ppermute x46, waiting for transfers between devices, swap(): return lax.ppermute(value, axis, [(i, i ^ mask) for i in range(size)])  86.9 us
    ppermute x46, starting transfers between devices, swap(): return lax.ppermute(value, axis, [(i, i ^ mask) for i in range(size)])  39.1 us
    pallas_call x1, Pallas kernels, layer(): pl.pallas_call(functools.partial(edge_kernel, pairs, mine, direct), compi...  6.09 us
    pallas_call x1, Pallas kernels, sender_rows(): pl.pallas_call(functools.partial(sender_kernel, by_swap, direct, pairs, h...  3.19 us
    pallas_call x1, Pallas kernels, halo_rows(): pl.pallas_call(functools.partial(halo_kernel, by_swap), in_specs=[VMEM] *...  3.07 us
  transfers between devices with their start and end apart: 48, of which 17 were waited for; matrix products, arithmetic and copies ran while one was open for 1% of the time, Pallas kernels for 8%

profile of v2, /device:TPU:0, one launch (start us, length us, event | category | flops | bytes accessed | tf_op | source)
XLA Modules:
  0.0 152.6 jit_solution(16217768097426108864)
XLA Ops:
  0.6 3.1 %shard_map.186 = (bf16[256,256]{1,0:T(8,128)(2,1)}, bf16[256,256]{1,0:T(8,128)(2,1)}, bf16[256,256]{1,0:T(8,128)(2,1)}, bf16[256,256]{1,0:T(8,128)(2,1)}, bf16[2...) custom-call(s32[8,256]{1,0:T(8,128)} %bitcast.11, ...), custom_call_target="tpu_custom_call" | custom-call | flops 1073741824 | bytes 262144 | tf_op jit(solution)/shard_map/pallas_call | solution.py:68
  3.7 3.0 %collective-permute-start.3 = (bf16[256,256]{1,0:T(8,128)(2,1)}, bf16[256,256]{1,0:T(8,128)(2,1)S(1)}, u32[]{:S(2)}, u32[]{:S(2)}) collective-permute-start(bf16[256,256]{1,0:T(8,128)(2,1)} %get-tuple-element.41), channel_id=1, source_target_pairs={{0,4},{4,0},{8,12},{12,8},{16,20},{20,16},{24,28},{28,24},{1,5},{5... | collective-permute-start | bytes 393224 | tf_op jit(solution)/shard_map/ppermute | solution.py:26
  6.7 1.6 %collective-permute-start.4 = (bf16[256,256]{1,0:T(8,128)(2,1)}, bf16[256,256]{1,0:T(8,128)(2,1)S(1)}, u32[]{:S(2)}, u32[]{:S(2)}) collective-permute-start(bf16[256,256]{1,0:T(8,128)(2,1)} %get-tuple-element.42), channel_id=1, source_target_pairs={{0,8},{4,12},{8,0},{12,4},{16,24},{20,28},{24,16},{28,20},{1,9},{5... | collective-permute-start | bytes 393224 | tf_op jit(solution)/shard_map/ppermute | solution.py:26
  8.2 1.5 reshape.34.ends_ref
  9.8 1.0 copy-done.4
  10.9 0.9 shard_map.190
  11.7 1.6 %collective-permute-start.19 = (bf16[1024,256]{1,0:T(8,128)(2,1)S(1)}, bf16[1024,256]{1,0:T(8,128)(2,1)S(1)}, u32[]{:S(2)}, u32[]{:S(2)}) collective-permute-start(bf16[1024,256]{1,0:T(8,128)(2,1)S(1)} %get-tuple-element.58), channel_id=1, source_target_pairs={{0,2},{1,3},{2,0},{3,1},{4,6},{5,7},{6,4},{7,5},{8,10},{9,11},{10,... | collective-permute-start | bytes 1572872 | tf_op jit(solution)/shard_map/ppermute | solution.py:26
  13.9 2.6 %collective-permute-start.6 = (bf16[256,256]{1,0:T(8,128)(2,1)S(1)}, bf16[256,256]{1,0:T(8,128)(2,1)S(1)}, u32[]{:S(2)}, u32[]{:S(2)}) collective-permute-start(bf16[256,256]{1,0:T(8,128)(2,1)S(1)} %copy-done.21), channel_id=1, source_target_pairs={{0,16},{4,20},{8,24},{12,28},{16,0},{20,4},{24,8},{28,12},{1,17},{... | collective-permute-start | bytes 393224 | tf_op jit(solution)/shard_map/ppermute | solution.py:26
  16.5 1.3 collective-permute-start.7
  17.8 3.4 %collective-permute-start.8 = (bf16[256,256]{1,0:T(8,128)(2,1)S(1)}, bf16[256,256]{1,0:T(8,128)(2,1)S(1)}, u32[]{:S(2)}, u32[]{:S(2)}) collective-permute-start(bf16[256,256]{1,0:T(8,128)(2,1)S(1)} %copy-done.19), channel_id=1, source_target_pairs={{0,24},{4,28},{8,16},{12,20},{16,8},{20,12},{24,0},{28,4},{1,25},{... | collective-permute-start | bytes 393224 | tf_op jit(solution)/shard_map/ppermute | solution.py:26
  21.2 1.8 %collective-permute-start.9 = (bf16[256,256]{1,0:T(8,128)(2,1)S(1)}, bf16[256,256]{1,0:T(8,128)(2,1)S(1)}, u32[]{:S(2)}, u32[]{:S(2)}) collective-permute-start(bf16[256,256]{1,0:T(8,128)(2,1)S(1)} %copy-done.18), channel_id=1, source_target_pairs={{0,28},{4,24},{8,20},{12,16},{16,12},{20,8},{24,4},{28,0},{1,29},{... | collective-permute-start | bytes 393224 | tf_op jit(solution)/shard_map/ppermute | solution.py:26
  23.8 0.6 copy-done.9
  24.4 7.7 %collective-permute-done.6.refs_4_ = bf16[256,256]{1,0:T(8,128)(2,1)S(1)} collective-permute-done((bf16[256,256]{1,0:T(8,128)(2,1)S(1)}, bf16[256,256]{1,0:T(8,128)(2,1)S(1)}, u32[]{:S(2)}, u32[]{:S(2)}) %collective-permute-start.6) | collective-permute-done | bytes 131104 | tf_op jit(solution)/shard_map/ppermute | solution.py:26
  32.1 4.0 %collective-permute-done.7.refs_5_ = bf16[256,256]{1,0:T(8,128)(2,1)S(1)} collective-permute-done((bf16[256,256]{1,0:T(8,128)(2,1)S(1)}, bf16[256,256]{1,0:T(8,128)(2,1)S(1)}, u32[]{:S(2)}, u32[]{:S(2)}) %collective-permute-start.7) | collective-permute-done | bytes 131104 | tf_op jit(solution)/shard_map/ppermute | solution.py:26
  38.1 1.6 %collective-permute-start.11 = (bf16[528,256]{1,0:T(8,128)(2,1)S(1)}, bf16[528,256]{1,0:T(8,128)(2,1)S(1)}, u32[]{:S(2)}, u32[]{:S(2)}) collective-permute-start(bf16[528,256]{1,0:T(8,128)(2,1)S(1)} %get-tuple-element.52), channel_id=1, source_target_pairs={{0,2},{1,3},{2,0},{3,1},{4,6},{5,7},{6,4},{7,5},{8,10},{9,11},{10,... | collective-permute-start | bytes 811016 | tf_op jit(solution)/shard_map/ppermute | solution.py:26
  39.9 1.3 collective-permute-done.1.refs_2_
  41.7 3.2 %shard_map.187 = (bf16[544,256]{1,0:T(8,128)(2,1)S(1)}, bf16[544,256]{1,0:T(8,128)(2,1)S(1)}, bf16[544,256]{1,0:T(8,128)(2,1)S(1)}, bf16[544,256]{1,0:T(8,128)(2...) custom-call(s32[8]{0:T(128)S(1)} %copy-done.8, s32[8,256]{1,0:T(8,128)S(1)} %copy-done.15, ...), custom_call_target="tpu_custom_call" | custom-call | flops 2281701376 | bytes 2228224 | tf_op jit(solution)/shard_map/pallas_call | solution.py:129
  45.1 2.4 %collective-permute-done.11.refs_2_ = bf16[528,256]{1,0:T(8,128)(2,1)S(1)} collective-permute-done((bf16[528,256]{1,0:T(8,128)(2,1)S(1)}, bf16[528,256]{1,0:T(8,128)(2,1)S(1)}, u32[]{:S(2)}, u32[]{:S(2)}) %collective-permute-start.11) | collective-permute-done | bytes 270368 | tf_op jit(solution)/shard_map/ppermute | solution.py:26
  47.5 1.5 collective-permute-start.14
  49.0 3.3 %collective-permute-done.12.refs_3_ = bf16[528,256]{1,0:T(8,128)(2,1)S(1)} collective-permute-done((bf16[528,256]{1,0:T(8,128)(2,1)S(1)}, bf16[528,256]{1,0:T(8,128)(2,1)S(1)}, u32[]{:S(2)}, u32[]{:S(2)}) %collective-permute-start.12) | collective-permute-done | bytes 270368 | tf_op jit(solution)/shard_map/ppermute | solution.py:26
  52.3 1.1 collective-permute-start.16
  53.4 8.3 %collective-permute-done.34.refs_12_ = bf16[768,256]{1,0:T(8,128)(2,1)S(1)} collective-permute-done((bf16[768,256]{1,0:T(8,128)(2,1)S(1)}, bf16[768,256]{1,0:T(8,128)(2,1)S(1)}, u32[]{:S(2)}, u32[]{:S(2)}) %collective-permute-start.34) | collective-permute-done | bytes 393248 | tf_op jit(solution)/shard_map/ppermute | solution.py:26
  61.9 1.5 collective-permute-start.18
  63.8 3.9 %collective-permute-done.14.refs_6_ = bf16[544,256]{1,0:T(8,128)(2,1)S(1)} collective-permute-done((bf16[544,256]{1,0:T(8,128)(2,1)S(1)}, bf16[544,256]{1,0:T(8,128)(2,1)S(1)}, u32[]{:S(2)}, u32[]{:S(2)}) %collective-permute-start.14) | collective-permute-done | bytes 278560 | tf_op jit(solution)/shard_map/ppermute | solution.py:26
  67.7 4.9 %collective-permute-done.15.refs_7_ = bf16[544,256]{1,0:T(8,128)(2,1)S(1)} collective-permute-done((bf16[544,256]{1,0:T(8,128)(2,1)S(1)}, bf16[544,256]{1,0:T(8,128)(2,1)S(1)}, u32[]{:S(2)}, u32[]{:S(2)}) %collective-permute-start.15) | collective-permute-done | bytes 278560 | tf_op jit(solution)/shard_map/ppermute | solution.py:26
  72.6 0.8 collective-permute-start.21
  73.4 1.2 collective-permute-start.22
  75.2 10.2 %collective-permute-done.35.refs_13_ = bf16[768,256]{1,0:T(8,128)(2,1)S(1)} collective-permute-done((bf16[768,256]{1,0:T(8,128)(2,1)S(1)}, bf16[768,256]{1,0:T(8,128)(2,1)S(1)}, u32[]{:S(2)}, u32[]{:S(2)}) %collective-permute-start.35) | collective-permute-done | bytes 393248 | tf_op jit(solution)/shard_map/ppermute | solution.py:26
  85.4 2.0 %collective-permute-done.21.refs_16_ = bf16[1024,256]{1,0:T(8,128)(2,1)S(1)} collective-permute-done((bf16[1024,256]{1,0:T(8,128)(2,1)S(1)}, bf16[1024,256]{1,0:T(8,128)(2,1)S(1)}, u32[]{:S(2)}, u32[]{:S(2)}) %collective-permute-start.21) | collective-permute-done | bytes 524320 | tf_op jit(solution)/shard_map/ppermute | solution.py:26
  87.4 10.6 %collective-permute-done.22.refs_17_ = bf16[1024,256]{1,0:T(8,128)(2,1)S(1)} collective-permute-done((bf16[1024,256]{1,0:T(8,128)(2,1)S(1)}, bf16[1024,256]{1,0:T(8,128)(2,1)S(1)}, u32[]{:S(2)}, u32[]{:S(2)}) %collective-permute-start.22) | collective-permute-done | bytes 524320 | tf_op jit(solution)/shard_map/ppermute | solution.py:26
  98.6 0.7 collective-permute-start.36
  99.3 1.3 collective-permute-start.37
  100.6 1.0 collective-permute-start.2
  101.6 6.1 %shard_map.191 = (bf16[512,256]{1,0:T(8,128)(2,1)S(1)}, bf16[512,256]{1,0:T(8,128)(2,1)S(1)}, bf16[512,256]{1,0:T(8,128)(2,1)S(1)}, bf16[512,256]{1,0:T(8,128)(2...) custom-call(s32[8]{0:T(128)S(1)} %copy-done.8, s32[8,256]{1,0:T(8,128)S(1)} %get-tuple-element.48.segrow_ref, ...), custom_call_target="tpu_custom_call" | custom-call | flops 3221225472 | bytes 10485760 | tf_op jit(solution)/shard_map/pallas_call | solution.py:493
  107.7 0.8 collective-permute-start.27
  109.0 1.6 %collective-permute-done.36.refs_14_ = bf16[768,256]{1,0:T(8,128)(2,1)S(1)} collective-permute-done((bf16[768,256]{1,0:T(8,128)(2,1)S(1)}, bf16[768,256]{1,0:T(8,128)(2,1)S(1)}, u32[]{:S(2)}, u32[]{:S(2)}) %collective-permute-start.36) | collective-permute-done | bytes 393248 | tf_op jit(solution)/shard_map/ppermute | solution.py:26
  110.6 1.5 collective-permute-start.38
  112.0 7.2 %collective-permute-done.37.refs_15_ = bf16[768,256]{1,0:T(8,128)(2,1)S(1)} collective-permute-done((bf16[768,256]{1,0:T(8,128)(2,1)S(1)}, bf16[768,256]{1,0:T(8,128)(2,1)S(1)}, u32[]{:S(2)}, u32[]{:S(2)}) %collective-permute-start.37) | collective-permute-done | bytes 393248 | tf_op jit(solution)/shard_map/ppermute | solution.py:26
  120.4 3.1 %collective-permute-start.30 = (bf16[32,1152]{1,0:T(8,128)(2,1)S(1)}, bf16[32,1152]{1,0:T(8,128)(2,1)S(1)}, u32[]{:S(2)}, u32[]{:S(2)}) collective-permute-start(bf16[32,1152]{1,0:T(8,128)(2,1)S(1)} %constant_dynamic-update-slice_fusion.refs_4_), channel_id=1, source_target_pairs={{0,2},{1,3},{2,0},{3,1},{4,6},{5,7},{6,4},{7,5},{8,10},{9,11},{10,... | collective-permute-start | bytes 221192 | tf_op jit(solution)/shard_map/ppermute | solution.py:26
  123.5 2.7 %collective-permute-done.30.refs_6_ = bf16[32,1152]{1,0:T(8,128)(2,1)S(1)} collective-permute-done((bf16[32,1152]{1,0:T(8,128)(2,1)S(1)}, bf16[32,1152]{1,0:T(8,128)(2,1)S(1)}, u32[]{:S(2)}, u32[]{:S(2)}) %collective-permute-start.30) | collective-permute-done | bytes 73760 | tf_op jit(solution)/shard_map/ppermute | solution.py:26
  126.3 1.5 collective-permute-done.31.refs_7_
  127.8 3.0 %shard_map.192 = (bf16[256,256]{1,0:T(8,128)(2,1)S(1)}, bf16[256,256]{1,0:T(8,128)(2,1)S(1)}, bf16[256,256]{1,0:T(8,128)(2,1)S(1)}, bf16[256,256]{1,0:T(8,128)(2,1)S(1)}) custom-call(s32[1]{0:T(128)S(6)} %copy.21.owner_ref.count_ref, s32[8,256]{1,0:T(8,128)S(1)} %bitcast.12, bf16[272,256]{1,0:T(8,128)(2,1)S(1)} %get-tuple-element.36.refs_0_, ...), custom_call_target="tpu_custom_call" | custom-call | flops 1610612736 | bytes 8388608 | tf_op jit(solution)/shard_map/pallas_call | solution.py:546
  131.4 1.2 collective-permute-start.46
  132.9 1.5 %collective-permute-start.43 = (bf16[256,256]{1,0:T(8,128)(2,1)S(1)}, bf16[256,256]{1,0:T(8,128)(2,1)S(1)}, u32[]{:S(2)}, u32[]{:S(2)}) collective-permute-start(bf16[256,256]{1,0:T(8,128)(2,1)S(1)} %get-tuple-element.64), channel_id=1, source_target_pairs={{0,2},{1,3},{2,0},{3,1},{4,6},{5,7},{6,4},{7,5},{8,10},{9,11},{10,... | collective-permute-start | bytes 393224 | tf_op jit(solution)/shard_map/ppermute | solution.py:26
  134.9 14.1 %collective-permute-done.43.refs_2_ = bf16[256,256]{1,0:T(8,128)(2,1)S(1)} collective-permute-done((bf16[256,256]{1,0:T(8,128)(2,1)S(1)}, bf16[256,256]{1,0:T(8,128)(2,1)S(1)}, u32[]{:S(2)}, u32[]{:S(2)}) %collective-permute-start.43) | collective-permute-done | bytes 131104 | tf_op jit(solution)/shard_map/ppermute | solution.py:26
  149.0 1.1 collective-permute-done.44.refs_3_
  150.1 0.8 shard_map.193
  150.9 1.7 %shard_map.194 = bf16[2048,256]{1,0:T(8,128)(2,1)} custom-call(s32[8]{0:T(128)S(1)} %copy-done.8, bf16[512,256]{1,0:T(8,128)(2,1)S(1)} %get-tuple-element.66.refs_0_, bf16[512,256]{1,0:T(8,128)(2,1)S(1)} %collective-permute-done.45.refs_1_, bf16[512,256]{1,0:T(8,128)(2,1)S(1)} %collective-permute-done.46.refs_2_, ...), custom_call_target="tpu_custom_call" | custom-call | tf_op jit(solution)/shard_map/pallas_call | solution.py:187
  (107 shorter events, 8.3 us)
Async XLA Ops:
  3.7 12.8 %collective-permute-start.3 = (bf16[256,256]{1,0:T(8,128)(2,1)}, bf16[256,256]{1,0:T(8,128)(2,1)S(1)}, u32[]{:S(2)}, u32[]{:S(2)}) collective-permute-start(bf16[256,256]{1,0:T(8,128)(2,1)} %get-tuple-element.41), channel_id=1, source_target_pairs={{0,4},{4,0},{8,12},{12,8},{16,20},{20,16},{24,28},{28,24},{1,5},{5... | collective-permute-start | bytes 393224 | tf_op jit(solution)/shard_map/ppermute | solution.py:26
  6.7 11.1 %collective-permute-start.4 = (bf16[256,256]{1,0:T(8,128)(2,1)}, bf16[256,256]{1,0:T(8,128)(2,1)S(1)}, u32[]{:S(2)}, u32[]{:S(2)}) collective-permute-start(bf16[256,256]{1,0:T(8,128)(2,1)} %get-tuple-element.42), channel_id=1, source_target_pairs={{0,8},{4,12},{8,0},{12,4},{16,24},{20,28},{24,16},{28,20},{1,9},{5... | collective-permute-start | bytes 393224 | tf_op jit(solution)/shard_map/ppermute | solution.py:26
  11.7 33.2 %collective-permute-start.19 = (bf16[1024,256]{1,0:T(8,128)(2,1)S(1)}, bf16[1024,256]{1,0:T(8,128)(2,1)S(1)}, u32[]{:S(2)}, u32[]{:S(2)}) collective-permute-start(bf16[1024,256]{1,0:T(8,128)(2,1)S(1)} %get-tuple-element.58), channel_id=1, source_target_pairs={{0,2},{1,3},{2,0},{3,1},{4,6},{5,7},{6,4},{7,5},{8,10},{9,11},{10,... | collective-permute-start | bytes 1572872 | tf_op jit(solution)/shard_map/ppermute | solution.py:26
  13.3 7.9 %collective-permute-start.5 = (bf16[256,256]{1,0:T(8,128)(2,1)S(1)}, bf16[256,256]{1,0:T(8,128)(2,1)S(1)}, u32[]{:S(2)}, u32[]{:S(2)}) collective-permute-start(bf16[256,256]{1,0:T(8,128)(2,1)S(1)} %copy-done.22), channel_id=1, source_target_pairs={{0,12},{4,8},{8,4},{12,0},{16,28},{20,24},{24,20},{28,16},{1,13},{... | collective-permute-start | bytes 393224 | tf_op jit(solution)/shard_map/ppermute | solution.py:26
  13.9 18.2 %collective-permute-start.6 = (bf16[256,256]{1,0:T(8,128)(2,1)S(1)}, bf16[256,256]{1,0:T(8,128)(2,1)S(1)}, u32[]{:S(2)}, u32[]{:S(2)}) collective-permute-start(bf16[256,256]{1,0:T(8,128)(2,1)S(1)} %copy-done.21), channel_id=1, source_target_pairs={{0,16},{4,20},{8,24},{12,28},{16,0},{20,4},{24,8},{28,12},{1,17},{... | collective-permute-start | bytes 393224 | tf_op jit(solution)/shard_map/ppermute | solution.py:26
  16.5 19.6 %collective-permute-start.7 = (bf16[256,256]{1,0:T(8,128)(2,1)S(1)}, bf16[256,256]{1,0:T(8,128)(2,1)S(1)}, u32[]{:S(2)}, u32[]{:S(2)}) collective-permute-start(bf16[256,256]{1,0:T(8,128)(2,1)S(1)} %copy-done.20), channel_id=1, source_target_pairs={{0,20},{4,16},{8,28},{12,24},{16,4},{20,0},{24,12},{28,8},{1,21},{... | collective-permute-start | bytes 393224 | tf_op jit(solution)/shard_map/ppermute | solution.py:26
  17.8 20.2 %collective-permute-start.8 = (bf16[256,256]{1,0:T(8,128)(2,1)S(1)}, bf16[256,256]{1,0:T(8,128)(2,1)S(1)}, u32[]{:S(2)}, u32[]{:S(2)}) collective-permute-start(bf16[256,256]{1,0:T(8,128)(2,1)S(1)} %copy-done.19), channel_id=1, source_target_pairs={{0,24},{4,28},{8,16},{12,20},{16,8},{20,12},{24,0},{28,4},{1,25},{... | collective-permute-start | bytes 393224 | tf_op jit(solution)/shard_map/ppermute | solution.py:26
  21.2 16.8 %collective-permute-start.9 = (bf16[256,256]{1,0:T(8,128)(2,1)S(1)}, bf16[256,256]{1,0:T(8,128)(2,1)S(1)}, u32[]{:S(2)}, u32[]{:S(2)}) collective-permute-start(bf16[256,256]{1,0:T(8,128)(2,1)S(1)} %copy-done.18), channel_id=1, source_target_pairs={{0,28},{4,24},{8,20},{12,16},{16,12},{20,8},{24,4},{28,0},{1,29},{... | collective-permute-start | bytes 393224 | tf_op jit(solution)/shard_map/ppermute | solution.py:26
  32.1 7.5 %collective-permute-start = (bf16[272,256]{1,0:T(8,128)(2,1)S(1)}, bf16[272,256]{1,0:T(8,128)(2,1)S(1)}, u32[]{:S(2)}, u32[]{:S(2)}) collective-permute-start(bf16[272,256]{1,0:T(8,128)(2,1)S(1)} %get-tuple-element.37), channel_id=1, source_target_pairs={{0,1},{1,0},{2,3},{3,2},{4,5},{5,4},{6,7},{7,6},{8,9},{9,8},{10,11... | collective-permute-start | bytes 417800 | tf_op jit(solution)/shard_map/ppermute | solution.py:26
  36.1 5.1 %collective-permute-start.1 = (bf16[272,256]{1,0:T(8,128)(2,1)S(1)}, bf16[272,256]{1,0:T(8,128)(2,1)S(1)}, u32[]{:S(2)}, u32[]{:S(2)}) collective-permute-start(bf16[272,256]{1,0:T(8,128)(2,1)S(1)} %get-tuple-element.38), channel_id=1, source_target_pairs={{0,2},{1,3},{2,0},{3,1},{4,6},{5,7},{6,4},{7,5},{8,10},{9,11},{10,... | collective-permute-start | bytes 417800 | tf_op jit(solution)/shard_map/ppermute | solution.py:26
  38.0 6.9 %collective-permute-start.10 = (bf16[528,256]{1,0:T(8,128)(2,1)S(1)}, bf16[528,256]{1,0:T(8,128)(2,1)S(1)}, u32[]{:S(2)}, u32[]{:S(2)}) collective-permute-start(bf16[528,256]{1,0:T(8,128)(2,1)S(1)} %get-tuple-element.51), channel_id=1, source_target_pairs={{0,1},{1,0},{2,3},{3,2},{4,5},{5,4},{6,7},{7,6},{8,9},{9,8},{10,11... | collective-permute-start | bytes 811016 | tf_op jit(solution)/shard_map/ppermute | solution.py:26
  38.1 9.4 %collective-permute-start.11 = (bf16[528,256]{1,0:T(8,128)(2,1)S(1)}, bf16[528,256]{1,0:T(8,128)(2,1)S(1)}, u32[]{:S(2)}, u32[]{:S(2)}) collective-permute-start(bf16[528,256]{1,0:T(8,128)(2,1)S(1)} %get-tuple-element.52), channel_id=1, source_target_pairs={{0,2},{1,3},{2,0},{3,1},{4,6},{5,7},{6,4},{7,5},{8,10},{9,11},{10,... | collective-permute-start | bytes 811016 | tf_op jit(solution)/shard_map/ppermute | solution.py:26
  39.6 12.7 %collective-permute-start.12 = (bf16[528,256]{1,0:T(8,128)(2,1)S(1)}, bf16[528,256]{1,0:T(8,128)(2,1)S(1)}, u32[]{:S(2)}, u32[]{:S(2)}) collective-permute-start(bf16[528,256]{1,0:T(8,128)(2,1)S(1)} %get-tuple-element.53), channel_id=1, source_target_pairs={{0,3},{1,2},{2,1},{3,0},{4,7},{5,6},{6,5},{7,4},{8,11},{9,10},{10,... | collective-permute-start | bytes 811016 | tf_op jit(solution)/shard_map/ppermute | solution.py:26
  41.2 20.5 %collective-permute-start.34 = (bf16[768,256]{1,0:T(8,128)(2,1)S(1)}, bf16[768,256]{1,0:T(8,128)(2,1)S(1)}, u32[]{:S(2)}, u32[]{:S(2)}) collective-permute-start(bf16[768,256]{1,0:T(8,128)(2,1)S(1)} %get-tuple-element.61), channel_id=1, source_target_pairs={{0,2},{1,3},{2,0},{3,1},{4,6},{5,7},{6,4},{7,5},{8,10},{9,11},{10,... | collective-permute-start | bytes 1179656 | tf_op jit(solution)/shard_map/ppermute | solution.py:26
  44.9 17.0 %collective-permute-start.13 = (bf16[544,256]{1,0:T(8,128)(2,1)S(1)}, bf16[544,256]{1,0:T(8,128)(2,1)S(1)}, u32[]{:S(2)}, u32[]{:S(2)}) collective-permute-start(bf16[544,256]{1,0:T(8,128)(2,1)S(1)} %get-tuple-element.55), channel_id=1, source_target_pairs={{0,1},{1,0},{2,3},{3,2},{4,5},{5,4},{6,7},{7,6},{8,9},{9,8},{10,11... | collective-permute-start | bytes 835592 | tf_op jit(solution)/shard_map/ppermute | solution.py:26
  45.0 28.4 %collective-permute-start.20 = (bf16[1024,256]{1,0:T(8,128)(2,1)S(1)}, bf16[1024,256]{1,0:T(8,128)(2,1)S(1)}, u32[]{:S(2)}, u32[]{:S(2)}) collective-permute-start(bf16[1024,256]{1,0:T(8,128)(2,1)S(1)} %collective-permute-done.19.refs_14_), channel_id=1, source_target_pairs={{0,4},{4,0},{8,12},{12,8},{16,20},{20,16},{24,28},{28,24},{1,5},{5... | collective-permute-start | bytes 1572872 | tf_op jit(solution)/shard_map/ppermute | solution.py:26
  47.5 20.2 %collective-permute-start.14 = (bf16[544,256]{1,0:T(8,128)(2,1)S(1)}, bf16[544,256]{1,0:T(8,128)(2,1)S(1)}, u32[]{:S(2)}, u32[]{:S(2)}) collective-permute-start(bf16[544,256]{1,0:T(8,128)(2,1)S(1)} %get-tuple-element.56), channel_id=1, source_target_pairs={{0,2},{1,3},{2,0},{3,1},{4,6},{5,7},{6,4},{7,5},{8,10},{9,11},{10,... | collective-permute-start | bytes 835592 | tf_op jit(solution)/shard_map/ppermute | solution.py:26
  52.3 22.3 %collective-permute-start.16 = (bf16[1024,256]{1,0:T(8,128)(2,1)S(1)}, bf16[1024,256]{1,0:T(8,128)(2,1)S(1)}, u32[]{:S(2)}, u32[]{:S(2)}) collective-permute-start(bf16[1024,256]{1,0:T(8,128)(2,1)S(1)} %copy-done.3), channel_id=1, source_target_pairs={{0,1},{1,0},{2,3},{3,2},{4,5},{5,4},{6,7},{7,6},{8,9},{9,8},{10,11... | collective-permute-start | bytes 1572872 | tf_op jit(solution)/shard_map/ppermute | solution.py:26
  61.7 10.9 %collective-permute-start.15 = (bf16[544,256]{1,0:T(8,128)(2,1)S(1)}, bf16[544,256]{1,0:T(8,128)(2,1)S(1)}, u32[]{:S(2)}, u32[]{:S(2)}) collective-permute-start(bf16[544,256]{1,0:T(8,128)(2,1)S(1)} %get-tuple-element.57), channel_id=1, source_target_pairs={{0,3},{1,2},{2,1},{3,0},{4,7},{5,6},{6,5},{7,4},{8,11},{9,10},{10,... | collective-permute-start | bytes 835592 | tf_op jit(solution)/shard_map/ppermute | solution.py:26
  61.9 13.4 %collective-permute-start.18 = (bf16[256,1024]{1,0:T(8,128)(2,1)S(1)}, bf16[256,1024]{1,0:T(8,128)(2,1)S(1)}, u32[]{:S(2)}, u32[]{:S(2)}) collective-permute-start(bf16[256,1024]{1,0:T(8,128)(2,1)S(1)} %copy-done.5), channel_id=1, source_target_pairs={{0,1},{1,0},{2,3},{3,2},{4,5},{5,4},{6,7},{7,6},{8,9},{9,8},{10,11... | collective-permute-start | bytes 1572872 | tf_op jit(solution)/shard_map/ppermute | solution.py:26
  67.7 30.9 %collective-permute-start.17 = (bf16[2048,256]{1,0:T(8,128)(2,1)S(1)}, bf16[2048,256]{1,0:T(8,128)(2,1)S(1)}, u32[]{:S(2)}, u32[]{:S(2)}) collective-permute-start(bf16[2048,256]{1,0:T(8,128)(2,1)S(1)} %shard_map.189.refs_9_), channel_id=1, source_target_pairs={{0,1},{1,0},{2,3},{3,2},{4,5},{5,4},{6,7},{7,6},{8,9},{9,8},{10,11... | collective-permute-start | bytes 3145736 | tf_op jit(solution)/shard_map/ppermute | solution.py:26
  72.6 14.8 %collective-permute-start.21 = (bf16[1024,256]{1,0:T(8,128)(2,1)S(1)}, bf16[1024,256]{1,0:T(8,128)(2,1)S(1)}, u32[]{:S(2)}, u32[]{:S(2)}) collective-permute-start(bf16[1024,256]{1,0:T(8,128)(2,1)S(1)} %collective-permute-done.19.refs_14_), channel_id=1, source_target_pairs={{0,8},{4,12},{8,0},{12,4},{16,24},{20,28},{24,16},{28,20},{1,9},{5... | collective-permute-start | bytes 1572872 | tf_op jit(solution)/shard_map/ppermute | solution.py:26
  73.4 24.6 %collective-permute-start.22 = (bf16[1024,256]{1,0:T(8,128)(2,1)S(1)}, bf16[1024,256]{1,0:T(8,128)(2,1)S(1)}, u32[]{:S(2)}, u32[]{:S(2)}) collective-permute-start(bf16[1024,256]{1,0:T(8,128)(2,1)S(1)} %collective-permute-done.20.refs_15_), channel_id=1, source_target_pairs={{0,8},{4,12},{8,0},{12,4},{16,24},{20,28},{24,16},{28,20},{1,9},{5... | collective-permute-start | bytes 1572872 | tf_op jit(solution)/shard_map/ppermute | solution.py:26
  74.6 10.8 %collective-permute-start.35 = (bf16[768,256]{1,0:T(8,128)(2,1)S(1)}, bf16[768,256]{1,0:T(8,128)(2,1)S(1)}, u32[]{:S(2)}, u32[]{:S(2)}) collective-permute-start(bf16[768,256]{1,0:T(8,128)(2,1)S(1)} %collective-permute-done.34.refs_12_), channel_id=1, source_target_pairs={{0,4},{4,0},{8,12},{12,8},{16,20},{20,16},{24,28},{28,24},{1,5},{5... | collective-permute-start | bytes 1179656 | tf_op jit(solution)/shard_map/ppermute | solution.py:26
  75.2 22.8 %collective-permute-start.23 = (bf16[1024,256]{1,0:T(8,128)(2,1)S(1)}, bf16[1024,256]{1,0:T(8,128)(2,1)S(1)}, u32[]{:S(2)}, u32[]{:S(2)}) collective-permute-start(bf16[1024,256]{1,0:T(8,128)(2,1)S(1)} %collective-permute-done.19.refs_14_), channel_id=1, source_target_pairs={{0,1},{1,0},{2,3},{3,2},{4,5},{5,4},{6,7},{7,6},{8,9},{9,8},{10,11... | collective-permute-start | bytes 1572872 | tf_op jit(solution)/shard_map/ppermute | solution.py:26
  85.4 13.2 %collective-permute-start.24 = (bf16[1024,256]{1,0:T(8,128)(2,1)S(1)}, bf16[1024,256]{1,0:T(8,128)(2,1)S(1)}, u32[]{:S(2)}, u32[]{:S(2)}) collective-permute-start(bf16[1024,256]{1,0:T(8,128)(2,1)S(1)} %collective-permute-done.20.refs_15_), channel_id=1, source_target_pairs={{0,1},{1,0},{2,3},{3,2},{4,5},{5,4},{6,7},{7,6},{8,9},{9,8},{10,11... | collective-permute-start | bytes 1572872 | tf_op jit(solution)/shard_map/ppermute | solution.py:26
  87.4 11.9 %collective-permute-start.25 = (bf16[1024,256]{1,0:T(8,128)(2,1)S(1)}, bf16[1024,256]{1,0:T(8,128)(2,1)S(1)}, u32[]{:S(2)}, u32[]{:S(2)}) collective-permute-start(bf16[1024,256]{1,0:T(8,128)(2,1)S(1)} %collective-permute-done.21.refs_16_), channel_id=1, source_target_pairs={{0,1},{1,0},{2,3},{3,2},{4,5},{5,4},{6,7},{7,6},{8,9},{9,8},{10,11... | collective-permute-start | bytes 1572872 | tf_op jit(solution)/shard_map/ppermute | solution.py:26
  98.0 2.6 %collective-permute-start.26 = (bf16[1024,256]{1,0:T(8,128)(2,1)S(1)}, bf16[1024,256]{1,0:T(8,128)(2,1)S(1)}, u32[]{:S(2)}, u32[]{:S(2)}) collective-permute-start(bf16[1024,256]{1,0:T(8,128)(2,1)S(1)} %collective-permute-done.22.refs_17_), channel_id=1, source_target_pairs={{0,1},{1,0},{2,3},{3,2},{4,5},{5,4},{6,7},{7,6},{8,9},{9,8},{10,11... | collective-permute-start | bytes 1572872 | tf_op jit(solution)/shard_map/ppermute | solution.py:26
  98.0 22.4 %collective-permute-start.32 = (bf16[2048,256]{1,0:T(8,128)(2,1)S(1)}, bf16[2048,256]{1,0:T(8,128)(2,1)S(1)}, u32[]{:S(2)}, u32[]{:S(2)}) collective-permute-start(bf16[2048,256]{1,0:T(8,128)(2,1)S(1)} %bitcast.9), channel_id=1, source_target_pairs={{0,1},{1,0},{2,3},{3,2},{4,5},{5,4},{6,7},{7,6},{8,9},{9,8},{10,11... | collective-permute-start | bytes 3145736 | tf_op jit(solution)/shard_map/ppermute | solution.py:26
  98.5 10.1 %collective-permute-start.33 = (bf16[256,1024]{1,0:T(8,128)(2,1)S(1)}, bf16[256,1024]{1,0:T(8,128)(2,1)S(1)}, u32[]{:S(2)}, u32[]{:S(2)}) collective-permute-start(bf16[256,1024]{1,0:T(8,128)(2,1)S(1)} %copy-done.1), channel_id=1, source_target_pairs={{0,1},{1,0},{2,3},{3,2},{4,5},{5,4},{6,7},{7,6},{8,9},{9,8},{10,11... | collective-permute-start | bytes 1572872 | tf_op jit(solution)/shard_map/ppermute | solution.py:26
  98.6 12.0 %collective-permute-start.36 = (bf16[768,256]{1,0:T(8,128)(2,1)S(1)}, bf16[768,256]{1,0:T(8,128)(2,1)S(1)}, u32[]{:S(2)}, u32[]{:S(2)}) collective-permute-start(bf16[768,256]{1,0:T(8,128)(2,1)S(1)} %collective-permute-done.34.refs_12_), channel_id=1, source_target_pairs={{0,8},{4,12},{8,0},{12,4},{16,24},{20,28},{24,16},{28,20},{1,9},{5... | collective-permute-start | bytes 1179656 | tf_op jit(solution)/shard_map/ppermute | solution.py:26
  99.3 19.9 %collective-permute-start.37 = (bf16[768,256]{1,0:T(8,128)(2,1)S(1)}, bf16[768,256]{1,0:T(8,128)(2,1)S(1)}, u32[]{:S(2)}, u32[]{:S(2)}) collective-permute-start(bf16[768,256]{1,0:T(8,128)(2,1)S(1)} %collective-permute-done.35.refs_13_), channel_id=1, source_target_pairs={{0,8},{4,12},{8,0},{12,4},{16,24},{20,28},{24,16},{28,20},{1,9},{5... | collective-permute-start | bytes 1179656 | tf_op jit(solution)/shard_map/ppermute | solution.py:26
  100.6 7.1 %collective-permute-start.2 = (bf16[272,256]{1,0:T(8,128)(2,1)S(1)}, bf16[272,256]{1,0:T(8,128)(2,1)S(1)}, u32[]{:S(2)}, u32[]{:S(2)}) collective-permute-start(bf16[272,256]{1,0:T(8,128)(2,1)S(1)} %get-tuple-element.39), channel_id=1, source_target_pairs={{0,3},{1,2},{2,1},{3,0},{4,7},{5,6},{6,5},{7,4},{8,11},{9,10},{10,... | collective-permute-start | bytes 417800 | tf_op jit(solution)/shard_map/ppermute | solution.py:26
  107.7 11.6 %collective-permute-start.27 = (bf16[16,1152]{1,0:T(8,128)(2,1)S(1)}, bf16[16,1152]{1,0:T(8,128)(2,1)S(1)}, u32[]{:S(2)}, u32[]{:S(2)}) collective-permute-start(bf16[16,1152]{1,0:T(8,128)(2,1)S(1)} %get-tuple-element.59), channel_id=1, source_target_pairs={{0,0},{1,8},{2,16},{3,24},{4,4},{5,12},{6,20},{7,28},{8,1},{9,9},{... | collective-permute-start | bytes 110600 | tf_op jit(solution)/shard_map/ppermute | solution.py:530
  108.6 11.2 %collective-permute-start.28 = (bf16[16,1152]{1,0:T(8,128)(2,1)S(1)}, bf16[16,1152]{1,0:T(8,128)(2,1)S(1)}, u32[]{:S(2)}, u32[]{:S(2)}) collective-permute-start(bf16[16,1152]{1,0:T(8,128)(2,1)S(1)} %get-tuple-element.60), channel_id=1, source_target_pairs={{0,4},{1,12},{2,20},{3,28},{4,0},{5,8},{6,16},{7,24},{8,5},{9,13},... | collective-permute-start | bytes 110600 | tf_op jit(solution)/shard_map/ppermute | solution.py:530
  110.6 9.3 %collective-permute-start.38 = (bf16[768,256]{1,0:T(8,128)(2,1)S(1)}, bf16[768,256]{1,0:T(8,128)(2,1)S(1)}, u32[]{:S(2)}, u32[]{:S(2)}) collective-permute-start(bf16[768,256]{1,0:T(8,128)(2,1)S(1)} %collective-permute-done.34.refs_12_), channel_id=1, source_target_pairs={{0,1},{1,0},{2,3},{3,2},{4,5},{5,4},{6,7},{7,6},{8,9},{9,8},{10,11... | collective-permute-start | bytes 1179656 | tf_op jit(solution)/shard_map/ppermute | solution.py:26
  119.3 4.2 %collective-permute-start.39 = (bf16[768,256]{1,0:T(8,128)(2,1)S(1)}, bf16[768,256]{1,0:T(8,128)(2,1)S(1)}, u32[]{:S(2)}, u32[]{:S(2)}) collective-permute-start(bf16[768,256]{1,0:T(8,128)(2,1)S(1)} %collective-permute-done.35.refs_13_), channel_id=1, source_target_pairs={{0,1},{1,0},{2,3},{3,2},{4,5},{5,4},{6,7},{7,6},{8,9},{9,8},{10,11... | collective-permute-start | bytes 1179656 | tf_op jit(solution)/shard_map/ppermute | solution.py:26
  119.3 4.3 %collective-permute-start.40 = (bf16[768,256]{1,0:T(8,128)(2,1)S(1)}, bf16[768,256]{1,0:T(8,128)(2,1)S(1)}, u32[]{:S(2)}, u32[]{:S(2)}) collective-permute-start(bf16[768,256]{1,0:T(8,128)(2,1)S(1)} %collective-permute-done.36.refs_14_), channel_id=1, source_target_pairs={{0,1},{1,0},{2,3},{3,2},{4,5},{5,4},{6,7},{7,6},{8,9},{9,8},{10,11... | collective-permute-start | bytes 1179656 | tf_op jit(solution)/shard_map/ppermute | solution.py:26
  119.8 3.8 %collective-permute-start.41 = (bf16[768,256]{1,0:T(8,128)(2,1)S(1)}, bf16[768,256]{1,0:T(8,128)(2,1)S(1)}, u32[]{:S(2)}, u32[]{:S(2)}) collective-permute-start(bf16[768,256]{1,0:T(8,128)(2,1)S(1)} %collective-permute-done.37.refs_15_), channel_id=1, source_target_pairs={{0,1},{1,0},{2,3},{3,2},{4,5},{5,4},{6,7},{7,6},{8,9},{9,8},{10,11... | collective-permute-start | bytes 1179656 | tf_op jit(solution)/shard_map/ppermute | solution.py:26
  119.9 3.7 %collective-permute-start.29 = (bf16[32,1152]{1,0:T(8,128)(2,1)S(1)}, bf16[32,1152]{1,0:T(8,128)(2,1)S(1)}, u32[]{:S(2)}, u32[]{:S(2)}) collective-permute-start(bf16[32,1152]{1,0:T(8,128)(2,1)S(1)} %constant_dynamic-update-slice_fusion.refs_4_), channel_id=1, source_target_pairs={{0,1},{1,0},{2,3},{3,2},{4,5},{5,4},{6,7},{7,6},{8,9},{9,8},{10,11... | collective-permute-start | bytes 221192 | tf_op jit(solution)/shard_map/ppermute | solution.py:26
  120.4 5.9 %collective-permute-start.30 = (bf16[32,1152]{1,0:T(8,128)(2,1)S(1)}, bf16[32,1152]{1,0:T(8,128)(2,1)S(1)}, u32[]{:S(2)}, u32[]{:S(2)}) collective-permute-start(bf16[32,1152]{1,0:T(8,128)(2,1)S(1)} %constant_dynamic-update-slice_fusion.refs_4_), channel_id=1, source_target_pairs={{0,2},{1,3},{2,0},{3,1},{4,6},{5,7},{6,4},{7,5},{8,10},{9,11},{10,... | collective-permute-start | bytes 221192 | tf_op jit(solution)/shard_map/ppermute | solution.py:26
  123.5 4.3 %collective-permute-start.31 = (bf16[32,1152]{1,0:T(8,128)(2,1)S(1)}, bf16[32,1152]{1,0:T(8,128)(2,1)S(1)}, u32[]{:S(2)}, u32[]{:S(2)}) collective-permute-start(bf16[32,1152]{1,0:T(8,128)(2,1)S(1)} %constant_dynamic-update-slice_fusion.refs_4_), channel_id=1, source_target_pairs={{0,3},{1,2},{2,1},{3,0},{4,7},{5,6},{6,5},{7,4},{8,11},{9,10},{10,... | collective-permute-start | bytes 221192 | tf_op jit(solution)/shard_map/ppermute | solution.py:26
  130.8 3.6 %collective-permute-start.42 = (bf16[256,256]{1,0:T(8,128)(2,1)S(1)}, bf16[256,256]{1,0:T(8,128)(2,1)S(1)}, u32[]{:S(2)}, u32[]{:S(2)}) collective-permute-start(bf16[256,256]{1,0:T(8,128)(2,1)S(1)} %get-tuple-element.63), channel_id=1, source_target_pairs={{0,1},{1,0},{2,3},{3,2},{4,5},{5,4},{6,7},{7,6},{8,9},{9,8},{10,11... | collective-permute-start | bytes 393224 | tf_op jit(solution)/shard_map/ppermute | solution.py:26
  131.0 19.9 %collective-permute-start.45 = (bf16[512,256]{1,0:T(8,128)(2,1)S(1)}, bf16[512,256]{1,0:T(8,128)(2,1)S(1)}, u32[]{:S(2)}, u32[]{:S(2)}) collective-permute-start(bf16[512,256]{1,0:T(8,128)(2,1)S(1)} %get-tuple-element.67), channel_id=1, source_target_pairs={{0,1},{1,0},{2,3},{3,2},{4,5},{5,4},{6,7},{7,6},{8,9},{9,8},{10,11... | collective-permute-start | bytes 786440 | tf_op jit(solution)/shard_map/ppermute | solution.py:26
  131.4 19.6 %collective-permute-start.46 = (bf16[512,256]{1,0:T(8,128)(2,1)S(1)}, bf16[512,256]{1,0:T(8,128)(2,1)S(1)}, u32[]{:S(2)}, u32[]{:S(2)}) collective-permute-start(bf16[512,256]{1,0:T(8,128)(2,1)S(1)} %get-tuple-element.68), channel_id=1, source_target_pairs={{0,2},{1,3},{2,0},{3,1},{4,6},{5,7},{6,4},{7,5},{8,10},{9,11},{10,... | collective-permute-start | bytes 786440 | tf_op jit(solution)/shard_map/ppermute | solution.py:26
  132.6 18.3 %collective-permute-start.47 = (bf16[512,256]{1,0:T(8,128)(2,1)S(1)}, bf16[512,256]{1,0:T(8,128)(2,1)S(1)}, u32[]{:S(2)}, u32[]{:S(2)}) collective-permute-start(bf16[512,256]{1,0:T(8,128)(2,1)S(1)} %get-tuple-element.69), channel_id=1, source_target_pairs={{0,3},{1,2},{2,1},{3,0},{4,7},{5,6},{6,5},{7,4},{8,11},{9,10},{10,... | collective-permute-start | bytes 786440 | tf_op jit(solution)/shard_map/ppermute | solution.py:26
  132.9 16.1 %collective-permute-start.43 = (bf16[256,256]{1,0:T(8,128)(2,1)S(1)}, bf16[256,256]{1,0:T(8,128)(2,1)S(1)}, u32[]{:S(2)}, u32[]{:S(2)}) collective-permute-start(bf16[256,256]{1,0:T(8,128)(2,1)S(1)} %get-tuple-element.64), channel_id=1, source_target_pairs={{0,2},{1,3},{2,0},{3,1},{4,6},{5,7},{6,4},{7,5},{8,10},{9,11},{10,... | collective-permute-start | bytes 393224 | tf_op jit(solution)/shard_map/ppermute | solution.py:26
  134.4 15.7 %collective-permute-start.44 = (bf16[256,256]{1,0:T(8,128)(2,1)S(1)}, bf16[256,256]{1,0:T(8,128)(2,1)S(1)}, u32[]{:S(2)}, u32[]{:S(2)}) collective-permute-start(bf16[256,256]{1,0:T(8,128)(2,1)S(1)} %get-tuple-element.65), channel_id=1, source_target_pairs={{0,3},{1,2},{2,1},{3,0},{4,7},{5,6},{6,5},{7,4},{8,11},{9,10},{10,... | collective-permute-start | bytes 393224 | tf_op jit(solution)/shard_map/ppermute | solution.py:26
  (23 other events, 170.6 us)

commit v3 on v2

--- a/solution.py
+++ b/solution.py
@@ -18,7 +18,7 @@
 F32 = jnp.float32
 VMEM = pl.BlockSpec(memory_space=pltpu.VMEM)
 SMEM = pl.BlockSpec(memory_space=pltpu.SMEM)
-ANY = pl.BlockSpec(memory_space=pl.ANY)
+HBM = pl.BlockSpec(memory_space=pltpu.HBM)
 
 
 def swap(value, axis, mask):
@@ -193,24 +193,10 @@
     )(owner, *values)
 
 
-def part_rows(source, rows, put):
-    step = 2 * LANES
+def parted_kernel(ends_ref, out_ref):
+    full = ends_ref.shape[0]
     for side in range(2):
-        lane = lax.broadcasted_iota(jnp.int32, (LANES, step), 1)
-        row = lax.broadcasted_iota(jnp.int32, (LANES, step), 0)
-        hot = jnp.where(lane == 2 * row + side, 1.0, 0.0).astype(BF)
-        for n in range(rows // step):
-            part = jnp.dot(hot, source[n * step : (n + 1) * step, :], preferred_element_type=F32)
-            put(side, n * LANES, part.astype(BF))
-
-
-def parted_kernel(ends_ref, out_ref):
-    half = ends_ref.shape[0] // 2
-
-    def put(side, at, value):
-        out_ref[side * half + at : side * half + at + LANES, :] = value
-
-    part_rows(ends_ref, ends_ref.shape[0], put)
+        out_ref[side * full : (side + 1) * full, :] = ends_ref[:, side, :]
 
 
 def pieces_kernel(unit, in_ref, ends_ref, out_ref, node_ref, last_ref, e_piece, n_piece, ends, sems):
@@ -219,7 +205,7 @@
     at = pl.multiple_of(a * unit, unit)
     below = pl.multiple_of(full + a * unit, unit)
     copies = [
-        (ends_ref.at[pl.ds(pl.multiple_of(a * 2 * unit, 2 * unit), 2 * unit)], ends),
+        (ends_ref.at[pl.ds(at, unit)], ends),
         (in_ref.at[pl.ds(at, unit)], e_piece.at[pl.ds(0, unit)]),
         (out_ref.at[:, pl.ds(at, unit)], e_piece.at[pl.ds(3 * unit, unit)]),
         (node_ref.at[pl.ds(at, unit)], n_piece.at[pl.ds(0, unit)]),
@@ -230,12 +216,8 @@
     for copy in copies:
         copy.start()
     copies[0].wait()
-
-    def put(side, row, value):
-        base = (1 + side) * unit + row
-        e_piece[base : base + LANES, :] = value
-
-    part_rows(ends, 2 * unit, put)
+    for side in range(2):
+        e_piece[(1 + side) * unit : (2 + side) * unit, :] = ends[:, side, :]
     for copy in copies[1:]:
         copy.wait()
 
@@ -257,10 +239,16 @@
     return pl.ds(pl.multiple_of(quarter * unit, unit), unit)
 
 
+def far_parts(pieces, unit):
+    parts = [[piece.at[pl.ds(n * unit, unit)] for n in range(piece.shape[0] // unit)] for piece in pieces]
+    return parts[:-2] + [parts[-2] + parts[-1]]
+
+
 def edge_kernel(pairs, groups, direct, owner_ref, segrow_ref, ids_ref, *refs):
     e_refs, refs = refs[:pairs], refs[pairs:]
     s_refs, refs = refs[:pairs], refs[pairs:]
-    whole, far, refs = (refs[:3], refs[3:6]), (refs[6:10], refs[10:14]), refs[14:]
+    whole, far, refs = (refs[:3], refs[3:6]), (refs[6:11], refs[11:16]), refs[16:]
+    far = [far_parts(pieces, refs[0].shape[1]) for pieces in far]
     outs, refs = refs[:pairs], refs[pairs:]
     sum_refs, refs = refs[:groups], refs[groups:]
     e_all, s_all, r_all, hidden, mixed_all, new_all, wide = refs
@@ -293,7 +281,7 @@
             receivers = None
             for r, piece in enumerate(far[k - 2]):
                 part = r_all[:, far_spot(r, local)]
-                part = jnp.dot(part, piece[2 * local : 3 * local, :], preferred_element_type=F32)
+                part = jnp.dot(part, piece[2][...], preferred_element_type=F32)
                 receivers = part if receivers is None else receivers + part
         receivers = receivers.astype(BF)
         for g in range(groups):
@@ -305,8 +293,8 @@
             else:
                 for r, piece in enumerate(far[k - 2]):
                     spot = far_spot(r, local)
-                    pre += jnp.dot(e_all[at, spot], piece[:local, :], preferred_element_type=F32)
-                    pre += jnp.dot(s_all[at, spot], piece[local : 2 * local, :], preferred_element_type=F32)
+                    pre += jnp.dot(e_all[at, spot], piece[0][...], preferred_element_type=F32)
+                    pre += jnp.dot(s_all[at, spot], piece[1][...], preferred_element_type=F32)
             hidden[at, k * local : (k + 1) * local] = silu(pre + bias[k]).astype(BF)
     for g in range(groups):
         at = slice(g * tile, (g + 1) * tile)
@@ -317,7 +305,7 @@
             total = None
             for near, (_, _, w_out), behind, pieces in zip(first, whole, last, far):
                 part = jnp.dot(near, w_out[:, spot], preferred_element_type=F32)
-                part += jnp.dot(behind, pieces[r][3 * local :, :], preferred_element_type=F32)
+                part += jnp.dot(behind, pieces[r][3][...], preferred_element_type=F32)
                 total = part if total is None else total + part
             mixed_all[at, spot] = total
         live = segments[g][:, :1] < RT
@@ -457,32 +445,33 @@
         picked = halo_rows(False, send_list.reshape(-1, 2 * LANES), node_latents)
         table = [lax.all_to_all(jnp.concatenate(picked, axis=0), "patch", 0, 0, tiled=True)]
 
-    ends = w_endpoints.reshape(2 * full, local)
     w_nodes = w_node_in.reshape(2 * full, local)
     e_piece, n_piece = pl.pallas_call(
         functools.partial(pieces_kernel, local),
-        compiler_params=grant(12),
-        in_specs=[ANY] * 5,
+        in_specs=[HBM] * 5,
         out_specs=[VMEM] * 2,
         out_shape=[jax.ShapeDtypeStruct((4 * local, local), BF), jax.ShapeDtypeStruct((3 * local, local), BF)],
-        scratch_shapes=[pltpu.VMEM((2 * local, local), BF), pltpu.SemaphoreType.DMA((6,))],
-    )(w_edge_in, ends, w_edge_out, w_nodes, w_node_out)
+        scratch_shapes=[pltpu.VMEM((local, 2, local), BF), pltpu.SemaphoreType.DMA((6,))],
+    )(w_edge_in, w_endpoints, w_edge_out, w_nodes, w_node_out)
     parted = pl.pallas_call(
         parted_kernel,
         compiler_params=grant(12),
         in_specs=[VMEM],
         out_specs=VMEM,
         out_shape=jax.ShapeDtypeStruct((2 * full, local), BF),
-    )(ends)
-
-    def gather_slices(own, piece):
+    )(w_endpoints)
+
+    def gather_slices(own, piece, cut=None):
         parts = list(own) + [swap(w, "pair", 1) for w in own]
         near = swap(piece, "pair", 2)
         side = swap(near, "patch", 1)
-        far = [near, side, swap(near, "patch", 2), swap(side, "patch", 2)]
+        ahead = swap(near, "patch", 2)
+        far = [near, side, ahead, swap(side if cut is None else side[:cut], "patch", 2)]
+        if cut is not None:
+            far.append(swap(ahead[cut:], "patch", 1))
         return parts + far + [swap(w, "pair", 1) for w in far]
 
-    e_weights = gather_slices((w_edge_in, parted, w_edge_out), e_piece)
+    e_weights = gather_slices((w_edge_in, parted, w_edge_out), e_piece, 2 * local)
     n_weights = gather_slices((w_nodes, w_node_out), n_piece)
 
     e_parts = to_pairs(split(block_owner, tile, mine, direct, pairs, edge_latents, edge_bias, edge_gain, edge_shift))

time: 153 us -> 161 us (1.052)
  starting transfers between devices: 40.4 us -> 51.5 us
  waiting for transfers between devices: 86.9 us -> 81.3 us
  Pallas kernels: 19.8 us -> 24.1 us
  local copies, waits for them, and re-layouts: 3.92 us -> 2.1 us
    ppermute x46 -> x48, starting transfers between devices: 39.1 us -> 49.8 us  [swap(): return lax.ppermute(value, axis, [(i, i ^ mask) for i in range(size)])]
    ppermute x46 -> x48, waiting for transfers between devices: 86.9 us -> 81.3 us  [swap(): return lax.ppermute(value, axis, [(i, i ^ mask) for i in range(size)])]
    pallas_call x1, Pallas kernels: 0.44 us -> 2.17 us  [layer(): pl.pallas_call(parted_kernel, compiler_params=grant(12), in_specs=[VMEM],...]
    pallas_call x1, Pallas kernels: 0.88 us -> 2.56 us  [layer(): pl.pallas_call(functools.partial(pieces_kernel, local), in_specs=[HBM] *...]
  transfers between devices with their start and end apart: 48 -> 50, of which waited for: 17 -> 17; matrix products, arithmetic and copies ran while one was open for 1% -> 0% of each run, Pallas kernels for 8% -> 10%
where the time goes in v3:
time: 161 us
  waiting for transfers between devices  81.3 us (50%)
  starting transfers between devices  51.5 us (32%)
  Pallas kernels  24.1 us (15%)
  local copies, waits for them, and re-layouts  2.1 us (1%)
  between operations  1.66 us (1%)
    ppermute x48, waiting for transfers between devices, swap(): return lax.ppermute(value, axis, [(i, i ^ mask) for i in range(size)])  81.3 us
    ppermute x48, starting transfers between devices, swap(): return lax.ppermute(value, axis, [(i, i ^ mask) for i in range(size)])  49.8 us
    pallas_call x1, Pallas kernels, layer(): pl.pallas_call(functools.partial(edge_kernel, pairs, mine, direct), compi...  6.3 us
    pallas_call x1, Pallas kernels, sender_rows(): pl.pallas_call(functools.partial(sender_kernel, by_swap, direct, pairs, h...  3.76 us
  transfers between devices with their start and end apart: 50, of which 17 were waited for; matrix products, arithmetic and copies ran while one was open for 0% of the time, Pallas kernels for 10%

profile of v3, /device:TPU:0, one launch (start us, length us, event | category | flops | bytes accessed | tf_op | source)
XLA Modules:
  0.0 160.7 jit_solution(16667868653886138111)
XLA Ops:
  0.7 3.2 %shard_map.186 = (bf16[256,256]{1,0:T(8,128)(2,1)}, bf16[256,256]{1,0:T(8,128)(2,1)}, bf16[256,256]{1,0:T(8,128)(2,1)}, bf16[256,256]{1,0:T(8,128)(2,1)}, bf16[2...) custom-call(s32[8,256]{1,0:T(8,128)} %bitcast.11, ...), custom_call_target="tpu_custom_call" | custom-call | flops 1073741824 | bytes 262144 | tf_op jit(solution)/shard_map/pallas_call | solution.py:68
  3.9 3.0 %collective-permute-start.3 = (bf16[256,256]{1,0:T(8,128)(2,1)}, bf16[256,256]{1,0:T(8,128)(2,1)S(1)}, u32[]{:S(2)}, u32[]{:S(2)}) collective-permute-start(bf16[256,256]{1,0:T(8,128)(2,1)} %get-tuple-element.41), channel_id=1, source_target_pairs={{0,4},{4,0},{8,12},{12,8},{16,20},{20,16},{24,28},{28,24},{1,5},{5... | collective-permute-start | bytes 393224 | tf_op jit(solution)/shard_map/ppermute | solution.py:26
  6.8 1.6 collective-permute-start.4
  8.4 3.0 %collective-permute-start.6 = (bf16[256,256]{1,0:T(8,128)(2,1)}, bf16[256,256]{1,0:T(8,128)(2,1)S(1)}, u32[]{:S(2)}, u32[]{:S(2)}) collective-permute-start(bf16[256,256]{1,0:T(8,128)(2,1)} %get-tuple-element.44), channel_id=1, source_target_pairs={{0,16},{4,20},{8,24},{12,28},{16,0},{20,4},{24,8},{28,12},{1,17},{... | collective-permute-start | bytes 393224 | tf_op jit(solution)/shard_map/ppermute | solution.py:26
  11.4 1.3 collective-permute-start.7
  12.7 3.6 %collective-permute-start.8 = (bf16[256,256]{1,0:T(8,128)(2,1)}, bf16[256,256]{1,0:T(8,128)(2,1)}, u32[]{:S(2)}, u32[]{:S(2)}) collective-permute-start(bf16[256,256]{1,0:T(8,128)(2,1)} %get-tuple-element.46), channel_id=1, source_target_pairs={{0,24},{4,28},{8,16},{12,20},{16,8},{20,12},{24,0},{28,4},{1,25},{... | collective-permute-start | bytes 393224 | tf_op jit(solution)/shard_map/ppermute | solution.py:26
  17.0 0.6 copy-done.9
  18.4 1.7 %collective-permute-start.1 = (bf16[272,256]{1,0:T(8,128)(2,1)S(1)}, bf16[272,256]{1,0:T(8,128)(2,1)S(1)}, u32[]{:S(2)}, u32[]{:S(2)}) collective-permute-start(bf16[272,256]{1,0:T(8,128)(2,1)S(1)} %get-tuple-element.38), channel_id=1, source_target_pairs={{0,2},{1,3},{2,0},{3,1},{4,6},{5,7},{6,4},{7,5},{8,10},{9,11},{10,... | collective-permute-start | bytes 417800 | tf_op jit(solution)/shard_map/ppermute | solution.py:26
  20.1 9.9 %collective-permute-start.9 = (bf16[256,256]{1,0:T(8,128)(2,1)}, bf16[256,256]{1,0:T(8,128)(2,1)}, u32[]{:S(2)}, u32[]{:S(2)}) collective-permute-start(bf16[256,256]{1,0:T(8,128)(2,1)} %get-tuple-element.47), channel_id=1, source_target_pairs={{0,28},{4,24},{8,20},{12,16},{16,12},{20,8},{24,4},{28,0},{1,29},{... | collective-permute-start | bytes 393224 | tf_op jit(solution)/shard_map/ppermute | solution.py:26
  31.4 0.6 copy-done.19
  32.1 2.6 %shard_map.190 = (bf16[1024,256]{1,0:T(8,128)(2,1)}, bf16[768,256]{1,0:T(8,128)(2,1)}) custom-call(bf16[1024,256]{1,0:T(8,128)(2,1)} %refs_8_.1, bf16[1024,2,256]{2,1,0:T(2,128)(2,1)} %ends_ref.3, bf16[256,1024]{1,0:T(8,128)(2,1)} %refs_10_.1, bf16[2048,256]{1,0:T(8,128)(2,1)} %bitcast.8, bf16[256,1024]{1,0:T(8,128)(2,1)} %refs_9_.1), custom_call_target="tpu_custom_call" | custom-call | tf_op jit(solution)/shard_map/pallas_call | solution.py:449
  34.7 1.6 collective-permute-start.36
  36.8 1.5 collective-permute-start.11
  38.4 3.8 %shard_map.187 = (bf16[544,256]{1,0:T(8,128)(2,1)S(1)}, bf16[544,256]{1,0:T(8,128)(2,1)S(1)}, bf16[544,256]{1,0:T(8,128)(2,1)S(1)}, bf16[544,256]{1,0:T(8,128)(2...) custom-call(s32[8]{0:T(128)S(1)} %copy-done.8, s32[8,256]{1,0:T(8,128)S(1)} %copy-done.21, ...), custom_call_target="tpu_custom_call" | custom-call | flops 2281701376 | bytes 2228224 | tf_op jit(solution)/shard_map/pallas_call | solution.py:129
  42.2 0.7 collective-permute-start.13
  42.8 21.1 %collective-permute-done.11.refs_2_ = bf16[528,256]{1,0:T(8,128)(2,1)S(1)} collective-permute-done((bf16[528,256]{1,0:T(8,128)(2,1)S(1)}, bf16[528,256]{1,0:T(8,128)(2,1)S(1)}, u32[]{:S(2)}, u32[]{:S(2)}) %collective-permute-start.11) | collective-permute-done | bytes 270368 | tf_op jit(solution)/shard_map/ppermute | solution.py:26
  63.9 1.5 collective-permute-start.14
  65.5 3.3 %collective-permute-done.12.refs_3_ = bf16[528,256]{1,0:T(8,128)(2,1)S(1)} collective-permute-done((bf16[528,256]{1,0:T(8,128)(2,1)S(1)}, bf16[528,256]{1,0:T(8,128)(2,1)S(1)}, u32[]{:S(2)}, u32[]{:S(2)}) %collective-permute-start.12) | collective-permute-done | bytes 270368 | tf_op jit(solution)/shard_map/ppermute | solution.py:26
  68.8 0.8 collective-permute-start.16
  69.7 1.6 collective-permute-start.15
  71.2 2.2 %shard_map.189.refs_9_ = bf16[2048,256]{1,0:T(8,128)(2,1)S(1)} custom-call(bf16[1024,2,256]{2,1,0:T(2,128)(2,1)S(1)} %copy-done), custom_call_target="tpu_custom_call" | custom-call | tf_op jit(solution)/shard_map/pallas_call | solution.py:456
  73.4 2.3 %collective-permute-done.14.refs_6_ = bf16[544,256]{1,0:T(8,128)(2,1)S(1)} collective-permute-done((bf16[544,256]{1,0:T(8,128)(2,1)S(1)}, bf16[544,256]{1,0:T(8,128)(2,1)S(1)}, u32[]{:S(2)}, u32[]{:S(2)}) %collective-permute-start.14) | collective-permute-done | bytes 278560 | tf_op jit(solution)/shard_map/ppermute | solution.py:26
  75.7 1.0 collective-permute-start.20
  76.7 4.0 %collective-permute-done.15.refs_7_ = bf16[544,256]{1,0:T(8,128)(2,1)S(1)} collective-permute-done((bf16[544,256]{1,0:T(8,128)(2,1)S(1)}, bf16[544,256]{1,0:T(8,128)(2,1)S(1)}, u32[]{:S(2)}, u32[]{:S(2)}) %collective-permute-start.15) | collective-permute-done | bytes 278560 | tf_op jit(solution)/shard_map/ppermute | solution.py:26
  81.3 1.0 collective-permute-start.37
  82.3 8.2 %collective-permute-done.20.refs_15_ = bf16[1024,256]{1,0:T(8,128)(2,1)S(1)} collective-permute-done((bf16[1024,256]{1,0:T(8,128)(2,1)S(1)}, bf16[1024,256]{1,0:T(8,128)(2,1)S(1)}, u32[]{:S(2)}, u32[]{:S(2)}) %collective-permute-start.20) | collective-permute-done | bytes 524320 | tf_op jit(solution)/shard_map/ppermute | solution.py:26
  90.5 4.6 %collective-permute-done.21.refs_16_ = bf16[1024,256]{1,0:T(8,128)(2,1)S(1)} collective-permute-done((bf16[1024,256]{1,0:T(8,128)(2,1)S(1)}, bf16[1024,256]{1,0:T(8,128)(2,1)S(1)}, u32[]{:S(2)}, u32[]{:S(2)}) %collective-permute-start.21) | collective-permute-done | bytes 524320 | tf_op jit(solution)/shard_map/ppermute | solution.py:26
  95.1 3.3 %collective-permute-done.37.refs_13_ = bf16[768,256]{1,0:T(8,128)(2,1)S(1)} collective-permute-done((bf16[768,256]{1,0:T(8,128)(2,1)S(1)}, bf16[768,256]{1,0:T(8,128)(2,1)S(1)}, u32[]{:S(2)}, u32[]{:S(2)}) %collective-permute-start.37) | collective-permute-done | bytes 393248 | tf_op jit(solution)/shard_map/ppermute | solution.py:26
  98.5 1.1 collective-permute-start.23
  99.6 6.8 %collective-permute-done.22.refs_17_ = bf16[512,256]{1,0:T(8,128)(2,1)S(1)} collective-permute-done((bf16[512,256]{1,0:T(8,128)(2,1)S(1)}, bf16[512,256]{1,0:T(8,128)(2,1)S(1)}, u32[]{:S(2)}, u32[]{:S(2)}) %collective-permute-start.22) | collective-permute-done | bytes 262176 | tf_op jit(solution)/shard_map/ppermute | solution.py:26
  107.4 1.4 collective-permute-start.38
  109.4 0.7 collective-permute-start.2
  110.1 6.3 %shard_map.191 = (bf16[512,256]{1,0:T(8,128)(2,1)S(1)}, bf16[512,256]{1,0:T(8,128)(2,1)S(1)}, bf16[512,256]{1,0:T(8,128)(2,1)S(1)}, bf16[512,256]{1,0:T(8,128)(2...) custom-call(s32[8]{0:T(128)S(1)} %copy-done.8, s32[8,256]{1,0:T(8,128)S(1)} %get-tuple-element.48.segrow_ref, ...), custom_call_target="tpu_custom_call" | custom-call | flops 3221225472 | bytes 10485760 | tf_op jit(solution)/shard_map/pallas_call | solution.py:482
  116.5 0.7 collective-permute-start.29
  117.1 1.1 collective-permute-start.30
  118.2 1.1 collective-permute-done.38.refs_14_
  119.4 2.2 %collective-permute-start.40 = (bf16[768,256]{1,0:T(8,128)(2,1)S(1)}, bf16[768,256]{1,0:T(8,128)(2,1)S(1)}, u32[]{:S(2)}, u32[]{:S(2)}) collective-permute-start(bf16[768,256]{1,0:T(8,128)(2,1)S(1)} %collective-permute-done.36.refs_12_), channel_id=1, source_target_pairs={{0,1},{1,0},{2,3},{3,2},{4,5},{5,4},{6,7},{7,6},{8,9},{9,8},{10,11... | collective-permute-start | bytes 1179656 | tf_op jit(solution)/shard_map/ppermute | solution.py:26
  121.6 6.2 %collective-permute-done.39.refs_15_ = bf16[768,256]{1,0:T(8,128)(2,1)S(1)} collective-permute-done((bf16[768,256]{1,0:T(8,128)(2,1)S(1)}, bf16[768,256]{1,0:T(8,128)(2,1)S(1)}, u32[]{:S(2)}, u32[]{:S(2)}) %collective-permute-start.39) | collective-permute-done | bytes 393248 | tf_op jit(solution)/shard_map/ppermute | solution.py:26
  128.9 2.7 %collective-permute-start.32 = (bf16[32,1152]{1,0:T(8,128)(2,1)S(1)}, bf16[32,1152]{1,0:T(8,128)(2,1)S(1)}, u32[]{:S(2)}, u32[]{:S(2)}) collective-permute-start(bf16[32,1152]{1,0:T(8,128)(2,1)S(1)} %constant_dynamic-update-slice_fusion.refs_4_), channel_id=1, source_target_pairs={{0,2},{1,3},{2,0},{3,1},{4,6},{5,7},{6,4},{7,5},{8,10},{9,11},{10,... | collective-permute-start | bytes 221192 | tf_op jit(solution)/shard_map/ppermute | solution.py:26
  131.7 2.7 %collective-permute-done.32.refs_6_ = bf16[32,1152]{1,0:T(8,128)(2,1)S(1)} collective-permute-done((bf16[32,1152]{1,0:T(8,128)(2,1)S(1)}, bf16[32,1152]{1,0:T(8,128)(2,1)S(1)}, u32[]{:S(2)}, u32[]{:S(2)}) %collective-permute-start.32) | collective-permute-done | bytes 73760 | tf_op jit(solution)/shard_map/ppermute | solution.py:26
  134.4 1.4 collective-permute-done.33.refs_7_
  135.8 3.0 %shard_map.192 = (bf16[256,256]{1,0:T(8,128)(2,1)S(1)}, bf16[256,256]{1,0:T(8,128)(2,1)S(1)}, bf16[256,256]{1,0:T(8,128)(2,1)S(1)}, bf16[256,256]{1,0:T(8,128)(2,1)S(1)}) custom-call(s32[1]{0:T(128)S(6)} %copy.21.owner_ref.count_ref, s32[8,256]{1,0:T(8,128)S(1)} %bitcast.12, bf16[272,256]{1,0:T(8,128)(2,1)S(1)} %get-tuple-element.36.refs_0_, ...), custom_call_target="tpu_custom_call" | custom-call | flops 1610612736 | bytes 8388608 | tf_op jit(solution)/shard_map/pallas_call | solution.py:535
  139.4 1.4 collective-permute-start.48
  140.9 1.6 %collective-permute-start.45 = (bf16[256,256]{1,0:T(8,128)(2,1)S(1)}, bf16[256,256]{1,0:T(8,128)(2,1)S(1)}, u32[]{:S(2)}, u32[]{:S(2)}) collective-permute-start(bf16[256,256]{1,0:T(8,128)(2,1)S(1)} %get-tuple-element.64), channel_id=1, source_target_pairs={{0,2},{1,3},{2,0},{3,1},{4,6},{5,7},{6,4},{7,5},{8,10},{9,11},{10,... | collective-permute-start | bytes 393224 | tf_op jit(solution)/shard_map/ppermute | solution.py:26
  142.9 14.1 %collective-permute-done.45.refs_2_ = bf16[256,256]{1,0:T(8,128)(2,1)S(1)} collective-permute-done((bf16[256,256]{1,0:T(8,128)(2,1)S(1)}, bf16[256,256]{1,0:T(8,128)(2,1)S(1)}, u32[]{:S(2)}, u32[]{:S(2)}) %collective-permute-start.45) | collective-permute-done | bytes 131104 | tf_op jit(solution)/shard_map/ppermute | solution.py:26
  157.0 1.2 collective-permute-done.46.refs_3_
  158.2 0.8 shard_map.193
  159.0 1.7 %shard_map.194 = bf16[2048,256]{1,0:T(8,128)(2,1)} custom-call(s32[8]{0:T(128)S(1)} %copy-done.8, bf16[512,256]{1,0:T(8,128)(2,1)S(1)} %get-tuple-element.66.refs_0_, bf16[512,256]{1,0:T(8,128)(2,1)S(1)} %collective-permute-done.47.refs_1_, bf16[512,256]{1,0:T(8,128)(2,1)S(1)} %collective-permute-done.48.refs_2_, ...), custom_call_target="tpu_custom_call" | custom-call | tf_op jit(solution)/shard_map/pallas_call | solution.py:187
  (114 shorter events, 7.5 us)
Async XLA Ops:
  3.9 8.8 %collective-permute-start.3 = (bf16[256,256]{1,0:T(8,128)(2,1)}, bf16[256,256]{1,0:T(8,128)(2,1)S(1)}, u32[]{:S(2)}, u32[]{:S(2)}) collective-permute-start(bf16[256,256]{1,0:T(8,128)(2,1)} %get-tuple-element.41), channel_id=1, source_target_pairs={{0,4},{4,0},{8,12},{12,8},{16,20},{20,16},{24,28},{28,24},{1,5},{5... | collective-permute-start | bytes 393224 | tf_op jit(solution)/shard_map/ppermute | solution.py:26
  6.8 11.0 %collective-permute-start.4 = (bf16[256,256]{1,0:T(8,128)(2,1)}, bf16[256,256]{1,0:T(8,128)(2,1)S(1)}, u32[]{:S(2)}, u32[]{:S(2)}) collective-permute-start(bf16[256,256]{1,0:T(8,128)(2,1)} %get-tuple-element.42), channel_id=1, source_target_pairs={{0,8},{4,12},{8,0},{12,4},{16,24},{20,28},{24,16},{28,20},{1,9},{5... | collective-permute-start | bytes 393224 | tf_op jit(solution)/shard_map/ppermute | solution.py:26
  8.4 10.0 %collective-permute-start.5 = (bf16[256,256]{1,0:T(8,128)(2,1)}, bf16[256,256]{1,0:T(8,128)(2,1)S(1)}, u32[]{:S(2)}, u32[]{:S(2)}) collective-permute-start(bf16[256,256]{1,0:T(8,128)(2,1)} %get-tuple-element.43), channel_id=1, source_target_pairs={{0,12},{4,8},{8,4},{12,0},{16,28},{20,24},{24,20},{28,16},{1,13},{... | collective-permute-start | bytes 393224 | tf_op jit(solution)/shard_map/ppermute | solution.py:26
  8.4 11.7 %collective-permute-start.6 = (bf16[256,256]{1,0:T(8,128)(2,1)}, bf16[256,256]{1,0:T(8,128)(2,1)S(1)}, u32[]{:S(2)}, u32[]{:S(2)}) collective-permute-start(bf16[256,256]{1,0:T(8,128)(2,1)} %get-tuple-element.44), channel_id=1, source_target_pairs={{0,16},{4,20},{8,24},{12,28},{16,0},{20,4},{24,8},{28,12},{1,17},{... | collective-permute-start | bytes 393224 | tf_op jit(solution)/shard_map/ppermute | solution.py:26
  11.4 20.0 %collective-permute-start.7 = (bf16[256,256]{1,0:T(8,128)(2,1)}, bf16[256,256]{1,0:T(8,128)(2,1)S(1)}, u32[]{:S(2)}, u32[]{:S(2)}) collective-permute-start(bf16[256,256]{1,0:T(8,128)(2,1)} %get-tuple-element.45), channel_id=1, source_target_pairs={{0,20},{4,16},{8,28},{12,24},{16,4},{20,0},{24,12},{28,8},{1,21},{... | collective-permute-start | bytes 393224 | tf_op jit(solution)/shard_map/ppermute | solution.py:26
  12.7 22.0 %collective-permute-start.8 = (bf16[256,256]{1,0:T(8,128)(2,1)}, bf16[256,256]{1,0:T(8,128)(2,1)}, u32[]{:S(2)}, u32[]{:S(2)}) collective-permute-start(bf16[256,256]{1,0:T(8,128)(2,1)} %get-tuple-element.46), channel_id=1, source_target_pairs={{0,24},{4,28},{8,16},{12,20},{16,8},{20,12},{24,0},{28,4},{1,25},{... | collective-permute-start | bytes 393224 | tf_op jit(solution)/shard_map/ppermute | solution.py:26
  17.8 18.9 %collective-permute-start = (bf16[272,256]{1,0:T(8,128)(2,1)S(1)}, bf16[272,256]{1,0:T(8,128)(2,1)S(1)}, u32[]{:S(2)}, u32[]{:S(2)}) collective-permute-start(bf16[272,256]{1,0:T(8,128)(2,1)S(1)} %get-tuple-element.37), channel_id=1, source_target_pairs={{0,1},{1,0},{2,3},{3,2},{4,5},{5,4},{6,7},{7,6},{8,9},{9,8},{10,11... | collective-permute-start | bytes 417800 | tf_op jit(solution)/shard_map/ppermute | solution.py:26
  18.4 19.8 %collective-permute-start.1 = (bf16[272,256]{1,0:T(8,128)(2,1)S(1)}, bf16[272,256]{1,0:T(8,128)(2,1)S(1)}, u32[]{:S(2)}, u32[]{:S(2)}) collective-permute-start(bf16[272,256]{1,0:T(8,128)(2,1)S(1)} %get-tuple-element.38), channel_id=1, source_target_pairs={{0,2},{1,3},{2,0},{3,1},{4,6},{5,7},{6,4},{7,5},{8,10},{9,11},{10,... | collective-permute-start | bytes 417800 | tf_op jit(solution)/shard_map/ppermute | solution.py:26
  20.1 16.1 %collective-permute-start.9 = (bf16[256,256]{1,0:T(8,128)(2,1)}, bf16[256,256]{1,0:T(8,128)(2,1)}, u32[]{:S(2)}, u32[]{:S(2)}) collective-permute-start(bf16[256,256]{1,0:T(8,128)(2,1)} %get-tuple-element.47), channel_id=1, source_target_pairs={{0,28},{4,24},{8,20},{12,16},{16,12},{20,8},{24,4},{28,0},{1,29},{... | collective-permute-start | bytes 393224 | tf_op jit(solution)/shard_map/ppermute | solution.py:26
  32.0 10.1 %collective-permute-start.10 = (bf16[528,256]{1,0:T(8,128)(2,1)S(1)}, bf16[528,256]{1,0:T(8,128)(2,1)S(1)}, u32[]{:S(2)}, u32[]{:S(2)}) collective-permute-start(bf16[528,256]{1,0:T(8,128)(2,1)S(1)} %get-tuple-element.51), channel_id=1, source_target_pairs={{0,1},{1,0},{2,3},{3,2},{4,5},{5,4},{6,7},{7,6},{8,9},{9,8},{10,11... | collective-permute-start | bytes 811016 | tf_op jit(solution)/shard_map/ppermute | solution.py:26
  34.7 34.9 %collective-permute-start.36 = (bf16[768,256]{1,0:T(8,128)(2,1)}, bf16[768,256]{1,0:T(8,128)(2,1)S(1)}, u32[]{:S(2)}, u32[]{:S(2)}) collective-permute-start(bf16[768,256]{1,0:T(8,128)(2,1)} %get-tuple-element.61), channel_id=1, source_target_pairs={{0,2},{1,3},{2,0},{3,1},{4,6},{5,7},{6,4},{7,5},{8,10},{9,11},{10,... | collective-permute-start | bytes 1179656 | tf_op jit(solution)/shard_map/ppermute | solution.py:26
  36.2 39.5 %collective-permute-start.19 = (bf16[1024,256]{1,0:T(8,128)(2,1)}, bf16[1024,256]{1,0:T(8,128)(2,1)S(1)}, u32[]{:S(2)}, u32[]{:S(2)}) collective-permute-start(bf16[1024,256]{1,0:T(8,128)(2,1)} %get-tuple-element.58), channel_id=1, source_target_pairs={{0,2},{1,3},{2,0},{3,1},{4,6},{5,7},{6,4},{7,5},{8,10},{9,11},{10,... | collective-permute-start | bytes 1572872 | tf_op jit(solution)/shard_map/ppermute | solution.py:26
  36.8 27.2 %collective-permute-start.11 = (bf16[528,256]{1,0:T(8,128)(2,1)S(1)}, bf16[528,256]{1,0:T(8,128)(2,1)S(1)}, u32[]{:S(2)}, u32[]{:S(2)}) collective-permute-start(bf16[528,256]{1,0:T(8,128)(2,1)S(1)} %get-tuple-element.52), channel_id=1, source_target_pairs={{0,2},{1,3},{2,0},{3,1},{4,6},{5,7},{6,4},{7,5},{8,10},{9,11},{10,... | collective-permute-start | bytes 811016 | tf_op jit(solution)/shard_map/ppermute | solution.py:26
  38.3 30.5 %collective-permute-start.12 = (bf16[528,256]{1,0:T(8,128)(2,1)S(1)}, bf16[528,256]{1,0:T(8,128)(2,1)S(1)}, u32[]{:S(2)}, u32[]{:S(2)}) collective-permute-start(bf16[528,256]{1,0:T(8,128)(2,1)S(1)} %get-tuple-element.53), channel_id=1, source_target_pairs={{0,3},{1,2},{2,1},{3,0},{4,7},{5,6},{6,5},{7,4},{8,11},{9,10},{10,... | collective-permute-start | bytes 811016 | tf_op jit(solution)/shard_map/ppermute | solution.py:26
  42.2 27.5 %collective-permute-start.13 = (bf16[544,256]{1,0:T(8,128)(2,1)S(1)}, bf16[544,256]{1,0:T(8,128)(2,1)S(1)}, u32[]{:S(2)}, u32[]{:S(2)}) collective-permute-start(bf16[544,256]{1,0:T(8,128)(2,1)S(1)} %get-tuple-element.55), channel_id=1, source_target_pairs={{0,1},{1,0},{2,3},{3,2},{4,5},{5,4},{6,7},{7,6},{8,9},{9,8},{10,11... | collective-permute-start | bytes 835592 | tf_op jit(solution)/shard_map/ppermute | solution.py:26
  63.9 11.8 %collective-permute-start.14 = (bf16[544,256]{1,0:T(8,128)(2,1)S(1)}, bf16[544,256]{1,0:T(8,128)(2,1)S(1)}, u32[]{:S(2)}, u32[]{:S(2)}) collective-permute-start(bf16[544,256]{1,0:T(8,128)(2,1)S(1)} %get-tuple-element.56), channel_id=1, source_target_pairs={{0,2},{1,3},{2,0},{3,1},{4,6},{5,7},{6,4},{7,5},{8,10},{9,11},{10,... | collective-permute-start | bytes 835592 | tf_op jit(solution)/shard_map/ppermute | solution.py:26
  68.8 11.9 %collective-permute-start.16 = (bf16[1024,256]{1,0:T(8,128)(2,1)S(1)}, bf16[1024,256]{1,0:T(8,128)(2,1)S(1)}, u32[]{:S(2)}, u32[]{:S(2)}) collective-permute-start(bf16[1024,256]{1,0:T(8,128)(2,1)S(1)} %copy-done.4), channel_id=1, source_target_pairs={{0,1},{1,0},{2,3},{3,2},{4,5},{5,4},{6,7},{7,6},{8,9},{9,8},{10,11... | collective-permute-start | bytes 1572872 | tf_op jit(solution)/shard_map/ppermute | solution.py:26
  69.6 11.8 %collective-permute-start.18 = (bf16[256,1024]{1,0:T(8,128)(2,1)S(1)}, bf16[256,1024]{1,0:T(8,128)(2,1)S(1)}, u32[]{:S(2)}, u32[]{:S(2)}) collective-permute-start(bf16[256,1024]{1,0:T(8,128)(2,1)S(1)} %copy-done.5), channel_id=1, source_target_pairs={{0,1},{1,0},{2,3},{3,2},{4,5},{5,4},{6,7},{7,6},{8,9},{9,8},{10,11... | collective-permute-start | bytes 1572872 | tf_op jit(solution)/shard_map/ppermute | solution.py:26
  69.7 11.1 %collective-permute-start.15 = (bf16[544,256]{1,0:T(8,128)(2,1)S(1)}, bf16[544,256]{1,0:T(8,128)(2,1)S(1)}, u32[]{:S(2)}, u32[]{:S(2)}) collective-permute-start(bf16[544,256]{1,0:T(8,128)(2,1)S(1)} %get-tuple-element.57), channel_id=1, source_target_pairs={{0,3},{1,2},{2,1},{3,0},{4,7},{5,6},{6,5},{7,4},{8,11},{9,10},{10,... | collective-permute-start | bytes 835592 | tf_op jit(solution)/shard_map/ppermute | solution.py:26
  75.7 31.1 %collective-permute-start.17 = (bf16[2048,256]{1,0:T(8,128)(2,1)S(1)}, bf16[2048,256]{1,0:T(8,128)(2,1)S(1)}, u32[]{:S(2)}, u32[]{:S(2)}) collective-permute-start(bf16[2048,256]{1,0:T(8,128)(2,1)S(1)} %shard_map.189.refs_9_), channel_id=1, source_target_pairs={{0,1},{1,0},{2,3},{3,2},{4,5},{5,4},{6,7},{7,6},{8,9},{9,8},{10,11... | collective-permute-start | bytes 3145736 | tf_op jit(solution)/shard_map/ppermute | solution.py:26
  75.7 14.8 %collective-permute-start.20 = (bf16[1024,256]{1,0:T(8,128)(2,1)S(1)}, bf16[1024,256]{1,0:T(8,128)(2,1)S(1)}, u32[]{:S(2)}, u32[]{:S(2)}) collective-permute-start(bf16[1024,256]{1,0:T(8,128)(2,1)S(1)} %collective-permute-done.19.refs_14_), channel_id=1, source_target_pairs={{0,4},{4,0},{8,12},{12,8},{16,20},{20,16},{24,28},{28,24},{1,5},{5... | collective-permute-start | bytes 1572872 | tf_op jit(solution)/shard_map/ppermute | solution.py:26
  80.7 14.4 %collective-permute-start.21 = (bf16[1024,256]{1,0:T(8,128)(2,1)S(1)}, bf16[1024,256]{1,0:T(8,128)(2,1)S(1)}, u32[]{:S(2)}, u32[]{:S(2)}) collective-permute-start(bf16[1024,256]{1,0:T(8,128)(2,1)S(1)} %collective-permute-done.19.refs_14_), channel_id=1, source_target_pairs={{0,8},{4,12},{8,0},{12,4},{16,24},{20,28},{24,16},{28,20},{1,9},{5... | collective-permute-start | bytes 1572872 | tf_op jit(solution)/shard_map/ppermute | solution.py:26
  80.7 17.8 %collective-permute-start.24 = (bf16[1024,256]{1,0:T(8,128)(2,1)S(1)}, bf16[1024,256]{1,0:T(8,128)(2,1)S(1)}, u32[]{:S(2)}, u32[]{:S(2)}) collective-permute-start(bf16[1024,256]{1,0:T(8,128)(2,1)S(1)} %collective-permute-done.19.refs_14_), channel_id=1, source_target_pairs={{0,1},{1,0},{2,3},{3,2},{4,5},{5,4},{6,7},{7,6},{8,9},{9,8},{10,11... | collective-permute-start | bytes 1572872 | tf_op jit(solution)/shard_map/ppermute | solution.py:26
  81.3 17.2 %collective-permute-start.37 = (bf16[768,256]{1,0:T(8,128)(2,1)S(1)}, bf16[768,256]{1,0:T(8,128)(2,1)S(1)}, u32[]{:S(2)}, u32[]{:S(2)}) collective-permute-start(bf16[768,256]{1,0:T(8,128)(2,1)S(1)} %collective-permute-done.36.refs_12_), channel_id=1, source_target_pairs={{0,4},{4,0},{8,12},{12,8},{16,20},{20,16},{24,28},{28,24},{1,5},{5... | collective-permute-start | bytes 1179656 | tf_op jit(solution)/shard_map/ppermute | solution.py:26
  90.5 16.4 %collective-permute-start.25 = (bf16[1024,256]{1,0:T(8,128)(2,1)S(1)}, bf16[1024,256]{1,0:T(8,128)(2,1)S(1)}, u32[]{:S(2)}, u32[]{:S(2)}) collective-permute-start(bf16[1024,256]{1,0:T(8,128)(2,1)S(1)} %collective-permute-done.20.refs_15_), channel_id=1, source_target_pairs={{0,1},{1,0},{2,3},{3,2},{4,5},{5,4},{6,7},{7,6},{8,9},{9,8},{10,11... | collective-permute-start | bytes 1572872 | tf_op jit(solution)/shard_map/ppermute | solution.py:26
  95.1 12.2 %collective-permute-start.26 = (bf16[1024,256]{1,0:T(8,128)(2,1)S(1)}, bf16[1024,256]{1,0:T(8,128)(2,1)S(1)}, u32[]{:S(2)}, u32[]{:S(2)}) collective-permute-start(bf16[1024,256]{1,0:T(8,128)(2,1)S(1)} %collective-permute-done.21.refs_16_), channel_id=1, source_target_pairs={{0,1},{1,0},{2,3},{3,2},{4,5},{5,4},{6,7},{7,6},{8,9},{9,8},{10,11... | collective-permute-start | bytes 1572872 | tf_op jit(solution)/shard_map/ppermute | solution.py:26
  98.5 7.9 %collective-permute-start.22 = (bf16[512,256]{1,0:T(8,128)(2,1)S(1)}, bf16[512,256]{1,0:T(8,128)(2,1)S(1)}, u32[]{:S(2)}, u32[]{:S(2)}) collective-permute-start(bf16[512,256]{1,0:T(8,128)(2,1)S(1)} %slice.8), channel_id=1, source_target_pairs={{0,8},{4,12},{8,0},{12,4},{16,24},{20,28},{24,16},{28,20},{1,9},{5... | collective-permute-start | bytes 786440 | tf_op jit(solution)/shard_map/ppermute | solution.py:26
  98.5 7.9 %collective-permute-start.23 = (bf16[512,256]{1,0:T(8,128)(2,1)S(1)}, bf16[512,256]{1,0:T(8,128)(2,1)S(1)}, u32[]{:S(2)}, u32[]{:S(2)}) collective-permute-start(bf16[512,256]{1,0:T(8,128)(2,1)S(1)} %slice.9), channel_id=1, source_target_pairs={{0,4},{4,0},{8,12},{12,8},{16,20},{20,16},{24,28},{28,24},{1,5},{5... | collective-permute-start | bytes 786440 | tf_op jit(solution)/shard_map/ppermute | solution.py:26
  106.4 3.0 %collective-permute-start.28 = (bf16[512,256]{1,0:T(8,128)(2,1)S(1)}, bf16[512,256]{1,0:T(8,128)(2,1)S(1)}, u32[]{:S(2)}, u32[]{:S(2)}) collective-permute-start(bf16[512,256]{1,0:T(8,128)(2,1)S(1)} %collective-permute-done.23.refs_18_), channel_id=1, source_target_pairs={{0,1},{1,0},{2,3},{3,2},{4,5},{5,4},{6,7},{7,6},{8,9},{9,8},{10,11... | collective-permute-start | bytes 786440 | tf_op jit(solution)/shard_map/ppermute | solution.py:26
  106.9 22.0 %collective-permute-start.34 = (bf16[2048,256]{1,0:T(8,128)(2,1)S(1)}, bf16[2048,256]{1,0:T(8,128)(2,1)S(1)}, u32[]{:S(2)}, u32[]{:S(2)}) collective-permute-start(bf16[2048,256]{1,0:T(8,128)(2,1)S(1)} %bitcast.9), channel_id=1, source_target_pairs={{0,1},{1,0},{2,3},{3,2},{4,5},{5,4},{6,7},{7,6},{8,9},{9,8},{10,11... | collective-permute-start | bytes 3145736 | tf_op jit(solution)/shard_map/ppermute | solution.py:26
  107.0 10.2 %collective-permute-start.35 = (bf16[256,1024]{1,0:T(8,128)(2,1)S(1)}, bf16[256,1024]{1,0:T(8,128)(2,1)S(1)}, u32[]{:S(2)}, u32[]{:S(2)}) collective-permute-start(bf16[256,1024]{1,0:T(8,128)(2,1)S(1)} %copy-done.2), channel_id=1, source_target_pairs={{0,1},{1,0},{2,3},{3,2},{4,5},{5,4},{6,7},{7,6},{8,9},{9,8},{10,11... | collective-permute-start | bytes 1572872 | tf_op jit(solution)/shard_map/ppermute | solution.py:26
  107.4 12.0 %collective-permute-start.38 = (bf16[768,256]{1,0:T(8,128)(2,1)S(1)}, bf16[768,256]{1,0:T(8,128)(2,1)S(1)}, u32[]{:S(2)}, u32[]{:S(2)}) collective-permute-start(bf16[768,256]{1,0:T(8,128)(2,1)S(1)} %collective-permute-done.36.refs_12_), channel_id=1, source_target_pairs={{0,8},{4,12},{8,0},{12,4},{16,24},{20,28},{24,16},{28,20},{1,9},{5... | collective-permute-start | bytes 1179656 | tf_op jit(solution)/shard_map/ppermute | solution.py:26
  108.8 18.9 %collective-permute-start.39 = (bf16[768,256]{1,0:T(8,128)(2,1)S(1)}, bf16[768,256]{1,0:T(8,128)(2,1)S(1)}, u32[]{:S(2)}, u32[]{:S(2)}) collective-permute-start(bf16[768,256]{1,0:T(8,128)(2,1)S(1)} %collective-permute-done.37.refs_13_), channel_id=1, source_target_pairs={{0,8},{4,12},{8,0},{12,4},{16,24},{20,28},{24,16},{28,20},{1,9},{5... | collective-permute-start | bytes 1179656 | tf_op jit(solution)/shard_map/ppermute | solution.py:26
  109.4 7.0 %collective-permute-start.2 = (bf16[272,256]{1,0:T(8,128)(2,1)S(1)}, bf16[272,256]{1,0:T(8,128)(2,1)S(1)}, u32[]{:S(2)}, u32[]{:S(2)}) collective-permute-start(bf16[272,256]{1,0:T(8,128)(2,1)S(1)} %get-tuple-element.39), channel_id=1, source_target_pairs={{0,3},{1,2},{2,1},{3,0},{4,7},{5,6},{6,5},{7,4},{8,11},{9,10},{10,... | collective-permute-start | bytes 417800 | tf_op jit(solution)/shard_map/ppermute | solution.py:26
  116.5 11.3 %collective-permute-start.29 = (bf16[16,1152]{1,0:T(8,128)(2,1)S(1)}, bf16[16,1152]{1,0:T(8,128)(2,1)S(1)}, u32[]{:S(2)}, u32[]{:S(2)}) collective-permute-start(bf16[16,1152]{1,0:T(8,128)(2,1)S(1)} %get-tuple-element.59), channel_id=1, source_target_pairs={{0,0},{1,8},{2,16},{3,24},{4,4},{5,12},{6,20},{7,28},{8,1},{9,9},{... | collective-permute-start | bytes 110600 | tf_op jit(solution)/shard_map/ppermute | solution.py:519
  117.1 11.1 %collective-permute-start.30 = (bf16[16,1152]{1,0:T(8,128)(2,1)S(1)}, bf16[16,1152]{1,0:T(8,128)(2,1)S(1)}, u32[]{:S(2)}, u32[]{:S(2)}) collective-permute-start(bf16[16,1152]{1,0:T(8,128)(2,1)S(1)} %get-tuple-element.60), channel_id=1, source_target_pairs={{0,4},{1,12},{2,20},{3,28},{4,0},{5,8},{6,16},{7,24},{8,5},{9,13},... | collective-permute-start | bytes 110600 | tf_op jit(solution)/shard_map/ppermute | solution.py:519
  119.4 9.4 %collective-permute-start.40 = (bf16[768,256]{1,0:T(8,128)(2,1)S(1)}, bf16[768,256]{1,0:T(8,128)(2,1)S(1)}, u32[]{:S(2)}, u32[]{:S(2)}) collective-permute-start(bf16[768,256]{1,0:T(8,128)(2,1)S(1)} %collective-permute-done.36.refs_12_), channel_id=1, source_target_pairs={{0,1},{1,0},{2,3},{3,2},{4,5},{5,4},{6,7},{7,6},{8,9},{9,8},{10,11... | collective-permute-start | bytes 1179656 | tf_op jit(solution)/shard_map/ppermute | solution.py:26
  127.7 3.9 %collective-permute-start.41 = (bf16[768,256]{1,0:T(8,128)(2,1)S(1)}, bf16[768,256]{1,0:T(8,128)(2,1)S(1)}, u32[]{:S(2)}, u32[]{:S(2)}) collective-permute-start(bf16[768,256]{1,0:T(8,128)(2,1)S(1)} %collective-permute-done.37.refs_13_), channel_id=1, source_target_pairs={{0,1},{1,0},{2,3},{3,2},{4,5},{5,4},{6,7},{7,6},{8,9},{9,8},{10,11... | collective-permute-start | bytes 1179656 | tf_op jit(solution)/shard_map/ppermute | solution.py:26
  127.7 4.0 %collective-permute-start.42 = (bf16[768,256]{1,0:T(8,128)(2,1)S(1)}, bf16[768,256]{1,0:T(8,128)(2,1)S(1)}, u32[]{:S(2)}, u32[]{:S(2)}) collective-permute-start(bf16[768,256]{1,0:T(8,128)(2,1)S(1)} %collective-permute-done.38.refs_14_), channel_id=1, source_target_pairs={{0,1},{1,0},{2,3},{3,2},{4,5},{5,4},{6,7},{7,6},{8,9},{9,8},{10,11... | collective-permute-start | bytes 1179656 | tf_op jit(solution)/shard_map/ppermute | solution.py:26
  128.2 3.4 %collective-permute-start.43 = (bf16[768,256]{1,0:T(8,128)(2,1)S(1)}, bf16[768,256]{1,0:T(8,128)(2,1)S(1)}, u32[]{:S(2)}, u32[]{:S(2)}) collective-permute-start(bf16[768,256]{1,0:T(8,128)(2,1)S(1)} %collective-permute-done.39.refs_15_), channel_id=1, source_target_pairs={{0,1},{1,0},{2,3},{3,2},{4,5},{5,4},{6,7},{7,6},{8,9},{9,8},{10,11... | collective-permute-start | bytes 1179656 | tf_op jit(solution)/shard_map/ppermute | solution.py:26
  128.9 5.5 %collective-permute-start.32 = (bf16[32,1152]{1,0:T(8,128)(2,1)S(1)}, bf16[32,1152]{1,0:T(8,128)(2,1)S(1)}, u32[]{:S(2)}, u32[]{:S(2)}) collective-permute-start(bf16[32,1152]{1,0:T(8,128)(2,1)S(1)} %constant_dynamic-update-slice_fusion.refs_4_), channel_id=1, source_target_pairs={{0,2},{1,3},{2,0},{3,1},{4,6},{5,7},{6,4},{7,5},{8,10},{9,11},{10,... | collective-permute-start | bytes 221192 | tf_op jit(solution)/shard_map/ppermute | solution.py:26
  131.6 4.2 %collective-permute-start.33 = (bf16[32,1152]{1,0:T(8,128)(2,1)S(1)}, bf16[32,1152]{1,0:T(8,128)(2,1)S(1)}, u32[]{:S(2)}, u32[]{:S(2)}) collective-permute-start(bf16[32,1152]{1,0:T(8,128)(2,1)S(1)} %constant_dynamic-update-slice_fusion.refs_4_), channel_id=1, source_target_pairs={{0,3},{1,2},{2,1},{3,0},{4,7},{5,6},{6,5},{7,4},{8,11},{9,10},{10,... | collective-permute-start | bytes 221192 | tf_op jit(solution)/shard_map/ppermute | solution.py:26
  138.8 3.7 %collective-permute-start.44 = (bf16[256,256]{1,0:T(8,128)(2,1)S(1)}, bf16[256,256]{1,0:T(8,128)(2,1)S(1)}, u32[]{:S(2)}, u32[]{:S(2)}) collective-permute-start(bf16[256,256]{1,0:T(8,128)(2,1)S(1)} %get-tuple-element.63), channel_id=1, source_target_pairs={{0,1},{1,0},{2,3},{3,2},{4,5},{5,4},{6,7},{7,6},{8,9},{9,8},{10,11... | collective-permute-start | bytes 393224 | tf_op jit(solution)/shard_map/ppermute | solution.py:26
  139.1 20.0 %collective-permute-start.47 = (bf16[512,256]{1,0:T(8,128)(2,1)S(1)}, bf16[512,256]{1,0:T(8,128)(2,1)S(1)}, u32[]{:S(2)}, u32[]{:S(2)}) collective-permute-start(bf16[512,256]{1,0:T(8,128)(2,1)S(1)} %get-tuple-element.67), channel_id=1, source_target_pairs={{0,1},{1,0},{2,3},{3,2},{4,5},{5,4},{6,7},{7,6},{8,9},{9,8},{10,11... | collective-permute-start | bytes 786440 | tf_op jit(solution)/shard_map/ppermute | solution.py:26
  139.4 19.6 %collective-permute-start.48 = (bf16[512,256]{1,0:T(8,128)(2,1)S(1)}, bf16[512,256]{1,0:T(8,128)(2,1)S(1)}, u32[]{:S(2)}, u32[]{:S(2)}) collective-permute-start(bf16[512,256]{1,0:T(8,128)(2,1)S(1)} %get-tuple-element.68), channel_id=1, source_target_pairs={{0,2},{1,3},{2,0},{3,1},{4,6},{5,7},{6,4},{7,5},{8,10},{9,11},{10,... | collective-permute-start | bytes 786440 | tf_op jit(solution)/shard_map/ppermute | solution.py:26
  140.8 18.2 %collective-permute-start.49 = (bf16[512,256]{1,0:T(8,128)(2,1)S(1)}, bf16[512,256]{1,0:T(8,128)(2,1)S(1)}, u32[]{:S(2)}, u32[]{:S(2)}) collective-permute-start(bf16[512,256]{1,0:T(8,128)(2,1)S(1)} %get-tuple-element.69), channel_id=1, source_target_pairs={{0,3},{1,2},{2,1},{3,0},{4,7},{5,6},{6,5},{7,4},{8,11},{9,10},{10,... | collective-permute-start | bytes 786440 | tf_op jit(solution)/shard_map/ppermute | solution.py:26
  140.9 16.1 %collective-permute-start.45 = (bf16[256,256]{1,0:T(8,128)(2,1)S(1)}, bf16[256,256]{1,0:T(8,128)(2,1)S(1)}, u32[]{:S(2)}, u32[]{:S(2)}) collective-permute-start(bf16[256,256]{1,0:T(8,128)(2,1)S(1)} %get-tuple-element.64), channel_id=1, source_target_pairs={{0,2},{1,3},{2,0},{3,1},{4,6},{5,7},{6,4},{7,5},{8,10},{9,11},{10,... | collective-permute-start | bytes 393224 | tf_op jit(solution)/shard_map/ppermute | solution.py:26
  142.5 15.7 %collective-permute-start.46 = (bf16[256,256]{1,0:T(8,128)(2,1)S(1)}, bf16[256,256]{1,0:T(8,128)(2,1)S(1)}, u32[]{:S(2)}, u32[]{:S(2)}) collective-permute-start(bf16[256,256]{1,0:T(8,128)(2,1)S(1)} %get-tuple-element.65), channel_id=1, source_target_pairs={{0,3},{1,2},{2,1},{3,0},{4,7},{5,6},{6,5},{7,4},{8,11},{9,10},{10,... | collective-permute-start | bytes 393224 | tf_op jit(solution)/shard_map/ppermute | solution.py:26
  (26 other events, 341.1 us)
